TPU v7x, 512 devices: a whole 4x4x16 slice. The times are simulated.
512 devices in a mesh: row: 16 (over x, y), col: 32 (over z, core).
Axes of the slice: x: 4, y: 4, z: 16, core: 2. Of those that a mesh axis runs over, the one named last changes fastest.
Arguments:
- start_vector: bfloat16 [4, 2048, 2048], P(None, 'row', 'col'), may hold values from -150 to 150
- left_env: bfloat16 [5, 2048, 2048], P(None, 'row', 'col'), may hold values from -5 to 6
- right_env: bfloat16 [5, 2048, 2048], P(None, 'col', 'row'), may hold values from -5 to 6
- left_tensor: float32 [5, 5, 2, 2], replicated, may hold values from -1.5 to 2.5
- right_tensor: float32 [5, 5, 2, 2], replicated, may hold values from -1.5 to 2.5
Outputs:
- next_vector: bfloat16 [4, 2048, 2048], P(None, 'row', 'col')
- coefficients: float32 [2], replicated
All inputs are finite; a program needn't handle non-finite values.
Results may differ from a plain program's by a relative error of at most 0.023.
Values may be sent and summed in bfloat16 or wider, within the bound.
No kernel may reach another device: no remote copies, remote signals or barrier semaphores. Data moves between devices by JAX's collectives and lax.ppermute only.
A program may use at most 64 MiB of HBM per device.

v0:
```python
import jax
import jax.numpy as jnp
from jax import lax
from jax.sharding import Mesh
from jax.sharding import PartitionSpec as P

ROW = ("row_0", "row_1")
COL = ("col_0", "col_1")
ROW_COL = ("row_0", "row_1", "col_0", "col_1")


epsilon = 1e-06


def copy_for_each(x, axis):
    size = lax.axis_size(axis)
    return lax.all_to_all(jnp.broadcast_to(x[None], (size, *x.shape)), axis, 0, 0, tiled=True)


def joined_along(pieces, dim):
    pieces = jnp.moveaxis(pieces, 0, dim)
    lengths = pieces.shape
    return pieces.reshape(*lengths[:dim], lengths[dim] * lengths[dim + 1], *lengths[dim + 2 :])


def gathered_copies(x, axis, dim):
    pieces = copy_for_each(x, axis)
    return joined_along(pieces, dim)


def sum_in_order(pieces, axes, sequence):
    lengths = [lax.axis_size(a) for a in axes]
    pieces = pieces.reshape(*lengths, *pieces.shape[1:])
    pieces = pieces.transpose(*sequence, *range(len(axes), pieces.ndim))
    pieces = pieces.reshape(-1, *pieces.shape[len(axes) :])
    for k in sequence:
        pieces = lax.psum_scatter(pieces, axes[k], scatter_dimension=0, tiled=True)
    return pieces[0]


def cut_along(x, dim, size):
    lengths = x.shape
    pieces = x.reshape(*lengths[:dim], size, lengths[dim] // size, *lengths[dim + 1 :])
    return jnp.moveaxis(pieces, dim, 0)


def scatter_axes(x, axes, sequence, dim):
    size = lax.axis_size(axes)
    return sum_in_order(cut_along(x, dim, size), axes, sequence)


def by_axis(x, axes):
    for axis in axes:
        x = lax.psum(x, axis)
    return x


def coupling(left_tensor, right_tensor):
    channels = left_tensor.shape[0]
    joined = jnp.einsum(
        "wuac,uvbd->vabwcd", left_tensor, right_tensor, precision=lax.Precision.HIGHEST
    )
    return joined.reshape(channels, 4, channels, 4)


def contract_left(portion, columns):
    return jnp.einsum("wax,txb->wtba", portion, columns, preferred_element_type=jnp.float32)


def mix_channels(coupling_table, cross):
    mixed_bond = jnp.einsum(
        "vswt,wtba->vsba", coupling_table, cross, precision=lax.Precision.HIGHEST
    )
    return mixed_bond.astype(jnp.bfloat16)


def contract_right(mixed_bond, portion):
    return jnp.einsum("vsba,vbc->sac", mixed_bond, portion, preferred_element_type=jnp.float32)


def apply_hamiltonian(vector, coupling_table, panels):
    columns = gathered_copies(vector, ROW, 1)
    cross = contract_left(panels[0], columns)
    mixed_bond = mix_channels(coupling_table, cross)
    partials = contract_right(mixed_bond, panels[1])
    return scatter_axes(partials.astype(jnp.bfloat16), COL, (1, 0), 2).astype(jnp.float32)


def local_mean(former, latter, entries):
    return jnp.sum(former * latter) / entries


def body(start_vector, left_env, right_env, left_tensor, right_tensor):
    coupling_table = coupling(left_tensor, right_tensor)
    entries = float(
        start_vector.shape[0]
        * start_vector.shape[1]
        * start_vector.shape[2]
        * lax.axis_size(ROW)
        * lax.axis_size(COL)
    )
    panels = (lax.all_gather(left_env, COL, axis=2, tiled=True), gathered_copies(right_env, ROW, 2))
    base_vector = start_vector.astype(jnp.float32)
    image = apply_hamiltonian(start_vector, coupling_table, panels)
    base_square, correlation, image_square = (
        by_axis(local_mean(base_vector, base_vector, entries), ROW_COL),
        by_axis(local_mean(base_vector, image, entries), ROW_COL),
        by_axis(local_mean(image, image, entries), ROW_COL),
    )
    alpha = correlation / (base_square + epsilon)
    residual = image - alpha * base_vector
    rho = jnp.sqrt(image_square - 2.0 * alpha * correlation + alpha * alpha * base_square + epsilon)
    next_vector = (residual / rho).astype(jnp.bfloat16)
    coefficients = jnp.stack([alpha, rho])
    return (next_vector, coefficients)


def solution(mesh):
    finer = Mesh(mesh.devices.reshape(4, 4, 16, 2), ("row_0", "row_1", "col_0", "col_1"))
    in_specs = (P(None, ROW, COL), P(None, ROW, COL), P(None, COL, ROW), P(), P())
    out_specs = (P(None, ROW, COL), P())
    return jax.shard_map(body, mesh=finer, in_specs=in_specs, out_specs=out_specs, check_vma=False)
```

profile of v0, /device:TPU:1, one launch (start us, length us, event | category | flops | bytes accessed | tf_op | source)
XLA Modules:
  0.0 263.9 jit_solution(11655160880378192590)
XLA Ops:
  7.2 0.0 copy-start
  7.2 0.0 copy-start.2
  7.2 0.0 all-gather.2.cloned.1.call-start
  7.2 0.7 all-gather.2.cloned.1.call-update
  7.9 1.1 broadcast_in_dim.4
  9.0 22.4 %all_to_all.10 = bf16[16,4,128,64]{2,3,1,0:T(8,128)(2,1)S(1)} all-to-all(bf16[16,4,128,64]{2,3,1,0:T(8,128)(2,1)S(1)} %broadcast_in_dim.4), channel_id=1, replica_groups=mesh['row_0'=4,'row_1'=4,'col_0'=16,'col_1'=2] {'row_0','row_1'}, dimensions={0} | all-to-all | bytes 2097152 | tf_op jit(solution)/shard_map/all_to_all | solution.py:17
  31.4 0.0 copy-done.2
  31.4 0.0 copy-start.3
  31.4 1.4 broadcast_in_dim.5
  32.8 3.7 %all-to-all-start.1 = ((bf16[16,5,64,128]{3,2,1,0:T(8,128)(2,1)}), bf16[16,5,64,128]{3,2,1,0:T(8,128)(2,1)S(1)}, u32[]{:S(2)}, u32[]{:S(2)}) async-start(bf16[16,5,64,128]{3,2,1,0:T(8,128)(2,1)} %broadcast_in_dim.5), calls=%async_computation.1 | async-start | bytes 2621440 | tf_op jit(solution)/shard_map/all_to_all | solution.py:17
  36.5 0.0 reduce-scatter.3.cloned.1.call-start
  36.6 0.0 copy-done
  36.6 0.0 copy-done.3
  36.6 0.4 convolution_bitcast_fusion.1
  37.0 0.7 copy.19
  37.7 1.3 reshape.35
  39.0 14.3 %all-to-all-done.1 = bf16[16,5,64,128]{3,2,1,0:T(8,128)(2,1)S(1)} async-done(((bf16[16,5,64,128]{3,2,1,0:T(8,128)(2,1)}), bf16[16,5,64,128]{3,2,1,0:T(8,128)(2,1)S(1)}, u32[]{:S(2)}, u32[]{:S(2)}) %all-to-all-start.1) | async-done | bytes 1310752 | tf_op jit(solution)/shard_map/all_to_all | solution.py:17
  53.3 0.9 copy.22
  54.2 0.6 reshape.40
  54.8 33.2 %all-gather.2.cloned.1.call-done = bf16[5,128,2048]{1,2,0:T(8,128)(2,1)} async-done(((bf16[5,128,64]{1,2,0:T(8,128)(2,1)}), bf16[5,128,2048]{1,2,0:T(8,128)(2,1)}) %all-gather.2.cloned.1.call-update) | async-done | bytes 2621456 | tf_op jit(solution)/shard_map/all_gather | solution.py:102
  88.0 3.0 %fusion.3 = f32[5,4,64,128]{3,2,0,1:T(8,128)S(1)} fusion(bf16[5,128,2048]{1,2,0:T(8,128)(2,1)} %all-gather.2.cloned.1.call-done, bf16[4,2048,64,1]{1,2,0,3:T(8,128)(2,1)} %reshape.35), kind=kOutput, calls=%fused_computation.5 | convolution fusion | flops 671088640 | bytes 4325376 | tf_op jit(solution)/shard_map/wax,txb->wtba/dot_general | solution.py:67
  91.1 4.0 %fusion.2 = bf16[5,4,64,128]{3,0,2,1:T(8,128)(2,1)S(1)} fusion(f32[5,4,64,128]{3,2,0,1:T(8,128)S(1)} %fusion.3, f32[5,4,5,4,1]{2,3,1,0,4:T(4,128)S(1)} %bitcast.57), kind=kOutput, calls=%fused_computation.4 | convolution fusion | flops 39485440 | bytes 984640 | tf_op jit(solution)/shard_map/vswt,wtba->vsba/dot_general | solution.py:71
  95.1 1.3 bitcast_convert_fusion
  96.4 2.5 copy.24
  98.9 3.2 %copy.25 = bf16[2,16,4,128,64]{3,4,2,1,0:T(8,128)(2,1)} copy(bf16[2,16,4,128,64]{3,4,0,1,2:T(8,128)(2,1)} %bitcast.54) | data formatting | bytes 4194304 | tf_op jit(solution)/shard_map/transpose | solution.py:34
  102.1 0.0 copy-start.1
  102.1 0.0 reduce-scatter.3.cloned.1.call-update
  102.1 0.0 reduce-scatter.5.cloned.1.call-start
  102.1 17.6 %reduce-scatter.3.cloned.1.call-done = bf16[16,4,128,64]{2,3,1,0:T(8,128)(2,1)} async-done(((bf16[32,4,128,64]{2,3,1,0:T(8,128)(2,1)}), bf16[16,4,128,64]{2,3,1,0:T(8,128)(2,1)}) %reduce-scatter.3.cloned.1.call-update) | async-done | bytes 1048592 | tf_op jit(solution)/shard_map/reduce_scatter | solution.py:37
  119.8 0.0 reduce-scatter.5.cloned.1.call-update
  119.8 64.3 %reduce-scatter.5.cloned.1.call-done = bf16[1,4,128,64]{2,3,1,0:T(8,128)(2,1)} async-done(((bf16[16,4,128,64]{2,3,1,0:T(8,128)(2,1)}), bf16[1,4,128,64]{2,3,1,0:T(8,128)(2,1)}) %reduce-scatter.5.cloned.1.call-update) | async-done | bytes 65552 | tf_op jit(solution)/shard_map/reduce_scatter | solution.py:37
  184.0 0.0 copy-done.1
  184.0 1.5 fusion.10
  187.5 9.5 %all-reduce.2 = (f32[]{:T(128)}, f32[]{:T(128)}, f32[]{:T(128)}) all-reduce(f32[]{:T(128)S(6)} %div.21, f32[]{:T(128)S(6)} %div.18, f32[]{:T(128)S(6)} %div.19), channel_id=1, replica_groups=mesh['row_0'=4,'row_1'=4,'col_0'=16,'col_1'=2] {'row_0'}, use_global_device_ids=true, to_apply=%region_13.0 | all-reduce | flops 3 | bytes 24 | tf_op jit(solution)/shard_map/psum | solution.py:54
  196.9 8.5 %all-reduce.1 = (f32[]{:T(128)}, f32[]{:T(128)}, f32[]{:T(128)}) all-reduce(f32[]{:T(128)} %get-tuple-element.11, f32[]{:T(128)} %get-tuple-element.12, f32[]{:T(128)} %get-tuple-element.13), channel_id=1, replica_groups=mesh['row_0'=4,'row_1'=4,'col_0'=16,'col_1'=2] {'row_1'}, use_global_device_ids=true, to_apply=%region_14.0 | all-reduce | flops 3 | bytes 24 | tf_op jit(solution)/shard_map/psum | solution.py:54
  205.5 22.2 %all-reduce = (f32[]{:T(128)}, f32[]{:T(128)}, f32[]{:T(128)}) all-reduce(f32[]{:T(128)} %get-tuple-element.8, f32[]{:T(128)} %get-tuple-element.9, f32[]{:T(128)} %get-tuple-element.10), channel_id=1, replica_groups=mesh['row_0'=4,'row_1'=4,'col_0'=16,'col_1'=2] {'col_0'}, use_global_device_ids=true, to_apply=%region_15.0 | all-reduce | flops 3 | bytes 24 | tf_op jit(solution)/shard_map/psum | solution.py:54
  227.7 24.4 %all-reduce.3 = (f32[]{:T(128)}, f32[]{:T(128)}, f32[]{:T(128)}) all-reduce(f32[]{:T(128)} %get-tuple-element.5, f32[]{:T(128)} %get-tuple-element.6, f32[]{:T(128)} %get-tuple-element.7), channel_id=1, replica_groups=mesh['row_0'=4,'row_1'=4,'col_0'=16,'col_1'=2] {'col_1'}, use_global_device_ids=true, to_apply=%region_16.0 | all-reduce | flops 3 | bytes 24 | tf_op jit(solution)/shard_map/psum | solution.py:54
  255.3 0.6 pad_maximum_fusion
  255.8 1.5 fusion.13
  (1 shorter events, 0.0 us)
Async XLA Ops:
  7.2 29.4 %copy-start = (f32[5,5,2,2]{1,3,2,0:T(2,128)S(1)}, f32[5,5,2,2]{1,3,2,0:T(2,128)}, u32[]{:S(2)}) copy-start(f32[5,5,2,2]{1,3,2,0:T(2,128)} %param.8) | copy-start | bytes 1204
  7.2 24.2 %copy-start.2 = (bf16[5,64,128]{2,1,0:T(8,128)(2,1)S(1)}, bf16[5,64,128]{2,1,0:T(8,128)(2,1)}, u32[]{:S(2)}) copy-start(bf16[5,64,128]{2,1,0:T(8,128)(2,1)} %param.7) | copy-start | bytes 245764
  7.2 80.8 %all-gather.2.cloned.1.call-start = ((), (), s32[]{:S(2)}) async-start(), calls=%async_computation.4 | async-start | bytes 2703360 | tf_op jit(solution)/shard_map/all_gather | solution.py:102
  31.4 5.2 %copy-start.3 = (f32[5,5,2,2]{1,3,2,0:T(2,128)S(1)}, f32[5,5,2,2]{1,3,2,0:T(2,128)}, u32[]{:S(2)}) copy-start(f32[5,5,2,2]{1,3,2,0:T(2,128)} %param.9) | copy-start | bytes 1204
  32.8 20.5 %all-to-all-start.1 = ((bf16[16,5,64,128]{3,2,1,0:T(8,128)(2,1)}), bf16[16,5,64,128]{3,2,1,0:T(8,128)(2,1)S(1)}, u32[]{:S(2)}, u32[]{:S(2)}) async-start(bf16[16,5,64,128]{3,2,1,0:T(8,128)(2,1)} %broadcast_in_dim.5), calls=%async_computation.1 | async-start | bytes 2621440 | tf_op jit(solution)/shard_map/all_to_all | solution.py:17
  36.5 83.2 %reduce-scatter.3.cloned.1.call-start = ((), (), s32[]{:S(2)}) async-start(), calls=%async_computation.5 | async-start | bytes 3145728 | tf_op jit(solution)/shard_map/reduce_scatter | solution.py:37
  102.1 82.0 %copy-start.1 = (bf16[4,128,64]{1,2,0:T(8,128)(2,1)S(1)}, bf16[4,128,64]{1,2,0:T(8,128)(2,1)}, u32[]{:S(2)}) copy-start(bf16[4,128,64]{1,2,0:T(8,128)(2,1)} %param.5) | copy-start | bytes 196612
  102.1 82.0 %reduce-scatter.5.cloned.1.call-start = ((), (), s32[]{:S(2)}) async-start(), calls=%async_computation.6 | async-start | bytes 1114112 | tf_op jit(solution)/shard_map/reduce_scatter | solution.py:37
Sparse Core Ops, SparseCore 0:
  10.1 77.8 all-gather.1
  102.2 17.5 reduce-scatter.2
  122.6 61.4 reduce-scatter.4
where the time goes:
time: 264 us
  waiting for transfers between devices  130 us (49%)
  blocking collectives  87.1 us (33%)
  between operations  18.9 us (7%)
  local copies, waits for them, and re-layouts  11.7 us (4%)
  matrix products  8.74 us (3%)
  starting transfers between devices  3.82 us (1%)
  other arithmetic  3.6 us (1%)
    reduce_scatter x2, waiting for transfers between devices, sum_in_order(): pieces = lax.psum_scatter(pieces, axes[k], scatter_dimension=0, tiled=True)  81.9 us
    psum x4, blocking collectives, by_axis(): x = lax.psum(x, axis)  64.7 us
    all_gather x1, waiting for transfers between devices, body(): lax.all_gather(left_env, COL, axis=2, tiled=True)  33.2 us
    all_to_all x1, blocking collectives, copy_for_each(): lax.all_to_all(jnp.broadcast_to(x[None], (size, *x.shape)), axis, 0, 0, t...  22.4 us
    all_to_all x1, waiting for transfers between devices, copy_for_each(): lax.all_to_all(jnp.broadcast_to(x[None], (size, *x.shape)), axis, 0, 0, t...  14.3 us
  transfers between devices with their start and end apart: 4, of which 4 were waited for; matrix products, arithmetic and copies ran while one was open for 2% of the time, Pallas kernels for 0%

commit v1 on v0

v1 whole, which is shorter than its diff:
```python
import jax
import jax.numpy as jnp
from jax import lax
from jax.experimental import pallas as pl
from jax.experimental.pallas import tpu as pltpu
from jax.sharding import Mesh
from jax.sharding import PartitionSpec as P

X, Y, Z, C = "row_0", "row_1", "col_0", "col_1"
ROW = (X, Y)
COL = (Z, C)
STATES = 4
CHANNELS = 5

epsilon = 1e-06
SCALE = 8192.0


def coupling(left_tensor, right_tensor):
    channels = left_tensor.shape[0]
    joined = jnp.einsum(
        "wuac,uvbd->vabwcd", left_tensor, right_tensor, precision=lax.Precision.HIGHEST
    )
    return joined.reshape(channels * STATES, channels * STATES)


def swap_of_cores(x):
    n, rows, cols = x.shape
    halves = jnp.moveaxis(x.reshape(n, 2, rows // 2, cols), 1, 0)
    halves = lax.all_to_all(halves, C, 0, 0, tiled=True)
    return jnp.moveaxis(halves, 0, 2).reshape(n, rows // 2, 2 * cols)


def other_core(x):
    return lax.ppermute(x, C, [(0, 1), (1, 0)])


def kernel(core_ref, table_ref, left_ref, own_ref, other_ref, out_ref, left_s, vec_s, right_s, cross_s, mixed_s):
    blocks, rows, width = out_ref.shape
    half = rows // STATES
    core = core_ref[0]
    own_at = pl.multiple_of(core * half, half)
    other_at = pl.multiple_of((1 - core) * half, half)
    for r in range(blocks):
        left_s[:, r * width : (r + 1) * width] = left_ref[r]
        for source, at in ((own_ref, own_at), (other_ref, other_at)):
            for t in range(STATES):
                vec_s[pl.ds(r * width + at, half), t * width : (t + 1) * width] = source[r, t * half : (t + 1) * half, :]
            for v in range(CHANNELS):
                k = (STATES + v) * half
                right_s[pl.ds(v * width + at, half), r * width : (r + 1) * width] = source[r, k : k + half, :]
    cross_s[...] = jnp.dot(left_s[...], vec_s[...], preferred_element_type=jnp.float32)
    for v in range(CHANNELS):
        for s in range(STATES):
            total = None
            for w in range(CHANNELS):
                for t in range(STATES):
                    part = (
                        table_ref[v * STATES + s, w * STATES + t]
                        * cross_s[w * half : (w + 1) * half, t * width : (t + 1) * width]
                    )
                    total = part if total is None else total + part
            mixed_s[s * half : (s + 1) * half, v * width : (v + 1) * width] = total.astype(jnp.bfloat16)
    for j in range(blocks // 2):
        image = jnp.dot(
            mixed_s[...], right_s[:, 2 * j * width : 2 * (j + 1) * width], preferred_element_type=jnp.float32
        ).astype(jnp.bfloat16)
        out_ref[2 * j] = image[:, :width]
        out_ref[2 * j + 1] = image[:, width:]


def terms(core, table, left, own, other):
    blocks, left_rows, width = left.shape
    half = left_rows // CHANNELS
    rows = STATES * half
    vmem = pl.BlockSpec(memory_space=pltpu.VMEM)
    smem = pl.BlockSpec(memory_space=pltpu.SMEM)
    return pl.pallas_call(
        kernel,
        out_shape=jax.ShapeDtypeStruct((blocks, rows, width), jnp.bfloat16),
        in_specs=[smem, smem, vmem, vmem, vmem],
        out_specs=vmem,
        scratch_shapes=[
            pltpu.VMEM((left_rows, blocks * width), jnp.bfloat16),
            pltpu.VMEM((blocks * width, STATES * width), jnp.bfloat16),
            pltpu.VMEM((CHANNELS * width, blocks * width), jnp.bfloat16),
            pltpu.VMEM((left_rows, STATES * width), jnp.float32),
            pltpu.VMEM((rows, CHANNELS * width), jnp.bfloat16),
        ],
        compiler_params=pltpu.CompilerParams(vmem_limit_bytes=40 * 1024 * 1024),
    )(core, table, left, own, other)


def summed(x, axes):
    size = lax.axis_size(axes)
    pieces = lax.all_to_all(jnp.broadcast_to(x[None], (size, *x.shape)), axes, 0, 0, tiled=True)
    return jnp.sum(pieces, 0)


def body(start_vector, left_env, right_env, left_tensor, right_tensor):
    n_row = lax.axis_size(ROW)
    n_z = lax.axis_size(Z)
    _, rows, cols = start_vector.shape
    half = rows // 2
    entries = float(STATES * rows * cols * n_row * n_z * lax.axis_size(C))
    core = lax.axis_index(C).astype(jnp.int32)
    table = coupling(left_tensor, right_tensor)

    both = swap_of_cores(jnp.concatenate([start_vector, left_env], 0))
    vector = both[:STATES]
    left = (both[STATES:].astype(jnp.float32) * SCALE).astype(jnp.float16)

    mine = jnp.concatenate([vector, right_env], 0).reshape(1, (STATES + CHANNELS) * half, 2 * cols)
    own = lax.all_to_all(jnp.broadcast_to(mine, (n_row, *mine.shape[1:])), ROW, 0, 0, tiled=True)
    left = lax.all_gather(left.reshape(CHANNELS * half, 2 * cols), Z, axis=0)
    own, left = lax.optimization_barrier((own, left))
    left = (left.astype(jnp.float32) * (1.0 / SCALE)).astype(jnp.bfloat16)
    other = other_core(own)

    sent = terms(core.reshape(1), table, left, own, other)
    pieces = lax.all_to_all(sent, Z, 0, 0, tiled=True)
    image = jnp.sum(pieces.astype(jnp.float32), 0).reshape(STATES, half, 2, cols)

    base = vector.astype(jnp.float32).reshape(STATES, half, 2, cols)
    sums = jnp.stack([jnp.sum(base * base), jnp.sum(base * image), jnp.sum(image * image)]) / entries
    sums = jnp.broadcast_to(sums[:, None, None], (3, 1, 128))
    sums = summed(summed(sums, (X, Y, C)), Z)[:, 0, 0]
    base_square, correlation, image_square = sums[0], sums[1], sums[2]

    kept = jnp.where(core == 0, image[:, :, 0], image[:, :, 1])
    received = other_core(jnp.where(core == 0, image[:, :, 1], image[:, :, 0]))
    image = jnp.where(
        core == 0, jnp.concatenate([kept, received], 1), jnp.concatenate([received, kept], 1)
    )
    alpha = correlation / (base_square + epsilon)
    residual = image - alpha * start_vector.astype(jnp.float32)
    rho = jnp.sqrt(image_square - 2.0 * alpha * correlation + alpha * alpha * base_square + epsilon)
    return (residual / rho).astype(jnp.bfloat16), jnp.stack([alpha, rho])


def solution(mesh):
    finer = Mesh(mesh.devices.reshape(4, 4, 16, 2), (X, Y, Z, C))
    in_specs = (P(None, ROW, COL), P(None, ROW, COL), P(None, COL, ROW), P(), P())
    out_specs = (P(None, ROW, COL), P())
    return jax.shard_map(body, mesh=finer, in_specs=in_specs, out_specs=out_specs, check_vma=False)
```

time: 264 us -> 178 us (0.67)
  waiting for transfers between devices: 130 us -> 63.4 us
  blocking collectives: 87.1 us -> 48.4 us
  starting transfers between devices: 3.82 us -> 40.6 us
  between operations: 18.9 us -> 3.99 us
  matrix products: 8.74 us -> 0.41 us
  Pallas kernels: 0 us -> 6.26 us
  local copies, waits for them, and re-layouts: 11.7 us -> 6.53 us
  other arithmetic: 3.6 us -> 7.71 us
    reduce_scatter x2 -> x0, waiting for transfers between devices: 81.9 us -> none  [sum_in_order(): pieces = lax.psum_scatter(pieces, axes[k], scatter_dimension=0, tiled=True)]
    psum x4 -> x0, blocking collectives: 64.7 us -> none  [by_axis(): x = lax.psum(x, axis)]
    all_to_all x1 -> x4, waiting for transfers between devices: 14.3 us -> 61.7 us  [the longest x1 45.4 us: body(): pieces = lax.all_to_all(sent, Z, 0, 0, tiled=True)]
    all_gather x0 -> x1, blocking collectives: none -> 38.1 us  [body(): left = lax.all_gather(left.reshape(CHANNELS * half, 2 * cols), Z, axis=0)]
    all_gather x1 -> x0, waiting for transfers between devices: 33.2 us -> none  [body(): lax.all_gather(left_env, COL, axis=2, tiled=True)]
    all_to_all x1 -> x4, starting transfers between devices: 3.7 us -> 30.2 us  [the longest x2 20.2 us: summed(): lax.all_to_all(jnp.broadcast_to(x[None], (size, *x.shape)), axes, 0, 0, t...]
    all_to_all x1, blocking collectives: 22.4 us -> 10.3 us  [swap_of_cores(): halves = lax.all_to_all(halves, C, 0, 0, tiled=True)]
    ppermute x0 -> x2, starting transfers between devices: none -> 10.3 us  [other_core(): return lax.ppermute(x, C, [(0, 1), (1, 0)])]
  transfers between devices with their start and end apart: 4 -> 6, of which waited for: 4 -> 4; matrix products, arithmetic and copies ran while one was open for 2% -> 3% of each run, Pallas kernels for 0% -> 0%
where the time goes in v1:
time: 178 us; the launch traced here: 177 us
  waiting for transfers between devices  63.4 us (36%)
  blocking collectives  48.4 us (27%)
  starting transfers between devices  40.6 us (23%)
  other arithmetic  7.71 us (4%)
  local copies, waits for them, and re-layouts  6.53 us (4%)
  Pallas kernels  6.26 us (4%)
  between operations  3.99 us (2%)
    all_to_all x1, waiting for transfers between devices, body(): pieces = lax.all_to_all(sent, Z, 0, 0, tiled=True)  45.4 us
    all_gather x1, blocking collectives, body(): left = lax.all_gather(left.reshape(CHANNELS * half, 2 * cols), Z, axis=0)  38.1 us
    all_to_all x2, starting transfers between devices, summed(): lax.all_to_all(jnp.broadcast_to(x[None], (size, *x.shape)), axes, 0, 0, t...  20.2 us
    all_to_all x2, waiting for transfers between devices, summed(): lax.all_to_all(jnp.broadcast_to(x[None], (size, *x.shape)), axes, 0, 0, t...  16.3 us
    ppermute x2, starting transfers between devices, other_core(): return lax.ppermute(x, C, [(0, 1), (1, 0)])  10.3 us
    all_to_all x1, blocking collectives, swap_of_cores(): halves = lax.all_to_all(halves, C, 0, 0, tiled=True)  10.3 us
    pallas_call x1, Pallas kernels, terms(): pl.pallas_call(kernel, out_shape=jax.ShapeDtypeStruct((blocks, rows, widt...  6.26 us
    all_to_all x1, starting transfers between devices, body(): pieces = lax.all_to_all(sent, Z, 0, 0, tiled=True)  6.21 us
  transfers between devices with their start and end apart: 6, of which 4 were waited for; matrix products, arithmetic and copies ran while one was open for 3% of the time, Pallas kernels for 0%

profile of v1, /device:TPU:1, one launch (start us, length us, event | category | flops | bytes accessed | tf_op | source)
XLA Modules:
  0.0 177.2 jit_solution(9834648756582325101)
XLA Ops:
  0.6 0.0 copy-start
  0.7 0.9 pad_maximum_fusion
  1.6 0.1 reshape.60
  1.7 0.1 copy.72
  1.8 0.3 reshape.64
  2.1 10.3 %all_to_all.25 = bf16[2,2,18432]{2,1,0:T(2,128)(2,1)S(1)} all-to-all(bf16[2,2,18432]{2,1,0:T(2,128)(2,1)S(1)} %reshape.64), channel_id=1, replica_groups=mesh['row_0'=4,'row_1'=4,'col_0'=16,'col_1'=2] {'col_1'}, dimensions={0} | all-to-all | bytes 294912 | tf_op jit(solution)/shard_map/all_to_all | solution.py:30
  12.4 0.2 reshape.65
  12.6 0.2 copy.49
  12.8 0.1 slice.42
  12.9 0.1 slice.35
  13.1 0.0 copy-done.2
  13.1 1.9 %broadcast_in_dim.7 = bf16[16,576,128]{2,1,0:T(8,128)(2,1)} broadcast(bf16[576,128]{1,0:T(8,128)(2,1)S(1)} %bitcast.37), dimensions={1,2} | broadcast | bytes 2506752 | tf_op jit(solution)/shard_map/broadcast_in_dim | solution.py:114
  15.0 3.9 %all-to-all-start.1 = ((bf16[16,576,128]{2,1,0:T(8,128)(2,1)}), bf16[16,576,128]{2,1,0:T(8,128)(2,1)S(1)}, u32[]{:S(2)}, u32[]{:S(2)}) async-start(bf16[16,576,128]{2,1,0:T(8,128)(2,1)} %broadcast_in_dim.7), calls=%async_computation.1 | async-start | bytes 4718592 | tf_op jit(solution)/shard_map/all_to_all | solution.py:114
  18.8 0.2 multiply_convert_fusion.1
  19.0 0.1 convert_element_type.45
  19.2 38.1 %all-gather.1 = f16[16,320,128]{2,1,0:T(8,128)(2,1)} all-gather(f16[1,320,128]{2,1,0:T(8,128)(2,1)S(1)} %convert_element_type.45), channel_id=1, replica_groups=mesh['row_0'=4,'row_1'=4,'col_0'=16,'col_1'=2] {'col_0'}, dimensions={0}, use_global_device_ids=true | all-gather | bytes 1392640 | tf_op jit(solution)/shard_map/all_gather | solution.py:115
  57.2 0.0 all-to-all-done.1.own_ref
  57.2 8.2 %collective-permute-start = (bf16[16,576,128]{2,1,0:T(8,128)(2,1)S(1)}, bf16[16,576,128]{2,1,0:T(8,128)(2,1)}, u32[]{:S(2)}, u32[]{:S(2)}) collective-permute-start(bf16[16,576,128]{2,1,0:T(8,128)(2,1)S(1)} %all-to-all-done.1.own_ref), channel_id=1, source_target_pairs={{0,1},{1,0},{2,3},{3,2},{4,5},{5,4},{6,7},{7,6},{8,9},{9,8},{10,11... | collective-permute-start | bytes 7077896 | tf_op jit(solution)/shard_map/ppermute | solution.py:35
  65.4 0.0 copy-done
  65.4 0.0 copy-done.3
  65.4 0.4 convolution_bitcast_fusion
  65.9 0.4 copy.47
  66.2 0.1 reshape.59.table_ref
  66.3 1.7 multiply_convert_fusion.left_ref
  68.0 1.7 collective-permute-done.other_ref
  69.7 6.3 %shard_map.68 = bf16[16,256,128]{2,1,0:T(8,128)(2,1)} custom-call(s32[1]{0:T(128)} %bitcast.core_ref, f32[20,20]{1,0:T(8,128)S(1)} %reshape.59.table_ref, bf16[16,320,128]{2,1,0:T(8,128)(2,1)S(1)} %multiply_convert_fusion.left_ref, bf16[16,576,128]{2,1,0:T(8,128)(2,1)S(1)} %all-to-all-done.1.own_ref, bf16[16,576,128]{2,1,0:T(8,128)(2,1)} %collective-permute-done.other_ref), custom_call_target="tpu_custom_call" | custom-call | tf_op jit(solution)/shard_map/pallas_call | solution.py:78
  75.9 6.2 %all-to-all-start.2 = ((bf16[16,256,128]{2,1,0:T(8,128)(2,1)}), bf16[16,256,128]{2,1,0:T(8,128)(2,1)S(1)}, u32[]{:S(2)}, u32[]{:S(2)}) async-start(bf16[16,256,128]{2,1,0:T(8,128)(2,1)} %shard_map.68), calls=%async_computation.2 | async-start | bytes 2097152 | tf_op jit(solution)/shard_map/all_to_all | solution.py:121
  82.2 0.1 copy.56
  82.3 45.4 %all-to-all-done.2 = bf16[16,256,128]{2,1,0:T(8,128)(2,1)S(1)} async-done(((bf16[16,256,128]{2,1,0:T(8,128)(2,1)}), bf16[16,256,128]{2,1,0:T(8,128)(2,1)S(1)}, u32[]{:S(2)}, u32[]{:S(2)}) %all-to-all-start.2) | async-done | bytes 1048608 | tf_op jit(solution)/shard_map/all_to_all | solution.py:121
  127.7 0.1 convert_reduce_fusion
  127.8 0.6 multiply_reduce_fusion
  128.4 0.2 reshape.61
  128.6 1.1 fusion
  129.7 2.1 %maximum_multiply_fusion = f32[3]{0:T(128)S(1)} fusion(f32[1]{0:T(128)} %bitcast.13, f32[1]{0:T(128)} %bitcast.12, f32[1]{0:T(128)} %bitcast.11), kind=kLoop, calls=%fused_computation.19 | loop fusion | flops 9 | bytes 24 | tf_op jit(solution)/shard_map/div | solution.py:125
  131.8 0.7 broadcast_in_dim_broadcast_in_dim_broadcast_in_dim.2
  132.5 12.5 %all-to-all-start.3 = ((f32[32,3,1,128]{3,2,1,0:T(1,128)}), f32[32,3,1,128]{3,2,1,0:T(1,128)S(1)}, u32[]{:S(2)}, u32[]{:S(2)}) async-start(f32[32,3,1,128]{3,2,1,0:T(1,128)} %broadcast_in_dim_broadcast_in_dim_broadcast_in_dim.2), calls=%async_computation.3 | async-start | bytes 98304 | tf_op jit(solution)/shard_map/all_to_all | solution.py:96
  145.0 0.2 broadcast_select_fusion
  145.2 2.1 %collective-permute-start.1 = (f32[4,64,64]{2,1,0:T(8,128)S(1)}, f32[4,64,64]{2,1,0:T(8,128)S(1)}, u32[]{:S(2)}, u32[]{:S(2)}) collective-permute-start(f32[4,64,64]{2,1,0:T(8,128)S(1)} %bitcast.40), channel_id=1, source_target_pairs={{0,1},{1,0},{2,3},{3,2},{4,5},{5,4},{6,7},{7,6},{8,9},{9,8},{10,11... | collective-permute-start | bytes 196616 | tf_op jit(solution)/shard_map/ppermute | solution.py:35
  147.4 4.9 %all-to-all-done.3 = f32[32,3,1,128]{3,2,1,0:T(1,128)S(1)} async-done(((f32[32,3,1,128]{3,2,1,0:T(1,128)}), f32[32,3,1,128]{3,2,1,0:T(1,128)S(1)}, u32[]{:S(2)}, u32[]{:S(2)}) %all-to-all-start.3) | async-done | bytes 49184 | tf_op jit(solution)/shard_map/all_to_all | solution.py:96
  152.3 0.1 reduce_sum.60
  152.4 0.6 broadcast_in_dim.16
  153.0 7.7 %all-to-all-start.4 = ((f32[16,3,1,128]{3,2,1,0:T(1,128)}), f32[16,3,1,128]{3,2,1,0:T(1,128)S(1)}, u32[]{:S(2)}, u32[]{:S(2)}) async-start(f32[16,3,1,128]{3,2,1,0:T(1,128)} %broadcast_in_dim.16), calls=%async_computation.4 | async-start | bytes 49152 | tf_op jit(solution)/shard_map/all_to_all | solution.py:96
  160.7 11.4 %all-to-all-done.4 = f32[16,3,1,128]{3,2,1,0:T(1,128)S(1)} async-done(((f32[16,3,1,128]{3,2,1,0:T(1,128)}), f32[16,3,1,128]{3,2,1,0:T(1,128)S(1)}, u32[]{:S(2)}, u32[]{:S(2)}) %all-to-all-start.4) | async-done | bytes 24608 | tf_op jit(solution)/shard_map/all_to_all | solution.py:96
  172.2 0.5 fusion.7
  175.8 0.0 collective-permute-done.1
  175.8 0.1 fusion.4
  175.9 0.7 copy.57
  176.6 0.6 pad_maximum_fusion.2
  (7 shorter events, 0.1 us)
Async XLA Ops:
  0.6 64.8 %copy-start = (f32[5,5,2,2]{1,3,2,0:T(2,128)S(1)}, f32[5,5,2,2]{1,3,2,0:T(2,128)}, u32[]{:S(2)}) copy-start(f32[5,5,2,2]{1,3,2,0:T(2,128)} %param.8) | copy-start | bytes 1204
  0.6 12.4 %copy-start.2 = (bf16[5,64,128]{2,1,0:T(8,128)(2,1)S(1)}, bf16[5,64,128]{2,1,0:T(8,128)(2,1)}, u32[]{:S(2)}) copy-start(bf16[5,64,128]{2,1,0:T(8,128)(2,1)} %param.7) | copy-start | bytes 245764
  15.0 50.5 %copy-start.3 = (f32[5,5,2,2]{1,3,2,0:T(2,128)S(1)}, f32[5,5,2,2]{1,3,2,0:T(2,128)}, u32[]{:S(2)}) copy-start(f32[5,5,2,2]{1,3,2,0:T(2,128)} %param.9) | copy-start | bytes 1204
  15.0 42.3 %all-to-all-start.1 = ((bf16[16,576,128]{2,1,0:T(8,128)(2,1)}), bf16[16,576,128]{2,1,0:T(8,128)(2,1)S(1)}, u32[]{:S(2)}, u32[]{:S(2)}) async-start(bf16[16,576,128]{2,1,0:T(8,128)(2,1)} %broadcast_in_dim.7), calls=%async_computation.1 | async-start | bytes 4718592 | tf_op jit(solution)/shard_map/all_to_all | solution.py:114
  57.2 12.5 %collective-permute-start = (bf16[16,576,128]{2,1,0:T(8,128)(2,1)S(1)}, bf16[16,576,128]{2,1,0:T(8,128)(2,1)}, u32[]{:S(2)}, u32[]{:S(2)}) collective-permute-start(bf16[16,576,128]{2,1,0:T(8,128)(2,1)S(1)} %all-to-all-done.1.own_ref), channel_id=1, source_target_pairs={{0,1},{1,0},{2,3},{3,2},{4,5},{5,4},{6,7},{7,6},{8,9},{9,8},{10,11... | collective-permute-start | bytes 7077896 | tf_op jit(solution)/shard_map/ppermute | solution.py:35
  69.7 12.5 %copy-start.1 = (bf16[4,128,64]{1,2,0:T(8,128)(2,1)S(1)}, bf16[4,128,64]{1,2,0:T(8,128)(2,1)}, u32[]{:S(2)}) copy-start(bf16[4,128,64]{1,2,0:T(8,128)(2,1)} %param.5) | copy-start | bytes 196612
  75.9 51.7 %all-to-all-start.2 = ((bf16[16,256,128]{2,1,0:T(8,128)(2,1)}), bf16[16,256,128]{2,1,0:T(8,128)(2,1)S(1)}, u32[]{:S(2)}, u32[]{:S(2)}) async-start(bf16[16,256,128]{2,1,0:T(8,128)(2,1)} %shard_map.68), calls=%async_computation.2 | async-start | bytes 2097152 | tf_op jit(solution)/shard_map/all_to_all | solution.py:121
  132.5 19.8 %all-to-all-start.3 = ((f32[32,3,1,128]{3,2,1,0:T(1,128)}), f32[32,3,1,128]{3,2,1,0:T(1,128)S(1)}, u32[]{:S(2)}, u32[]{:S(2)}) async-start(f32[32,3,1,128]{3,2,1,0:T(1,128)} %broadcast_in_dim_broadcast_in_dim_broadcast_in_dim.2), calls=%async_computation.3 | async-start | bytes 98304 | tf_op jit(solution)/shard_map/all_to_all | solution.py:96
  145.2 30.5 %collective-permute-start.1 = (f32[4,64,64]{2,1,0:T(8,128)S(1)}, f32[4,64,64]{2,1,0:T(8,128)S(1)}, u32[]{:S(2)}, u32[]{:S(2)}) collective-permute-start(f32[4,64,64]{2,1,0:T(8,128)S(1)} %bitcast.40), channel_id=1, source_target_pairs={{0,1},{1,0},{2,3},{3,2},{4,5},{5,4},{6,7},{7,6},{8,9},{9,8},{10,11... | collective-permute-start | bytes 196616 | tf_op jit(solution)/shard_map/ppermute | solution.py:35
  153.0 19.1 %all-to-all-start.4 = ((f32[16,3,1,128]{3,2,1,0:T(1,128)}), f32[16,3,1,128]{3,2,1,0:T(1,128)S(1)}, u32[]{:S(2)}, u32[]{:S(2)}) async-start(f32[16,3,1,128]{3,2,1,0:T(1,128)} %broadcast_in_dim.16), calls=%async_computation.4 | async-start | bytes 49152 | tf_op jit(solution)/shard_map/all_to_all | solution.py:96

commit v2 on v1

v2 whole, which is shorter than its diff:
```python
import jax
import jax.numpy as jnp
from jax import lax
from jax.experimental import pallas as pl
from jax.experimental.pallas import tpu as pltpu
from jax.sharding import Mesh
from jax.sharding import PartitionSpec as P

X, Y, Z, C = "row_0", "row_1", "col_0", "col_1"
ROW = (X, Y)
COL = (Z, C)
STATES = 4
CHANNELS = 5
PAIRS = STATES * CHANNELS

epsilon = 1e-06
SCALE = 8192.0

VMEM = pl.BlockSpec(memory_space=pltpu.VMEM)
SMEM = pl.BlockSpec(memory_space=pltpu.SMEM)
PARAMS = pltpu.CompilerParams(vmem_limit_bytes=48 * 1024 * 1024)


def coupling(left_tensor, right_tensor):
    joined = jnp.einsum(
        "wuac,uvbd->vabwcd", left_tensor, right_tensor, precision=lax.Precision.HIGHEST
    )
    return joined.reshape(PAIRS, PAIRS)


def pack_kernel(vector_ref, right_ref, out_ref):
    states, half, width = vector_ref.shape
    for r in range(out_ref.shape[0]):
        for t in range(states):
            out_ref[r, t * half : (t + 1) * half, :] = vector_ref[t]
    for v in range(right_ref.shape[0]):
        turned = right_ref[v].astype(jnp.float32).T
        turned = jnp.concatenate([turned[:half], turned[half:]], 1).astype(jnp.bfloat16)
        at = (states + v) * half
        for r in range(out_ref.shape[0]):
            out_ref[r, at : at + half, :] = turned


def pack(vector, right, size):
    states, half, width = vector.shape
    rows = (states + right.shape[0]) * half
    return pl.pallas_call(
        pack_kernel,
        out_shape=jax.ShapeDtypeStruct((size, rows, width), jnp.bfloat16),
        in_specs=[VMEM, VMEM],
        out_specs=VMEM,
        compiler_params=PARAMS,
    )(vector, right)


def terms_kernel(core_ref, table_ref, left_own, left_other, own_ref, other_ref, out_ref, vec_s, left_s, right_s, cross_s, mixed_s):
    blocks, half, _ = out_ref.shape
    width = 2 * half
    core = core_ref[0]
    own_at = pl.multiple_of(core * half, half)
    other_at = pl.multiple_of((1 - core) * half, half)
    for r in range(blocks):
        for source, left, at in ((own_ref, left_own, own_at), (other_ref, left_other, other_at)):
            for t in range(STATES):
                vec_s[pl.ds(t * width + at, half), r * width : (r + 1) * width] = source[r, t * half : (t + 1) * half, :]
            for w in range(CHANNELS):
                left_s[pl.ds(r * width + at, half), w * width : (w + 1) * width] = left[r, w * half : (w + 1) * half, :]
    cross_s[...] = jnp.dot(vec_s[...], left_s[...], preferred_element_type=jnp.float32)
    for v in range(CHANNELS):
        for s in range(STATES):
            total = None
            for w in range(CHANNELS):
                for t in range(STATES):
                    part = (
                        table_ref[v * STATES + s, w * STATES + t]
                        * cross_s[t * width : (t + 1) * width, w * width : (w + 1) * width]
                    )
                    total = part if total is None else total + part
            mixed_s[v * width : (v + 1) * width, s * width : (s + 1) * width] = total.astype(jnp.bfloat16)
    mine = lax.broadcasted_iota(jnp.int32, (half, width), 1) // half == core
    for r in range(blocks):
        for v in range(CHANNELS):
            at = (STATES + v) * half
            own = own_ref[r, at : at + half, :].astype(jnp.float32)
            other = other_ref[r, at : at + half, :].astype(jnp.float32)
            other = jnp.concatenate([other[:, half:], other[:, :half]], 1)
            right_s[r * half : (r + 1) * half, v * width : (v + 1) * width] = jnp.where(mine, own, other).astype(jnp.bfloat16)
    image = jnp.dot(right_s[...], mixed_s[...], preferred_element_type=jnp.float32)
    for r in range(blocks):
        out_ref[r] = image[r * half : (r + 1) * half].astype(jnp.bfloat16)


def terms(core, table, left_own, left_other, own, other):
    blocks, left_rows, width = left_own.shape
    half = left_rows // CHANNELS
    return pl.pallas_call(
        terms_kernel,
        out_shape=jax.ShapeDtypeStruct((blocks, half, STATES * width), jnp.bfloat16),
        in_specs=[SMEM, SMEM, VMEM, VMEM, VMEM, VMEM],
        out_specs=VMEM,
        scratch_shapes=[
            pltpu.VMEM((STATES * width, blocks * width), jnp.bfloat16),
            pltpu.VMEM((blocks * width, CHANNELS * width), jnp.bfloat16),
            pltpu.VMEM((blocks * half, CHANNELS * width), jnp.bfloat16),
            pltpu.VMEM((STATES * width, CHANNELS * width), jnp.float32),
            pltpu.VMEM((CHANNELS * width, STATES * width), jnp.bfloat16),
        ],
        compiler_params=PARAMS,
    )(core, table, left_own, left_other, own, other)


def lanes_of(total):
    rows, cols = total.shape
    total = sum(total[:, k : k + 128] for k in range(0, cols, 128))
    return sum(total[k : k + 8] for k in range(0, rows, 8))


def sums_kernel(pieces_ref, vector_ref, image_ref, sums_ref):
    image = pieces_ref[0].astype(jnp.float32)
    for k in range(1, pieces_ref.shape[0]):
        image = image + pieces_ref[k].astype(jnp.float32)
    image_ref[...] = image
    base = jnp.concatenate([vector_ref[t].astype(jnp.float32) for t in range(STATES)], 1)
    found = [lanes_of(base * base), lanes_of(base * image), lanes_of(image * image)]
    found = [jnp.broadcast_to(jnp.sum(f, keepdims=True), (1, 128)) for f in found]
    found = jnp.concatenate([*found, jnp.zeros((5, 128), jnp.float32)], 0)
    for r in range(sums_ref.shape[0]):
        sums_ref[r] = found


def sums_of(pieces, vector, size):
    return pl.pallas_call(
        sums_kernel,
        out_shape=(
            jax.ShapeDtypeStruct(pieces.shape[1:], jnp.float32),
            jax.ShapeDtypeStruct((size, 8, 128), jnp.float32),
        ),
        in_specs=[VMEM, VMEM],
        out_specs=(VMEM, VMEM),
        compiler_params=PARAMS,
    )(pieces, vector)


def again_kernel(pieces_ref, out_ref):
    total = pieces_ref[0]
    for k in range(1, pieces_ref.shape[0]):
        total = total + pieces_ref[k]
    for r in range(out_ref.shape[0]):
        out_ref[r] = total


def again(pieces, size):
    return pl.pallas_call(
        again_kernel,
        out_shape=jax.ShapeDtypeStruct((size, *pieces.shape[1:]), jnp.float32),
        in_specs=[VMEM],
        out_specs=VMEM,
        compiler_params=PARAMS,
    )(pieces)


def last_kernel(entries, pieces_ref, image_ref, vector_ref, next_ref, coefficients_ref):
    total = pieces_ref[0]
    for k in range(1, pieces_ref.shape[0]):
        total = total + pieces_ref[k]
    total = total / entries
    base_square, correlation, image_square = total[0:1], total[1:2], total[2:3]
    alpha = correlation / (base_square + epsilon)
    rho = jnp.sqrt(image_square - 2.0 * alpha * correlation + alpha * alpha * base_square + epsilon)
    width = next_ref.shape[2]
    for t in range(STATES):
        residual = image_ref[:, t * width : (t + 1) * width] - alpha * vector_ref[t].astype(jnp.float32)
        next_ref[t] = (residual / rho).astype(jnp.bfloat16)
    coefficients_ref[0] = alpha[0, 0]
    coefficients_ref[1] = rho[0, 0]


def last(entries, pieces, image, vector):
    def step(*refs):
        last_kernel(entries, *refs)

    return pl.pallas_call(
        step,
        out_shape=(
            jax.ShapeDtypeStruct(vector.shape, jnp.bfloat16),
            jax.ShapeDtypeStruct((2,), jnp.float32),
        ),
        in_specs=[VMEM, VMEM, VMEM],
        out_specs=(VMEM, SMEM),
        compiler_params=PARAMS,
    )(pieces, image, vector)


def all_to_all(x, axes):
    return lax.all_to_all(x, axes, 0, 0, tiled=True)


def other_core(x):
    return lax.ppermute(x, C, [(0, 1), (1, 0)])


def body(start_vector, left_env, right_env, left_tensor, right_tensor):
    n_row = lax.axis_size(ROW)
    n_z = lax.axis_size(Z)
    _, rows, half = start_vector.shape
    entries = float(STATES * rows * half * n_row * n_z * lax.axis_size(C))
    core = lax.axis_index(C).astype(jnp.int32).reshape(1)
    table = coupling(left_tensor, right_tensor)
    vector = jnp.swapaxes(start_vector, 1, 2)
    left = jnp.swapaxes(left_env, 1, 2).reshape(CHANNELS * half, rows)
    left = (left.astype(jnp.float32) * SCALE).astype(jnp.float16)

    own = all_to_all(pack(vector, right_env, n_row), ROW)
    left = lax.all_gather(left, Z, axis=0)
    own, left = lax.optimization_barrier((own, left))
    left = (left.astype(jnp.float32) * (1.0 / SCALE)).astype(jnp.bfloat16)
    sent = terms(core, table, left, other_core(left), own, other_core(own))

    pieces = all_to_all(sent, Z)
    image, sums = sums_of(pieces, vector, lax.axis_size((X, Y, C)))
    sums = again(all_to_all(sums, (X, Y, C)), n_z)
    next_vector, coefficients = last(entries, all_to_all(sums, Z), image, vector)
    return jnp.swapaxes(next_vector, 1, 2), coefficients


def solution(mesh):
    finer = Mesh(mesh.devices.reshape(4, 4, 16, 2), (X, Y, Z, C))
    in_specs = (P(None, ROW, COL), P(None, ROW, COL), P(None, COL, ROW), P(), P())
    out_specs = (P(None, ROW, COL), P())
    return jax.shard_map(body, mesh=finer, in_specs=in_specs, out_specs=out_specs, check_vma=False)
```

time: 178 us -> 169 us (0.949)
  blocking collectives: 48.4 us -> 131 us
  waiting for transfers between devices: 63.4 us -> 2.42 us
  starting transfers between devices: 40.6 us -> 18.3 us
  other arithmetic: 7.71 us -> 2.78 us
  between operations: 3.99 us -> 0.76 us
  Pallas kernels: 6.26 us -> 9.25 us
  local copies, waits for them, and re-layouts: 6.53 us -> 3.65 us
    all_to_all x1 -> x3, blocking collectives: 10.3 us -> 90.8 us  [all_to_all(): return lax.all_to_all(x, axes, 0, 0, tiled=True)]
    all_to_all x4 -> x1, waiting for transfers between devices: 61.7 us -> 0.01 us  [all_to_all(): return lax.all_to_all(x, axes, 0, 0, tiled=True)]
    all_to_all x4 -> x1, starting transfers between devices: 30.2 us -> 7.7 us  [all_to_all(): return lax.all_to_all(x, axes, 0, 0, tiled=True)]
    pallas_call x1 -> x5, Pallas kernels: 6.26 us -> 9.25 us  [the longest x1 7.83 us: terms(): pl.pallas_call(terms_kernel, out_shape=jax.ShapeDtypeStruct((blocks, half...]
    broadcast_in_dim x2 -> x0, local copies, waits for them, and re-layouts: 2.49 us -> none  [the longest x1 1.87 us: body(): jnp.broadcast_to(mine, (n_row, *mine.shape[1:]))]
    div x1 -> x0, other arithmetic: 2.06 us -> none  [body(): jnp.stack([jnp.sum(base * base), jnp.sum(base * image), jnp.sum(image * i...]
    reduce_sum x5 -> x0, other arithmetic: 1.96 us -> none  [the longest x1 1.08 us: body(): jnp.sum(base * base)]
    all_gather x1, blocking collectives: 38.1 us -> 40 us  [body(): left = lax.all_gather(left, Z, axis=0)]
  transfers between devices with their start and end apart: 6 -> 3, of which waited for: 4 -> 1; matrix products, arithmetic and copies ran while one was open for 3% -> 2% of each run, Pallas kernels for 0% -> 0%
where the time goes in v2:
time: 169 us; the launch traced here: 168 us
  blocking collectives  131 us (78%)
  starting transfers between devices  18.3 us (11%)
  Pallas kernels  9.25 us (5%)
  local copies, waits for them, and re-layouts  3.65 us (2%)
  other arithmetic  2.78 us (2%)
  waiting for transfers between devices  2.42 us (1%)
    all_to_all x3, blocking collectives, all_to_all(): return lax.all_to_all(x, axes, 0, 0, tiled=True)  90.8 us
    all_gather x1, blocking collectives, body(): left = lax.all_gather(left, Z, axis=0)  40 us
    ppermute x2, starting transfers between devices, other_core(): return lax.ppermute(x, C, [(0, 1), (1, 0)])  10.6 us
    pallas_call x1, Pallas kernels, terms(): pl.pallas_call(terms_kernel, out_shape=jax.ShapeDtypeStruct((blocks, half...  7.83 us
    all_to_all x1, starting transfers between devices, all_to_all(): return lax.all_to_all(x, axes, 0, 0, tiled=True)  7.7 us
  transfers between devices with their start and end apart: 3, of which 1 were waited for; matrix products, arithmetic and copies ran while one was open for 2% of the time, Pallas kernels for 0%

profile of v2, /device:TPU:1, one launch (start us, length us, event | category | flops | bytes accessed | tf_op | source)
XLA Modules:
  0.0 168.4 jit_solution(6577873109076691652)
XLA Ops:
  0.6 0.0 copy-start
  0.6 0.0 copy-start.2
  0.7 0.8 copy-done.2
  1.5 0.0 copy-start.4
  1.5 0.9 copy-done.4
  2.4 0.4 shard_map.68
  2.8 0.0 copy-start.1
  2.8 1.4 copy-done.1
  4.2 0.0 copy-start.5
  4.2 7.7 %all-to-all-start = ((bf16[16,576,128]{2,1,0:T(8,128)(2,1)}), bf16[16,576,128]{2,1,0:T(8,128)(2,1)S(1)}, u32[]{:S(2)}, u32[]{:S(2)}) async-start(bf16[16,576,128]{2,1,0:T(8,128)(2,1)} %copy-done.1), calls=%async_computation | async-start | bytes 4718592 | tf_op jit(solution)/shard_map/all_to_all | solution.py:195
  11.9 0.0 copy-done.5
  11.9 0.0 copy-start.6
  12.0 40.0 %all-gather.1 = f16[16,320,128]{2,1,0:T(8,128)(2,1)} all-gather(f16[1,320,128]{2,1,0:T(8,128)(2,1)S(1)} %bitcast.14), channel_id=1, replica_groups=mesh['row_0'=4,'row_1'=4,'col_0'=16,'col_1'=2] {'col_0'}, dimensions={0}, use_global_device_ids=true | all-gather | bytes 1392640 | tf_op jit(solution)/shard_map/all_gather | solution.py:214
  51.9 0.0 all-to-all-done.own_ref
  51.9 8.7 %collective-permute-start.1 = (bf16[16,576,128]{2,1,0:T(8,128)(2,1)S(1)}, bf16[16,576,128]{2,1,0:T(8,128)(2,1)}, u32[]{:S(2)}, u32[]{:S(2)}) collective-permute-start(bf16[16,576,128]{2,1,0:T(8,128)(2,1)S(1)} %all-to-all-done.own_ref), channel_id=1, source_target_pairs={{0,1},{1,0},{2,3},{3,2},{4,5},{5,4},{6,7},{7,6},{8,9},{9,8},{10,11... | collective-permute-start | bytes 7077896 | tf_op jit(solution)/shard_map/ppermute | solution.py:199
  60.6 2.8 %multiply_convert_fusion.left_own = bf16[16,320,128]{2,1,0:T(8,128)(2,1)} fusion(f16[16,320,128]{2,1,0:T(8,128)(2,1)} %all-gather.1), kind=kLoop, calls=%fused_computation | loop fusion | flops 1966080 | bytes 2621440 | tf_op jit(solution)/shard_map/convert_element_type | solution.py:216
  63.4 1.9 %collective-permute-start = (bf16[16,320,128]{2,1,0:T(8,128)(2,1)}, bf16[16,320,128]{2,1,0:T(8,128)(2,1)}, u32[]{:S(2)}, u32[]{:S(2)}) collective-permute-start(bf16[16,320,128]{2,1,0:T(8,128)(2,1)} %multiply_convert_fusion.left_own), channel_id=1, source_target_pairs={{0,1},{1,0},{2,3},{3,2},{4,5},{5,4},{6,7},{7,6},{8,9},{9,8},{10,11... | collective-permute-start | bytes 3932168 | tf_op jit(solution)/shard_map/ppermute | solution.py:199
  65.3 0.0 copy-done
  65.3 0.0 copy-done.6
  65.3 0.4 convolution_bitcast_fusion
  65.8 0.4 copy.15
  66.1 0.1 reshape.32.table_ref
  66.3 2.4 %collective-permute-done.left_other = bf16[16,320,128]{2,1,0:T(8,128)(2,1)} collective-permute-done((bf16[16,320,128]{2,1,0:T(8,128)(2,1)}, bf16[16,320,128]{2,1,0:T(8,128)(2,1)}, u32[]{:S(2)}, u32[]{:S(2)}) %collective-permute-start) | collective-permute-done | bytes 1310752 | tf_op jit(solution)/shard_map/ppermute | solution.py:199
  68.7 0.0 collective-permute-done.1.other_ref
  68.7 0.0 copy-start.3
  68.7 7.8 %shard_map.69 = bf16[16,64,512]{2,1,0:T(8,128)(2,1)S(1)} custom-call(s32[1]{0:T(128)} %bitcast.core_ref, f32[20,20]{1,0:T(8,128)S(1)} %reshape.32.table_ref, bf16[16,320,128]{2,1,0:T(8,128)(2,1)} %multiply_convert_fusion.left_own, bf16[16,320,128]{2,1,0:T(8,128)(2,1)} %collective-permute-done.left_other, bf16[16,576,128]{2,1,0:T(8,128)(2,1)S(1)} %all-to-all-done.own_ref, ...), custom_call_target="tpu_custom_call" | custom-call | tf_op jit(solution)/shard_map/pallas_call | solution.py:96
  76.5 51.8 %all_to_all.20.pieces_ref = bf16[16,64,512]{2,1,0:T(8,128)(2,1)S(1)} all-to-all(bf16[16,64,512]{2,1,0:T(8,128)(2,1)S(1)} %shard_map.69), channel_id=1, replica_groups=mesh['row_0'=4,'row_1'=4,'col_0'=16,'col_1'=2] {'col_0'}, dimensions={0} | all-to-all | bytes 2097152 | tf_op jit(solution)/shard_map/all_to_all | solution.py:195
  128.3 0.0 copy-done.3
  128.3 0.3 shard_map.70
  128.6 21.5 %all_to_all.21.pieces_ref = f32[32,8,128]{2,1,0:T(8,128)S(1)} all-to-all(f32[32,8,128]{2,1,0:T(8,128)S(1)} %get-tuple-element.10), channel_id=1, replica_groups=mesh['row_0'=4,'row_1'=4,'col_0'=16,'col_1'=2] {'row_0','row_1','col_1'}, dimensions={0} | all-to-all | bytes 262144 | tf_op jit(solution)/shard_map/all_to_all | solution.py:195
  150.2 17.5 %all_to_all.22.refs_0_ = f32[16,8,128]{2,1,0:T(8,128)S(1)} all-to-all(f32[16,8,128]{2,1,0:T(8,128)S(1)} %shard_map.71), channel_id=1, replica_groups=mesh['row_0'=4,'row_1'=4,'col_0'=16,'col_1'=2] {'col_0'}, dimensions={0} | all-to-all | bytes 131072 | tf_op jit(solution)/shard_map/all_to_all | solution.py:195
  167.7 0.7 shard_map.72
  (2 shorter events, 0.1 us)
Async XLA Ops:
  0.6 64.7 %copy-start = (f32[5,5,2,2]{1,3,2,0:T(2,128)S(1)}, f32[5,5,2,2]{1,3,2,0:T(2,128)}, u32[]{:S(2)}) copy-start(f32[5,5,2,2]{1,3,2,0:T(2,128)} %param.8) | copy-start | bytes 1204
  0.6 0.8 copy-start.2
  1.5 0.9 copy-start.4
  2.8 1.4 copy-start.1
  4.2 7.7 %copy-start.5 = (bf16[5,128,64]{1,2,0:T(8,128)(2,1)S(1)}, bf16[5,128,64]{1,2,0:T(8,128)(2,1)}, u32[]{:S(2)}) copy-start(bf16[5,128,64]{1,2,0:T(8,128)(2,1)} %param.6) | copy-start | bytes 245764
  4.2 47.7 %all-to-all-start = ((bf16[16,576,128]{2,1,0:T(8,128)(2,1)}), bf16[16,576,128]{2,1,0:T(8,128)(2,1)S(1)}, u32[]{:S(2)}, u32[]{:S(2)}) async-start(bf16[16,576,128]{2,1,0:T(8,128)(2,1)} %copy-done.1), calls=%async_computation | async-start | bytes 4718592 | tf_op jit(solution)/shard_map/all_to_all | solution.py:195
  11.9 53.4 %copy-start.6 = (f32[5,5,2,2]{1,3,2,0:T(2,128)S(1)}, f32[5,5,2,2]{1,3,2,0:T(2,128)}, u32[]{:S(2)}) copy-start(f32[5,5,2,2]{1,3,2,0:T(2,128)} %param.9) | copy-start | bytes 1204
  51.9 16.7 %collective-permute-start.1 = (bf16[16,576,128]{2,1,0:T(8,128)(2,1)S(1)}, bf16[16,576,128]{2,1,0:T(8,128)(2,1)}, u32[]{:S(2)}, u32[]{:S(2)}) collective-permute-start(bf16[16,576,128]{2,1,0:T(8,128)(2,1)S(1)} %all-to-all-done.own_ref), channel_id=1, source_target_pairs={{0,1},{1,0},{2,3},{3,2},{4,5},{5,4},{6,7},{7,6},{8,9},{9,8},{10,11... | collective-permute-start | bytes 7077896 | tf_op jit(solution)/shard_map/ppermute | solution.py:199
  63.4 5.3 %collective-permute-start = (bf16[16,320,128]{2,1,0:T(8,128)(2,1)}, bf16[16,320,128]{2,1,0:T(8,128)(2,1)}, u32[]{:S(2)}, u32[]{:S(2)}) collective-permute-start(bf16[16,320,128]{2,1,0:T(8,128)(2,1)} %multiply_convert_fusion.left_own), channel_id=1, source_target_pairs={{0,1},{1,0},{2,3},{3,2},{4,5},{5,4},{6,7},{7,6},{8,9},{9,8},{10,11... | collective-permute-start | bytes 3932168 | tf_op jit(solution)/shard_map/ppermute | solution.py:199
  68.7 59.7 %copy-start.3 = (bf16[4,128,64]{1,2,0:T(8,128)(2,1)S(1)}, bf16[4,128,64]{1,2,0:T(8,128)(2,1)}, u32[]{:S(2)}) copy-start(bf16[4,128,64]{1,2,0:T(8,128)(2,1)} %param.5) | copy-start | bytes 196612

commit v3 on v2

--- a/solution.py
+++ b/solution.py
@@ -18,53 +18,72 @@
 
 VMEM = pl.BlockSpec(memory_space=pltpu.VMEM)
 SMEM = pl.BlockSpec(memory_space=pltpu.SMEM)
-PARAMS = pltpu.CompilerParams(vmem_limit_bytes=48 * 1024 * 1024)
+SMALL = pltpu.CompilerParams(vmem_limit_bytes=4 * 1024 * 1024)
+LARGE = pltpu.CompilerParams(vmem_limit_bytes=24 * 1024 * 1024)
 
 
 def coupling(left_tensor, right_tensor):
-    joined = jnp.einsum(
-        "wuac,uvbd->vabwcd", left_tensor, right_tensor, precision=lax.Precision.HIGHEST
-    )
+    joined = jnp.einsum("wuac,uvbd->vabwcd", left_tensor, right_tensor, precision=lax.Precision.HIGHEST)
     return joined.reshape(PAIRS, PAIRS)
 
 
-def pack_kernel(vector_ref, right_ref, out_ref):
-    states, half, width = vector_ref.shape
-    for r in range(out_ref.shape[0]):
-        for t in range(states):
-            out_ref[r, t * half : (t + 1) * half, :] = vector_ref[t]
-    for v in range(right_ref.shape[0]):
-        turned = right_ref[v].astype(jnp.float32).T
+def pack_kernel(vector_hbm, right_hbm, out_hbm, vector_s, right_s, piece_s, in_sems, out_sems):
+    states, half, width = vector_s.shape
+    rights = right_s.shape[0]
+    loads = [
+        pltpu.make_async_copy(vector_hbm, vector_s, in_sems.at[0]),
+        pltpu.make_async_copy(right_hbm, right_s, in_sems.at[1]),
+    ]
+    for load in loads:
+        load.start()
+    loads[0].wait()
+    for t in range(states):
+        piece_s[t * half : (t + 1) * half, :] = vector_s[t]
+    loads[1].wait()
+    for v in range(rights):
+        turned = right_s[v].astype(jnp.float32).T
         turned = jnp.concatenate([turned[:half], turned[half:]], 1).astype(jnp.bfloat16)
-        at = (states + v) * half
-        for r in range(out_ref.shape[0]):
-            out_ref[r, at : at + half, :] = turned
+        piece_s[(states + v) * half : (states + v + 1) * half, :] = turned
+    stores = [pltpu.make_async_copy(piece_s, out_hbm.at[r], out_sems.at[r]) for r in range(out_hbm.shape[0])]
+    for store in stores:
+        store.start()
+    for store in stores:
+        store.wait()
 
 
 def pack(vector, right, size):
     states, half, width = vector.shape
     rows = (states + right.shape[0]) * half
+    hbm = pl.BlockSpec(memory_space=pltpu.HBM)
     return pl.pallas_call(
         pack_kernel,
-        out_shape=jax.ShapeDtypeStruct((size, rows, width), jnp.bfloat16),
-        in_specs=[VMEM, VMEM],
-        out_specs=VMEM,
-        compiler_params=PARAMS,
-    )(vector, right)
-
-
-def terms_kernel(core_ref, table_ref, left_own, left_other, own_ref, other_ref, out_ref, vec_s, left_s, right_s, cross_s, mixed_s):
+        out_shape=pltpu.HBM((size, rows, width), jnp.bfloat16),
+        in_specs=[hbm, hbm],
+        out_specs=hbm,
+        scratch_shapes=[
+            pltpu.VMEM(vector.shape, jnp.bfloat16),
+            pltpu.VMEM(right.shape, jnp.bfloat16),
+            pltpu.VMEM((rows, width), jnp.bfloat16),
+            pltpu.SemaphoreType.DMA((2,)),
+            pltpu.SemaphoreType.DMA((size,)),
+        ],
+        compiler_params=SMALL,
+    )(pltpu.with_memory_space_constraint(vector, pltpu.HBM), pltpu.with_memory_space_constraint(right, pltpu.HBM))
+
+
+def terms_kernel(core_ref, table_ref, left_ref, own_ref, other_ref, out_ref, vec_s, left_s, right_s, cross_s, mixed_s):
     blocks, half, _ = out_ref.shape
     width = 2 * half
     core = core_ref[0]
     own_at = pl.multiple_of(core * half, half)
     other_at = pl.multiple_of((1 - core) * half, half)
     for r in range(blocks):
-        for source, left, at in ((own_ref, left_own, own_at), (other_ref, left_other, other_at)):
+        for source, at in ((own_ref, own_at), (other_ref, other_at)):
             for t in range(STATES):
                 vec_s[pl.ds(t * width + at, half), r * width : (r + 1) * width] = source[r, t * half : (t + 1) * half, :]
-            for w in range(CHANNELS):
-                left_s[pl.ds(r * width + at, half), w * width : (w + 1) * width] = left[r, w * half : (w + 1) * half, :]
+    for r in range(left_ref.shape[0]):
+        for w in range(CHANNELS):
+            left_s[r * half : (r + 1) * half, w * width : (w + 1) * width] = left_ref[r, w * half : (w + 1) * half, :]
     cross_s[...] = jnp.dot(vec_s[...], left_s[...], preferred_element_type=jnp.float32)
     for v in range(CHANNELS):
         for s in range(STATES):
@@ -90,13 +109,13 @@
         out_ref[r] = image[r * half : (r + 1) * half].astype(jnp.bfloat16)
 
 
-def terms(core, table, left_own, left_other, own, other):
-    blocks, left_rows, width = left_own.shape
-    half = left_rows // CHANNELS
+def terms(core, table, left, own, other):
+    blocks, rows, width = own.shape
+    half = rows // (STATES + CHANNELS)
     return pl.pallas_call(
         terms_kernel,
         out_shape=jax.ShapeDtypeStruct((blocks, half, STATES * width), jnp.bfloat16),
-        in_specs=[SMEM, SMEM, VMEM, VMEM, VMEM, VMEM],
+        in_specs=[SMEM, SMEM, VMEM, VMEM, VMEM],
         out_specs=VMEM,
         scratch_shapes=[
             pltpu.VMEM((STATES * width, blocks * width), jnp.bfloat16),
@@ -105,8 +124,8 @@
             pltpu.VMEM((STATES * width, CHANNELS * width), jnp.float32),
             pltpu.VMEM((CHANNELS * width, STATES * width), jnp.bfloat16),
         ],
-        compiler_params=PARAMS,
-    )(core, table, left_own, left_other, own, other)
+        compiler_params=LARGE,
+    )(core, table, left, own, other)
 
 
 def lanes_of(total):
@@ -137,7 +156,7 @@
         ),
         in_specs=[VMEM, VMEM],
         out_specs=(VMEM, VMEM),
-        compiler_params=PARAMS,
+        compiler_params=SMALL,
     )(pieces, vector)
 
 
@@ -155,7 +174,7 @@
         out_shape=jax.ShapeDtypeStruct((size, *pieces.shape[1:]), jnp.float32),
         in_specs=[VMEM],
         out_specs=VMEM,
-        compiler_params=PARAMS,
+        compiler_params=SMALL,
     )(pieces)
 
 
@@ -187,7 +206,7 @@
         ),
         in_specs=[VMEM, VMEM, VMEM],
         out_specs=(VMEM, SMEM),
-        compiler_params=PARAMS,
+        compiler_params=SMALL,
     )(pieces, image, vector)
 
 
@@ -211,10 +230,10 @@
     left = (left.astype(jnp.float32) * SCALE).astype(jnp.float16)
 
     own = all_to_all(pack(vector, right_env, n_row), ROW)
-    left = lax.all_gather(left, Z, axis=0)
+    left = lax.all_gather(left, COL, axis=0)
     own, left = lax.optimization_barrier((own, left))
     left = (left.astype(jnp.float32) * (1.0 / SCALE)).astype(jnp.bfloat16)
-    sent = terms(core, table, left, other_core(left), own, other_core(own))
+    sent = terms(core, table, left, own, other_core(own))
 
     pieces = all_to_all(sent, Z)
     image, sums = sums_of(pieces, vector, lax.axis_size((X, Y, C)))

time: 169 us -> 164 us (0.970)
  starting transfers between devices: 18.3 us -> 9.77 us
  blocking collectives: 131 us -> 138 us
  local copies, waits for them, and re-layouts: 3.65 us -> 0.51 us
    ppermute x2 -> x1, starting transfers between devices: 10.6 us -> 2.05 us  [other_core(): return lax.ppermute(x, C, [(0, 1), (1, 0)])]
    all_gather x1, blocking collectives: 40 us -> 46.8 us  [body(): left = lax.all_gather(left, COL, axis=0)]
    unnamed x14 -> x8, local copies, waits for them, and re-layouts: 3.17 us -> 0.03 us
    pallas_call x1, Pallas kernels: 0.4 us -> 2.74 us  [pack(): pl.pallas_call(pack_kernel, out_shape=pltpu.HBM((size, rows, width), jnp....]
  transfers between devices with their start and end apart: 3 -> 2, of which waited for: 1 -> 1; matrix products, arithmetic and copies ran while one was open for 2% -> 2% of each run, Pallas kernels for 0% -> 0%
where the time goes in v3:
time: 164 us; the launch traced here: 163 us
  blocking collectives  138 us (84%)
  Pallas kernels  10.7 us (7%)
  starting transfers between devices  9.77 us (6%)
  other arithmetic  2.52 us (2%)
    all_to_all x3, blocking collectives, all_to_all(): return lax.all_to_all(x, axes, 0, 0, tiled=True)  90.9 us
    all_gather x1, blocking collectives, body(): left = lax.all_gather(left, COL, axis=0)  46.8 us
    all_to_all x1, starting transfers between devices, all_to_all(): return lax.all_to_all(x, axes, 0, 0, tiled=True)  7.72 us
    pallas_call x1, Pallas kernels, terms(): pl.pallas_call(terms_kernel, out_shape=jax.ShapeDtypeStruct((blocks, half...  6.91 us
  transfers between devices with their start and end apart: 2, of which 1 were waited for; matrix products, arithmetic and copies ran while one was open for 2% of the time, Pallas kernels for 0%

profile of v3, /device:TPU:1, one launch (start us, length us, event | category | flops | bytes accessed | tf_op | source)
XLA Modules:
  0.0 163.4 jit_solution(1968535419849956815)
XLA Ops:
  0.6 0.0 copy-start
  0.6 2.7 %shard_map.68 = bf16[16,576,128]{2,1,0:T(8,128)(2,1)} custom-call(bf16[4,64,128]{2,1,0:T(8,128)(2,1)} %bitcast.11, bf16[5,64,128]{2,1,0:T(8,128)(2,1)} %right_hbm.1), custom_call_target="tpu_custom_call" | custom-call | tf_op jit(solution)/shard_map/pallas_call | solution.py:58
  3.4 0.0 copy-start.2
  3.4 0.0 copy-start.3
  3.4 7.7 %all-to-all-start = ((bf16[16,576,128]{2,1,0:T(8,128)(2,1)}), bf16[16,576,128]{2,1,0:T(8,128)(2,1)S(1)}, u32[]{:S(2)}, u32[]{:S(2)}) async-start(bf16[16,576,128]{2,1,0:T(8,128)(2,1)} %shard_map.68), calls=%async_computation | async-start | bytes 4718592 | tf_op jit(solution)/shard_map/all_to_all | solution.py:214
  11.1 0.0 copy-done.2
  11.2 46.8 %all-gather.1 = f16[32,320,128]{2,1,0:T(8,128)(2,1)} all-gather(f16[1,320,128]{2,1,0:T(8,128)(2,1)S(1)} %bitcast.14), channel_id=1, replica_groups=mesh['row_0'=4,'row_1'=4,'col_0'=16,'col_1'=2] {'col_0','col_1'}, dimensions={0}, use_global_device_ids=true | all-gather | bytes 2703360 | tf_op jit(solution)/shard_map/all_gather | solution.py:233
  58.0 0.0 all-to-all-done.own_ref
  58.0 2.1 %collective-permute-start = (bf16[16,576,128]{2,1,0:T(8,128)(2,1)S(1)}, bf16[16,576,128]{2,1,0:T(8,128)(2,1)}, u32[]{:S(2)}, u32[]{:S(2)}) collective-permute-start(bf16[16,576,128]{2,1,0:T(8,128)(2,1)S(1)} %all-to-all-done.own_ref), channel_id=1, source_target_pairs={{0,1},{1,0},{2,3},{3,2},{4,5},{5,4},{6,7},{7,6},{8,9},{9,8},{10,11... | collective-permute-start | bytes 7077896 | tf_op jit(solution)/shard_map/ppermute | solution.py:218
  60.1 0.0 copy-done
  60.1 0.0 copy-done.3
  60.1 0.4 convolution_bitcast_fusion
  60.5 0.4 copy.15
  60.9 0.1 reshape.32.table_ref
  61.0 2.5 %multiply_convert_fusion.left_ref = bf16[32,320,128]{2,1,0:T(8,128)(2,1)S(1)} fusion(f16[32,320,128]{2,1,0:T(8,128)(2,1)} %all-gather.1), kind=kLoop, calls=%fused_computation | loop fusion | flops 3932160 | bytes 5242880 | tf_op jit(solution)/shard_map/convert_element_type | solution.py:235
  63.5 1.1 collective-permute-done.other_ref
  64.6 0.0 copy-start.1
  64.6 6.9 %shard_map.69 = bf16[16,64,512]{2,1,0:T(8,128)(2,1)S(1)} custom-call(s32[1]{0:T(128)} %bitcast.core_ref, f32[20,20]{1,0:T(8,128)S(1)} %reshape.32.table_ref, bf16[32,320,128]{2,1,0:T(8,128)(2,1)S(1)} %multiply_convert_fusion.left_ref, bf16[16,576,128]{2,1,0:T(8,128)(2,1)S(1)} %all-to-all-done.own_ref, bf16[16,576,128]{2,1,0:T(8,128)(2,1)} %collective-permute-done.other_ref), custom_call_target="tpu_custom_call" | custom-call | tf_op jit(solution)/shard_map/pallas_call | solution.py:115
  71.5 51.7 %all_to_all.20.pieces_ref = bf16[16,64,512]{2,1,0:T(8,128)(2,1)S(1)} all-to-all(bf16[16,64,512]{2,1,0:T(8,128)(2,1)S(1)} %shard_map.69), channel_id=1, replica_groups=mesh['row_0'=4,'row_1'=4,'col_0'=16,'col_1'=2] {'col_0'}, dimensions={0} | all-to-all | bytes 2097152 | tf_op jit(solution)/shard_map/all_to_all | solution.py:214
  123.2 0.0 copy-done.1
  123.2 0.3 shard_map.70
  123.5 21.8 %all_to_all.21.pieces_ref = f32[32,8,128]{2,1,0:T(8,128)S(1)} all-to-all(f32[32,8,128]{2,1,0:T(8,128)S(1)} %get-tuple-element.10), channel_id=1, replica_groups=mesh['row_0'=4,'row_1'=4,'col_0'=16,'col_1'=2] {'row_0','row_1','col_1'}, dimensions={0} | all-to-all | bytes 262144 | tf_op jit(solution)/shard_map/all_to_all | solution.py:214
  145.3 17.5 %all_to_all.22.refs_0_ = f32[16,8,128]{2,1,0:T(8,128)S(1)} all-to-all(f32[16,8,128]{2,1,0:T(8,128)S(1)} %shard_map.71), channel_id=1, replica_groups=mesh['row_0'=4,'row_1'=4,'col_0'=16,'col_1'=2] {'col_0'}, dimensions={0} | all-to-all | bytes 131072 | tf_op jit(solution)/shard_map/all_to_all | solution.py:214
  162.7 0.7 shard_map.72
  (2 shorter events, 0.1 us)
Async XLA Ops:
  0.6 59.5 %copy-start = (f32[5,5,2,2]{1,3,2,0:T(2,128)S(1)}, f32[5,5,2,2]{1,3,2,0:T(2,128)}, u32[]{:S(2)}) copy-start(f32[5,5,2,2]{1,3,2,0:T(2,128)} %param.8) | copy-start | bytes 1204
  3.4 7.8 %copy-start.2 = (bf16[5,128,64]{1,2,0:T(8,128)(2,1)S(1)}, bf16[5,128,64]{1,2,0:T(8,128)(2,1)}, u32[]{:S(2)}) copy-start(bf16[5,128,64]{1,2,0:T(8,128)(2,1)} %param.6) | copy-start | bytes 245764
  3.4 56.7 %copy-start.3 = (f32[5,5,2,2]{1,3,2,0:T(2,128)S(1)}, f32[5,5,2,2]{1,3,2,0:T(2,128)}, u32[]{:S(2)}) copy-start(f32[5,5,2,2]{1,3,2,0:T(2,128)} %param.9) | copy-start | bytes 1204
  3.4 54.6 %all-to-all-start = ((bf16[16,576,128]{2,1,0:T(8,128)(2,1)}), bf16[16,576,128]{2,1,0:T(8,128)(2,1)S(1)}, u32[]{:S(2)}, u32[]{:S(2)}) async-start(bf16[16,576,128]{2,1,0:T(8,128)(2,1)} %shard_map.68), calls=%async_computation | async-start | bytes 4718592 | tf_op jit(solution)/shard_map/all_to_all | solution.py:214
  58.0 6.6 %collective-permute-start = (bf16[16,576,128]{2,1,0:T(8,128)(2,1)S(1)}, bf16[16,576,128]{2,1,0:T(8,128)(2,1)}, u32[]{:S(2)}, u32[]{:S(2)}) collective-permute-start(bf16[16,576,128]{2,1,0:T(8,128)(2,1)S(1)} %all-to-all-done.own_ref), channel_id=1, source_target_pairs={{0,1},{1,0},{2,3},{3,2},{4,5},{5,4},{6,7},{7,6},{8,9},{9,8},{10,11... | collective-permute-start | bytes 7077896 | tf_op jit(solution)/shard_map/ppermute | solution.py:218
  64.6 58.6 %copy-start.1 = (bf16[4,128,64]{1,2,0:T(8,128)(2,1)S(1)}, bf16[4,128,64]{1,2,0:T(8,128)(2,1)}, u32[]{:S(2)}) copy-start(bf16[4,128,64]{1,2,0:T(8,128)(2,1)} %param.5) | copy-start | bytes 196612

commit v4 on v3

--- a/solution.py
+++ b/solution.py
@@ -6,9 +6,10 @@
 from jax.sharding import Mesh
 from jax.sharding import PartitionSpec as P
 
-X, Y, Z, C = "row_0", "row_1", "col_0", "col_1"
+X, Y, FAR, NEAR, C = "row_0", "row_1", "far", "near", "core"
 ROW = (X, Y)
-COL = (Z, C)
+Z = (FAR, NEAR)
+COL = (FAR, NEAR, C)
 STATES = 4
 CHANNELS = 5
 PAIRS = STATES * CHANNELS
@@ -71,7 +72,7 @@
     )(pltpu.with_memory_space_constraint(vector, pltpu.HBM), pltpu.with_memory_space_constraint(right, pltpu.HBM))
 
 
-def terms_kernel(core_ref, table_ref, left_ref, own_ref, other_ref, out_ref, vec_s, left_s, right_s, cross_s, mixed_s):
+def terms_kernel(order, core_ref, table_ref, left_ref, own_ref, other_ref, out_ref, vec_s, left_s, right_s, cross_s, mixed_s):
     blocks, half, _ = out_ref.shape
     width = 2 * half
     core = core_ref[0]
@@ -106,14 +107,17 @@
             right_s[r * half : (r + 1) * half, v * width : (v + 1) * width] = jnp.where(mine, own, other).astype(jnp.bfloat16)
     image = jnp.dot(right_s[...], mixed_s[...], preferred_element_type=jnp.float32)
     for r in range(blocks):
-        out_ref[r] = image[r * half : (r + 1) * half].astype(jnp.bfloat16)
-
-
-def terms(core, table, left, own, other):
+        out_ref[order[r]] = image[r * half : (r + 1) * half].astype(jnp.bfloat16)
+
+
+def terms(order, core, table, left, own, other):
+    def step(*refs):
+        terms_kernel(order, *refs)
+
     blocks, rows, width = own.shape
     half = rows // (STATES + CHANNELS)
     return pl.pallas_call(
-        terms_kernel,
+        step,
         out_shape=jax.ShapeDtypeStruct((blocks, half, STATES * width), jnp.bfloat16),
         in_specs=[SMEM, SMEM, VMEM, VMEM, VMEM],
         out_specs=VMEM,
@@ -126,6 +130,35 @@
         ],
         compiler_params=LARGE,
     )(core, table, left, own, other)
+
+
+def near_kernel(pieces_ref, out_ref):
+    for j in range(out_ref.shape[0]):
+        total = pieces_ref[0, j].astype(jnp.float32)
+        for k in range(1, pieces_ref.shape[0]):
+            total = total + pieces_ref[k, j].astype(jnp.float32)
+        out_ref[j] = total.astype(jnp.bfloat16)
+
+
+def near_sum(pieces):
+    return pl.pallas_call(
+        near_kernel,
+        out_shape=jax.ShapeDtypeStruct(pieces.shape[1:], jnp.bfloat16),
+        in_specs=[VMEM],
+        out_specs=VMEM,
+        compiler_params=SMALL,
+    )(pieces)
+
+
+def neighbours(n_far, n_near):
+    n_z = n_far * n_near
+    groups = []
+    for core in range(2):
+        for j in range(n_far):
+            first = j * n_near + core * (n_near // 2)
+            chips = sorted(((first + i) % n_z for i in range(n_near)), key=lambda z: z % n_near)
+            groups.append([2 * z + core for z in chips])
+    return groups
 
 
 def lanes_of(total):
@@ -220,7 +253,8 @@
 
 def body(start_vector, left_env, right_env, left_tensor, right_tensor):
     n_row = lax.axis_size(ROW)
-    n_z = lax.axis_size(Z)
+    n_far, n_near = lax.axis_size(FAR), lax.axis_size(NEAR)
+    n_z = n_far * n_near
     _, rows, half = start_vector.shape
     entries = float(STATES * rows * half * n_row * n_z * lax.axis_size(C))
     core = lax.axis_index(C).astype(jnp.int32).reshape(1)
@@ -233,9 +267,11 @@
     left = lax.all_gather(left, COL, axis=0)
     own, left = lax.optimization_barrier((own, left))
     left = (left.astype(jnp.float32) * (1.0 / SCALE)).astype(jnp.bfloat16)
-    sent = terms(core, table, left, own, other_core(own))
-
-    pieces = all_to_all(sent, Z)
+    order = [n_far * (z % n_near) + z // n_near for z in range(n_z)]
+    sent = terms(order, core, table, left, own, other_core(own))
+
+    pieces = lax.all_to_all(sent, COL, 0, 0, axis_index_groups=neighbours(n_far, n_near), tiled=True)
+    pieces = all_to_all(near_sum(pieces.reshape(n_near, n_far, *pieces.shape[1:])), FAR)
     image, sums = sums_of(pieces, vector, lax.axis_size((X, Y, C)))
     sums = again(all_to_all(sums, (X, Y, C)), n_z)
     next_vector, coefficients = last(entries, all_to_all(sums, Z), image, vector)
@@ -243,7 +279,7 @@
 
 
 def solution(mesh):
-    finer = Mesh(mesh.devices.reshape(4, 4, 16, 2), (X, Y, Z, C))
+    finer = Mesh(mesh.devices.reshape(4, 4, 4, 4, 2), (X, Y, FAR, NEAR, C))
     in_specs = (P(None, ROW, COL), P(None, ROW, COL), P(None, COL, ROW), P(), P())
     out_specs = (P(None, ROW, COL), P())
     return jax.shard_map(body, mesh=finer, in_specs=in_specs, out_specs=out_specs, check_vma=False)

time: 164 us -> 154 us (0.939)
  blocking collectives: 138 us -> 128 us
    all_to_all x3, blocking collectives: 90.9 us -> 57.1 us  [all_to_all(): return lax.all_to_all(x, axes, 0, 0, tiled=True)]
    all_to_all x0 -> x1, blocking collectives: none -> 24.1 us  [body(): lax.all_to_all(sent, COL, 0, 0, axis_index_groups=neighbours(n_far, n_nea...]
    pallas_call x1 -> x2, Pallas kernels: 6.91 us -> 7.01 us  [the longest x1 6.88 us: terms(): pl.pallas_call(step, out_shape=jax.ShapeDtypeStruct((blocks, half, STATES...]
where the time goes in v4:
time: 154 us
  blocking collectives  128 us (83%)
  Pallas kernels  10.7 us (7%)
  starting transfers between devices  9.77 us (6%)
  other arithmetic  2.52 us (2%)
    all_to_all x3, blocking collectives, all_to_all(): return lax.all_to_all(x, axes, 0, 0, tiled=True)  57.1 us
    all_gather x1, blocking collectives, body(): left = lax.all_gather(left, COL, axis=0)  46.8 us
    all_to_all x1, blocking collectives, body(): lax.all_to_all(sent, COL, 0, 0, axis_index_groups=neighbours(n_far, n_nea...  24.1 us
    all_to_all x1, starting transfers between devices, all_to_all(): return lax.all_to_all(x, axes, 0, 0, tiled=True)  7.72 us
    pallas_call x1, Pallas kernels, terms(): pl.pallas_call(step, out_shape=jax.ShapeDtypeStruct((blocks, half, STATES...  6.88 us
  transfers between devices with their start and end apart: 2, of which 1 were waited for; matrix products, arithmetic and copies ran while one was open for 2% of the time, Pallas kernels for 0%

profile of v4, /device:TPU:1, one launch (start us, length us, event | category | flops | bytes accessed | tf_op | source)
XLA Modules:
  0.0 153.8 jit_solution(383546818868954697)
XLA Ops:
  0.6 0.0 copy-start
  0.6 2.7 %shard_map.68 = bf16[16,576,128]{2,1,0:T(8,128)(2,1)} custom-call(bf16[4,64,128]{2,1,0:T(8,128)(2,1)} %bitcast.13, bf16[5,64,128]{2,1,0:T(8,128)(2,1)} %right_hbm.1), custom_call_target="tpu_custom_call" | custom-call | tf_op jit(solution)/shard_map/pallas_call | solution.py:59
  3.4 0.0 copy-start.2
  3.4 0.0 copy-start.3
  3.4 7.7 %all-to-all-start = ((bf16[16,576,128]{2,1,0:T(8,128)(2,1)}), bf16[16,576,128]{2,1,0:T(8,128)(2,1)S(1)}, u32[]{:S(2)}, u32[]{:S(2)}) async-start(bf16[16,576,128]{2,1,0:T(8,128)(2,1)} %shard_map.68), calls=%async_computation | async-start | bytes 4718592 | tf_op jit(solution)/shard_map/all_to_all | solution.py:247
  11.1 0.0 copy-done.2
  11.2 46.8 %all-gather.1 = f16[32,320,128]{2,1,0:T(8,128)(2,1)} all-gather(f16[1,320,128]{2,1,0:T(8,128)(2,1)S(1)} %bitcast.16), channel_id=1, replica_groups=mesh['row_0'=4,'row_1'=4,'far'=4,'near'=4,'core'=2] {'far','near','core'}, dimensions={0}, use_global_device_ids=true | all-gather | bytes 2703360 | tf_op jit(solution)/shard_map/all_gather | solution.py:267
  58.0 0.0 all-to-all-done.refs_3_
  58.0 2.1 %collective-permute-start = (bf16[16,576,128]{2,1,0:T(8,128)(2,1)S(1)}, bf16[16,576,128]{2,1,0:T(8,128)(2,1)}, u32[]{:S(2)}, u32[]{:S(2)}) collective-permute-start(bf16[16,576,128]{2,1,0:T(8,128)(2,1)S(1)} %all-to-all-done.refs_3_), channel_id=1, source_target_pairs={{0,1},{1,0},{2,3},{3,2},{4,5},{5,4},{6,7},{7,6},{8,9},{9,8},{10,11... | collective-permute-start | bytes 7077896 | tf_op jit(solution)/shard_map/ppermute | solution.py:251
  60.1 0.0 copy-done
  60.1 0.0 copy-done.3
  60.1 0.4 convolution_bitcast_fusion
  60.5 0.4 copy.15
  60.9 0.1 reshape.35.refs_1_
  61.0 2.5 %multiply_convert_fusion.refs_2_ = bf16[32,320,128]{2,1,0:T(8,128)(2,1)S(1)} fusion(f16[32,320,128]{2,1,0:T(8,128)(2,1)} %all-gather.1), kind=kLoop, calls=%fused_computation | loop fusion | flops 3932160 | bytes 5242880 | tf_op jit(solution)/shard_map/convert_element_type | solution.py:269
  63.5 1.1 collective-permute-done.refs_4_
  64.6 6.9 %shard_map.69 = bf16[16,64,512]{2,1,0:T(8,128)(2,1)S(1)} custom-call(s32[1]{0:T(128)} %bitcast.refs_0_, f32[20,20]{1,0:T(8,128)S(1)} %reshape.35.refs_1_, bf16[32,320,128]{2,1,0:T(8,128)(2,1)S(1)} %multiply_convert_fusion.refs_2_, bf16[16,576,128]{2,1,0:T(8,128)(2,1)S(1)} %all-to-all-done.refs_3_, bf16[16,576,128]{2,1,0:T(8,128)(2,1)} %collective-permute-done.refs_4_), custom_call_target="tpu_custom_call" | custom-call | tf_op jit(solution)/shard_map/pallas_call | solution.py:119
  71.5 0.0 copy-start.1
  71.5 24.1 %all_to_all.25 = bf16[16,64,512]{2,1,0:T(8,128)(2,1)S(1)} all-to-all(bf16[16,64,512]{2,1,0:T(8,128)(2,1)S(1)} %shard_map.69), channel_id=1, replica_groups={{0,2,4,6},{8,10,12,14},{16,18,20,22},{24,26,28,30},{9,11,5,7},{17,19,13..., dimensions={0} | all-to-all | bytes 2097152 | tf_op jit(solution)/shard_map/all_to_all | solution.py:273
  95.6 0.1 shard_map.70
  95.7 24.2 %all_to_all.26.pieces_ref = bf16[4,64,512]{2,1,0:T(8,128)(2,1)S(1)} all-to-all(bf16[4,64,512]{2,1,0:T(8,128)(2,1)S(1)} %shard_map.70), channel_id=1, replica_groups=mesh['row_0'=4,'row_1'=4,'far'=4,'near'=4,'core'=2] {'far'}, dimensions={0} | all-to-all | bytes 524288 | tf_op jit(solution)/shard_map/all_to_all | solution.py:247
  120.0 0.0 copy-done.1
  120.0 0.2 shard_map.71
  120.2 15.9 %all_to_all.27.pieces_ref = f32[32,8,128]{2,1,0:T(8,128)S(1)} all-to-all(f32[32,8,128]{2,1,0:T(8,128)S(1)} %get-tuple-element.10), channel_id=1, replica_groups=mesh['row_0'=4,'row_1'=4,'far'=4,'near'=4,'core'=2] {'row_0','row_1','co..., dimensions={0} | all-to-all | bytes 262144 | tf_op jit(solution)/shard_map/all_to_all | solution.py:247
  136.1 17.0 %all_to_all.28.refs_0_ = f32[16,8,128]{2,1,0:T(8,128)S(1)} all-to-all(f32[16,8,128]{2,1,0:T(8,128)S(1)} %shard_map.72), channel_id=1, replica_groups=mesh['row_0'=4,'row_1'=4,'far'=4,'near'=4,'core'=2] {'far','near'}, dimensions={0} | all-to-all | bytes 131072 | tf_op jit(solution)/shard_map/all_to_all | solution.py:247
  153.1 0.7 shard_map.73
  (2 shorter events, 0.1 us)
Async XLA Ops:
  0.6 59.5 %copy-start = (f32[5,5,2,2]{1,3,2,0:T(2,128)S(1)}, f32[5,5,2,2]{1,3,2,0:T(2,128)}, u32[]{:S(2)}) copy-start(f32[5,5,2,2]{1,3,2,0:T(2,128)} %param.8) | copy-start | bytes 1204
  3.4 7.8 %copy-start.2 = (bf16[5,128,64]{1,2,0:T(8,128)(2,1)S(1)}, bf16[5,128,64]{1,2,0:T(8,128)(2,1)}, u32[]{:S(2)}) copy-start(bf16[5,128,64]{1,2,0:T(8,128)(2,1)} %param.6) | copy-start | bytes 245764
  3.4 56.7 %copy-start.3 = (f32[5,5,2,2]{1,3,2,0:T(2,128)S(1)}, f32[5,5,2,2]{1,3,2,0:T(2,128)}, u32[]{:S(2)}) copy-start(f32[5,5,2,2]{1,3,2,0:T(2,128)} %param.9) | copy-start | bytes 1204
  3.4 54.6 %all-to-all-start = ((bf16[16,576,128]{2,1,0:T(8,128)(2,1)}), bf16[16,576,128]{2,1,0:T(8,128)(2,1)S(1)}, u32[]{:S(2)}, u32[]{:S(2)}) async-start(bf16[16,576,128]{2,1,0:T(8,128)(2,1)} %shard_map.68), calls=%async_computation | async-start | bytes 4718592 | tf_op jit(solution)/shard_map/all_to_all | solution.py:247
  58.0 6.6 %collective-permute-start = (bf16[16,576,128]{2,1,0:T(8,128)(2,1)S(1)}, bf16[16,576,128]{2,1,0:T(8,128)(2,1)}, u32[]{:S(2)}, u32[]{:S(2)}) collective-permute-start(bf16[16,576,128]{2,1,0:T(8,128)(2,1)S(1)} %all-to-all-done.refs_3_), channel_id=1, source_target_pairs={{0,1},{1,0},{2,3},{3,2},{4,5},{5,4},{6,7},{7,6},{8,9},{9,8},{10,11... | collective-permute-start | bytes 7077896 | tf_op jit(solution)/shard_map/ppermute | solution.py:251
  71.5 48.5 %copy-start.1 = (bf16[4,128,64]{1,2,0:T(8,128)(2,1)S(1)}, bf16[4,128,64]{1,2,0:T(8,128)(2,1)}, u32[]{:S(2)}) copy-start(bf16[4,128,64]{1,2,0:T(8,128)(2,1)} %param.5) | copy-start | bytes 196612

commit v5 on v4

--- a/solution.py
+++ b/solution.py
@@ -19,8 +19,13 @@
 
 VMEM = pl.BlockSpec(memory_space=pltpu.VMEM)
 SMEM = pl.BlockSpec(memory_space=pltpu.SMEM)
+HBM = pl.BlockSpec(memory_space=pltpu.HBM)
 SMALL = pltpu.CompilerParams(vmem_limit_bytes=4 * 1024 * 1024)
-LARGE = pltpu.CompilerParams(vmem_limit_bytes=24 * 1024 * 1024)
+LARGE = pltpu.CompilerParams(vmem_limit_bytes=32 * 1024 * 1024)
+
+
+def in_hbm(x):
+    return pltpu.with_memory_space_constraint(x, pltpu.HBM)
 
 
 def coupling(left_tensor, right_tensor):
@@ -55,12 +60,11 @@
 def pack(vector, right, size):
     states, half, width = vector.shape
     rows = (states + right.shape[0]) * half
-    hbm = pl.BlockSpec(memory_space=pltpu.HBM)
     return pl.pallas_call(
         pack_kernel,
         out_shape=pltpu.HBM((size, rows, width), jnp.bfloat16),
-        in_specs=[hbm, hbm],
-        out_specs=hbm,
+        in_specs=[HBM, HBM],
+        out_specs=HBM,
         scratch_shapes=[
             pltpu.VMEM(vector.shape, jnp.bfloat16),
             pltpu.VMEM(right.shape, jnp.bfloat16),
@@ -69,22 +73,32 @@
             pltpu.SemaphoreType.DMA((size,)),
         ],
         compiler_params=SMALL,
-    )(pltpu.with_memory_space_constraint(vector, pltpu.HBM), pltpu.with_memory_space_constraint(right, pltpu.HBM))
-
-
-def terms_kernel(order, core_ref, table_ref, left_ref, own_ref, other_ref, out_ref, vec_s, left_s, right_s, cross_s, mixed_s):
+    )(in_hbm(vector), in_hbm(right))
+
+
+def terms_kernel(order, core_ref, table_ref, left_ref, own_hbm, other_hbm, out_ref, vec_s, left_s, right_s, cross_s, mixed_s, own_ref, other_ref, sems):
     blocks, half, _ = out_ref.shape
     width = 2 * half
     core = core_ref[0]
     own_at = pl.multiple_of(core * half, half)
     other_at = pl.multiple_of((1 - core) * half, half)
+    parts = (pl.ds(0, STATES * half), pl.ds(STATES * half, CHANNELS * half))
+    copies = [
+        [pltpu.make_async_copy(src.at[:, part], dst.at[:, part], sems.at[i, j]) for j, (src, dst) in enumerate(((own_hbm, own_ref), (other_hbm, other_ref)))]
+        for i, part in enumerate(parts)
+    ]
+    for pair in copies:
+        for copy in pair:
+            copy.start()
+    for r in range(left_ref.shape[0]):
+        for w in range(CHANNELS):
+            left_s[r * half : (r + 1) * half, w * width : (w + 1) * width] = left_ref[r, w * half : (w + 1) * half, :]
+    for copy in copies[0]:
+        copy.wait()
     for r in range(blocks):
         for source, at in ((own_ref, own_at), (other_ref, other_at)):
             for t in range(STATES):
                 vec_s[pl.ds(t * width + at, half), r * width : (r + 1) * width] = source[r, t * half : (t + 1) * half, :]
-    for r in range(left_ref.shape[0]):
-        for w in range(CHANNELS):
-            left_s[r * half : (r + 1) * half, w * width : (w + 1) * width] = left_ref[r, w * half : (w + 1) * half, :]
     cross_s[...] = jnp.dot(vec_s[...], left_s[...], preferred_element_type=jnp.float32)
     for v in range(CHANNELS):
         for s in range(STATES):
@@ -97,6 +111,8 @@
                     )
                     total = part if total is None else total + part
             mixed_s[v * width : (v + 1) * width, s * width : (s + 1) * width] = total.astype(jnp.bfloat16)
+    for copy in copies[1]:
+        copy.wait()
     mine = lax.broadcasted_iota(jnp.int32, (half, width), 1) // half == core
     for r in range(blocks):
         for v in range(CHANNELS):
@@ -119,7 +135,7 @@
     return pl.pallas_call(
         step,
         out_shape=jax.ShapeDtypeStruct((blocks, half, STATES * width), jnp.bfloat16),
-        in_specs=[SMEM, SMEM, VMEM, VMEM, VMEM],
+        in_specs=[SMEM, SMEM, VMEM, HBM, HBM],
         out_specs=VMEM,
         scratch_shapes=[
             pltpu.VMEM((STATES * width, blocks * width), jnp.bfloat16),
@@ -127,9 +143,12 @@
             pltpu.VMEM((blocks * half, CHANNELS * width), jnp.bfloat16),
             pltpu.VMEM((STATES * width, CHANNELS * width), jnp.float32),
             pltpu.VMEM((CHANNELS * width, STATES * width), jnp.bfloat16),
+            pltpu.VMEM(own.shape, jnp.bfloat16),
+            pltpu.VMEM(other.shape, jnp.bfloat16),
+            pltpu.SemaphoreType.DMA((2, 2)),
         ],
         compiler_params=LARGE,
-    )(core, table, left, own, other)
+    )(core, table, left, in_hbm(own), in_hbm(other))
 
 
 def near_kernel(pieces_ref, out_ref):
@@ -174,10 +193,12 @@
     image_ref[...] = image
     base = jnp.concatenate([vector_ref[t].astype(jnp.float32) for t in range(STATES)], 1)
     found = [lanes_of(base * base), lanes_of(base * image), lanes_of(image * image)]
-    found = [jnp.broadcast_to(jnp.sum(f, keepdims=True), (1, 128)) for f in found]
-    found = jnp.concatenate([*found, jnp.zeros((5, 128), jnp.float32)], 0)
+    lane = lax.broadcasted_iota(jnp.int32, (1, 128), 1)
+    row = jnp.zeros((1, 128), jnp.float32)
+    for k in range(3):
+        row = jnp.where(lane == k, jnp.sum(found[k], keepdims=True), row)
     for r in range(sums_ref.shape[0]):
-        sums_ref[r] = found
+        sums_ref[r] = row
 
 
 def sums_of(pieces, vector, size):
@@ -185,7 +206,7 @@
         sums_kernel,
         out_shape=(
             jax.ShapeDtypeStruct(pieces.shape[1:], jnp.float32),
-            jax.ShapeDtypeStruct((size, 8, 128), jnp.float32),
+            jax.ShapeDtypeStruct((size, 1, 128), jnp.float32),
         ),
         in_specs=[VMEM, VMEM],
         out_specs=(VMEM, VMEM),
@@ -216,7 +237,10 @@
     for k in range(1, pieces_ref.shape[0]):
         total = total + pieces_ref[k]
     total = total / entries
-    base_square, correlation, image_square = total[0:1], total[1:2], total[2:3]
+    lane = lax.broadcasted_iota(jnp.int32, total.shape, 1)
+    base_square, correlation, image_square = (
+        jnp.sum(jnp.where(lane == k, total, 0.0), 1, keepdims=True) for k in range(3)
+    )
     alpha = correlation / (base_square + epsilon)
     rho = jnp.sqrt(image_square - 2.0 * alpha * correlation + alpha * alpha * base_square + epsilon)
     width = next_ref.shape[2]

time: 154 us -> 154 us (level)
  blocking collectives: 128 us -> 125 us
  Pallas kernels: 10.7 us -> 12.7 us
  waiting for transfers between devices: 1.06 us -> 2.95 us
  other arithmetic: 2.52 us -> 0.84 us
    all_gather x1, blocking collectives: 46.8 us -> 44.7 us  [body(): left = lax.all_gather(left, COL, axis=0)]
    pallas_call x1, Pallas kernels: 6.88 us -> 8.89 us  [terms(): pl.pallas_call(step, out_shape=jax.ShapeDtypeStruct((blocks, half, STATES...]
    ppermute x1, waiting for transfers between devices: 1.05 us -> 2.94 us  [other_core(): return lax.ppermute(x, C, [(0, 1), (1, 0)])]
    convert_element_type x1, other arithmetic: 2.5 us -> 0.82 us  [body(): left = (left.astype(jnp.float32) * (1.0 / SCALE)).astype(jnp.bfloat16)]
  transfers between devices with their start and end apart: 2 -> 2, of which waited for: 1 -> 1; matrix products, arithmetic and copies ran while one was open for 2% -> 1% of each run, Pallas kernels for 0% -> 0%
where the time goes in v5:
time: 154 us; the launch traced here: 153 us
  blocking collectives  125 us (81%)
  Pallas kernels  12.7 us (8%)
  starting transfers between devices  9.82 us (6%)
  waiting for transfers between devices  2.95 us (2%)
    all_to_all x3, blocking collectives, all_to_all(): return lax.all_to_all(x, axes, 0, 0, tiled=True)  56.2 us
    all_gather x1, blocking collectives, body(): left = lax.all_gather(left, COL, axis=0)  44.7 us
    all_to_all x1, blocking collectives, body(): lax.all_to_all(sent, COL, 0, 0, axis_index_groups=neighbours(n_far, n_nea...  24.1 us
    pallas_call x1, Pallas kernels, terms(): pl.pallas_call(step, out_shape=jax.ShapeDtypeStruct((blocks, half, STATES...  8.89 us
    all_to_all x1, starting transfers between devices, all_to_all(): return lax.all_to_all(x, axes, 0, 0, tiled=True)  7.76 us
  transfers between devices with their start and end apart: 2, of which 1 were waited for; matrix products, arithmetic and copies ran while one was open for 1% of the time, Pallas kernels for 0%

profile of v5, /device:TPU:1, one launch (start us, length us, event | category | flops | bytes accessed | tf_op | source)
XLA Modules:
  0.0 153.1 jit_solution(12280529086345497318)
XLA Ops:
  0.6 0.0 copy-start
  0.6 2.7 %shard_map.68 = bf16[16,576,128]{2,1,0:T(8,128)(2,1)} custom-call(bf16[4,64,128]{2,1,0:T(8,128)(2,1)} %bitcast.13, bf16[5,64,128]{2,1,0:T(8,128)(2,1)} %right_hbm.1), custom_call_target="tpu_custom_call" | custom-call | tf_op jit(solution)/shard_map/pallas_call | solution.py:63
  3.4 0.0 copy-start.2
  3.4 0.0 copy-start.3
  3.4 7.8 %all-to-all-start = ((bf16[16,576,128]{2,1,0:T(8,128)(2,1)}), bf16[16,576,128]{2,1,0:T(8,128)(2,1)}, u32[]{:S(2)}, u32[]{:S(2)}) async-start(bf16[16,576,128]{2,1,0:T(8,128)(2,1)} %shard_map.68), calls=%async_computation | async-start | bytes 4718592 | tf_op jit(solution)/shard_map/all_to_all | solution.py:271
  11.2 0.0 copy-done.2
  11.2 44.7 %all-gather.1 = f16[32,320,128]{2,1,0:T(8,128)(2,1)S(1)} all-gather(f16[1,320,128]{2,1,0:T(8,128)(2,1)S(1)} %bitcast.16), channel_id=1, replica_groups=mesh['row_0'=4,'row_1'=4,'far'=4,'near'=4,'core'=2] {'far','near','core'}, dimensions={0}, use_global_device_ids=true | all-gather | bytes 2703360 | tf_op jit(solution)/shard_map/all_gather | solution.py:291
  55.9 0.0 all-to-all-done.refs_3_
  55.9 2.1 %collective-permute-start = (bf16[16,576,128]{2,1,0:T(8,128)(2,1)}, bf16[16,576,128]{2,1,0:T(8,128)(2,1)}, u32[]{:S(2)}, u32[]{:S(2)}) collective-permute-start(bf16[16,576,128]{2,1,0:T(8,128)(2,1)} %all-to-all-done.refs_3_), channel_id=1, source_target_pairs={{0,1},{1,0},{2,3},{3,2},{4,5},{5,4},{6,7},{7,6},{8,9},{9,8},{10,11... | collective-permute-start | bytes 7077896 | tf_op jit(solution)/shard_map/ppermute | solution.py:275
  58.0 0.0 copy-done
  58.0 0.0 copy-done.3
  58.0 0.4 convolution_bitcast_fusion
  58.4 0.4 copy.15
  58.8 0.1 reshape.35.refs_1_
  58.9 0.8 multiply_convert_fusion.refs_2_
  59.8 2.9 %collective-permute-done.refs_4_ = bf16[16,576,128]{2,1,0:T(8,128)(2,1)} collective-permute-done((bf16[16,576,128]{2,1,0:T(8,128)(2,1)}, bf16[16,576,128]{2,1,0:T(8,128)(2,1)}, u32[]{:S(2)}, u32[]{:S(2)}) %collective-permute-start) | collective-permute-done | bytes 2359328 | tf_op jit(solution)/shard_map/ppermute | solution.py:275
  62.7 8.9 %shard_map.69 = bf16[16,64,512]{2,1,0:T(8,128)(2,1)S(1)} custom-call(s32[1]{0:T(128)} %bitcast.refs_0_, f32[20,20]{1,0:T(8,128)S(1)} %reshape.35.refs_1_, bf16[32,320,128]{2,1,0:T(8,128)(2,1)S(1)} %multiply_convert_fusion.refs_2_, bf16[16,576,128]{2,1,0:T(8,128)(2,1)} %all-to-all-done.refs_3_, bf16[16,576,128]{2,1,0:T(8,128)(2,1)} %collective-permute-done.refs_4_), custom_call_target="tpu_custom_call" | custom-call | tf_op jit(solution)/shard_map/pallas_call | solution.py:135
  71.6 0.0 copy-start.1
  71.6 24.1 %all_to_all.25 = bf16[16,64,512]{2,1,0:T(8,128)(2,1)S(1)} all-to-all(bf16[16,64,512]{2,1,0:T(8,128)(2,1)S(1)} %shard_map.69), channel_id=1, replica_groups={{0,2,4,6},{8,10,12,14},{16,18,20,22},{24,26,28,30},{9,11,5,7},{17,19,13..., dimensions={0} | all-to-all | bytes 2097152 | tf_op jit(solution)/shard_map/all_to_all | solution.py:297
  95.7 0.1 shard_map.70
  95.9 21.6 %all_to_all.26.pieces_ref = bf16[4,64,512]{2,1,0:T(8,128)(2,1)S(1)} all-to-all(bf16[4,64,512]{2,1,0:T(8,128)(2,1)S(1)} %shard_map.70), channel_id=1, replica_groups=mesh['row_0'=4,'row_1'=4,'far'=4,'near'=4,'core'=2] {'far'}, dimensions={0} | all-to-all | bytes 524288 | tf_op jit(solution)/shard_map/all_to_all | solution.py:271
  117.5 0.0 copy-done.1
  117.5 0.2 shard_map.71
  117.7 17.7 %all_to_all.27.pieces_ref = f32[32,1,128]{2,1,0:T(1,128)S(1)} all-to-all(f32[32,1,128]{2,1,0:T(1,128)S(1)} %get-tuple-element.10), channel_id=1, replica_groups=mesh['row_0'=4,'row_1'=4,'far'=4,'near'=4,'core'=2] {'row_0','row_1','co..., dimensions={0} | all-to-all | bytes 32768 | tf_op jit(solution)/shard_map/all_to_all | solution.py:271
  135.4 16.9 %all_to_all.28.refs_0_ = f32[16,1,128]{2,1,0:T(1,128)S(1)} all-to-all(f32[16,1,128]{2,1,0:T(1,128)S(1)} %shard_map.72), channel_id=1, replica_groups=mesh['row_0'=4,'row_1'=4,'far'=4,'near'=4,'core'=2] {'far','near'}, dimensions={0} | all-to-all | bytes 16384 | tf_op jit(solution)/shard_map/all_to_all | solution.py:271
  152.3 0.8 shard_map.73
  (2 shorter events, 0.1 us)
Async XLA Ops:
  0.6 57.4 %copy-start = (f32[5,5,2,2]{1,3,2,0:T(2,128)S(1)}, f32[5,5,2,2]{1,3,2,0:T(2,128)}, u32[]{:S(2)}) copy-start(f32[5,5,2,2]{1,3,2,0:T(2,128)} %param.8) | copy-start | bytes 1204
  3.4 7.8 %copy-start.2 = (bf16[5,128,64]{1,2,0:T(8,128)(2,1)S(1)}, bf16[5,128,64]{1,2,0:T(8,128)(2,1)}, u32[]{:S(2)}) copy-start(bf16[5,128,64]{1,2,0:T(8,128)(2,1)} %param.6) | copy-start | bytes 245764
  3.4 54.6 %copy-start.3 = (f32[5,5,2,2]{1,3,2,0:T(2,128)S(1)}, f32[5,5,2,2]{1,3,2,0:T(2,128)}, u32[]{:S(2)}) copy-start(f32[5,5,2,2]{1,3,2,0:T(2,128)} %param.9) | copy-start | bytes 1204
  3.4 52.5 %all-to-all-start = ((bf16[16,576,128]{2,1,0:T(8,128)(2,1)}), bf16[16,576,128]{2,1,0:T(8,128)(2,1)}, u32[]{:S(2)}, u32[]{:S(2)}) async-start(bf16[16,576,128]{2,1,0:T(8,128)(2,1)} %shard_map.68), calls=%async_computation | async-start | bytes 4718592 | tf_op jit(solution)/shard_map/all_to_all | solution.py:271
  55.9 6.8 %collective-permute-start = (bf16[16,576,128]{2,1,0:T(8,128)(2,1)}, bf16[16,576,128]{2,1,0:T(8,128)(2,1)}, u32[]{:S(2)}, u32[]{:S(2)}) collective-permute-start(bf16[16,576,128]{2,1,0:T(8,128)(2,1)} %all-to-all-done.refs_3_), channel_id=1, source_target_pairs={{0,1},{1,0},{2,3},{3,2},{4,5},{5,4},{6,7},{7,6},{8,9},{9,8},{10,11... | collective-permute-start | bytes 7077896 | tf_op jit(solution)/shard_map/ppermute | solution.py:275
  71.6 45.9 %copy-start.1 = (bf16[4,128,64]{1,2,0:T(8,128)(2,1)S(1)}, bf16[4,128,64]{1,2,0:T(8,128)(2,1)}, u32[]{:S(2)}) copy-start(bf16[4,128,64]{1,2,0:T(8,128)(2,1)} %param.5) | copy-start | bytes 196612

commit v6 on v5

--- a/solution.py
+++ b/solution.py
@@ -21,7 +21,7 @@
 SMEM = pl.BlockSpec(memory_space=pltpu.SMEM)
 HBM = pl.BlockSpec(memory_space=pltpu.HBM)
 SMALL = pltpu.CompilerParams(vmem_limit_bytes=4 * 1024 * 1024)
-LARGE = pltpu.CompilerParams(vmem_limit_bytes=32 * 1024 * 1024)
+LARGE = pltpu.CompilerParams(vmem_limit_bytes=24 * 1024 * 1024)
 
 
 def in_hbm(x):
@@ -76,30 +76,12 @@
     )(in_hbm(vector), in_hbm(right))
 
 
-def terms_kernel(order, core_ref, table_ref, left_ref, own_hbm, other_hbm, out_ref, vec_s, left_s, right_s, cross_s, mixed_s, own_ref, other_ref, sems):
-    blocks, half, _ = out_ref.shape
-    width = 2 * half
-    core = core_ref[0]
-    own_at = pl.multiple_of(core * half, half)
-    other_at = pl.multiple_of((1 - core) * half, half)
-    parts = (pl.ds(0, STATES * half), pl.ds(STATES * half, CHANNELS * half))
-    copies = [
-        [pltpu.make_async_copy(src.at[:, part], dst.at[:, part], sems.at[i, j]) for j, (src, dst) in enumerate(((own_hbm, own_ref), (other_hbm, other_ref)))]
-        for i, part in enumerate(parts)
-    ]
-    for pair in copies:
-        for copy in pair:
-            copy.start()
-    for r in range(left_ref.shape[0]):
-        for w in range(CHANNELS):
-            left_s[r * half : (r + 1) * half, w * width : (w + 1) * width] = left_ref[r, w * half : (w + 1) * half, :]
-    for copy in copies[0]:
-        copy.wait()
+def contract_and_mix(table_ref, left_ref, source, vec_s, cross_s, store):
+    blocks, rows, width = source.shape
+    half = rows // STATES
     for r in range(blocks):
-        for source, at in ((own_ref, own_at), (other_ref, other_at)):
-            for t in range(STATES):
-                vec_s[pl.ds(t * width + at, half), r * width : (r + 1) * width] = source[r, t * half : (t + 1) * half, :]
-    cross_s[...] = jnp.dot(vec_s[...], left_s[...], preferred_element_type=jnp.float32)
+        vec_s[:, r * width : (r + 1) * width] = source[r]
+    cross_s[...] = jnp.dot(vec_s[...], left_ref[...], preferred_element_type=jnp.float32)
     for v in range(CHANNELS):
         for s in range(STATES):
             total = None
@@ -107,18 +89,83 @@
                 for t in range(STATES):
                     part = (
                         table_ref[v * STATES + s, w * STATES + t]
-                        * cross_s[t * width : (t + 1) * width, w * width : (w + 1) * width]
+                        * cross_s[t * half : (t + 1) * half, w * width : (w + 1) * width]
                     )
                     total = part if total is None else total + part
-            mixed_s[v * width : (v + 1) * width, s * width : (s + 1) * width] = total.astype(jnp.bfloat16)
-    for copy in copies[1]:
-        copy.wait()
+            store(v, s, total.astype(jnp.bfloat16))
+
+
+def own_kernel(table_ref, left_ref, own_hbm, left_out, mixed_out, right_out, piece_s, vec_s, cross_s, sems):
+    _, rows, width = piece_s.shape
+    half = rows // STATES
+    load = pltpu.make_async_copy(own_hbm.at[:, pl.ds(0, rows)], piece_s, sems.at[0])
+    load.start()
+    passed = pltpu.make_async_copy(own_hbm.at[:, pl.ds(rows, CHANNELS * half)], right_out, sems.at[1])
+    passed.start()
+    for k in range(left_ref.shape[0]):
+        for w in range(CHANNELS):
+            left_out[k * half : (k + 1) * half, w * width : (w + 1) * width] = left_ref[k, w * half : (w + 1) * half, :]
+    load.wait()
+
+    def store(v, s, x):
+        mixed_out[v * half : (v + 1) * half, s * width : (s + 1) * width] = x
+
+    contract_and_mix(table_ref, left_out, piece_s, vec_s, cross_s, store)
+    passed.wait()
+
+
+def own_part(table, left, own):
+    blocks, rows, width = own.shape
+    half = rows // (STATES + CHANNELS)
+    return pl.pallas_call(
+        own_kernel,
+        out_shape=(
+            jax.ShapeDtypeStruct((left.shape[0] * half, CHANNELS * width), jnp.bfloat16),
+            jax.ShapeDtypeStruct((CHANNELS * half, STATES * width), jnp.bfloat16),
+            jax.ShapeDtypeStruct((blocks, CHANNELS * half, width), jnp.bfloat16),
+        ),
+        in_specs=[SMEM, VMEM, HBM],
+        out_specs=(VMEM, VMEM, VMEM),
+        scratch_shapes=[
+            pltpu.VMEM((blocks, STATES * half, width), jnp.bfloat16),
+            pltpu.VMEM((STATES * half, blocks * width), jnp.bfloat16),
+            pltpu.VMEM((STATES * half, CHANNELS * width), jnp.float32),
+            pltpu.SemaphoreType.DMA((2,)),
+        ],
+        compiler_params=LARGE,
+    )(table, left, in_hbm(own))
+
+
+def terms_kernel(
+    order, core_ref, table_ref, left_ref, mixed_ref, right_own, other_hbm, out_ref,
+    piece_s, right_other, vec_s, cross_s, right_s, mixed_s, sems,
+):
+    blocks, half, _ = out_ref.shape
+    width = 2 * half
+    core = core_ref[0]
+    own_at = pl.multiple_of(core * half, half)
+    other_at = pl.multiple_of((1 - core) * half, half)
+    vectors, rights = pl.ds(0, STATES * half), pl.ds(STATES * half, CHANNELS * half)
+    loads = [
+        pltpu.make_async_copy(other_hbm.at[:, vectors], piece_s, sems.at[0]),
+        pltpu.make_async_copy(other_hbm.at[:, rights], right_other, sems.at[1]),
+    ]
+    for load in loads:
+        load.start()
+    for v in range(CHANNELS):
+        mixed_s[pl.ds(v * width + own_at, half), :] = mixed_ref[v * half : (v + 1) * half, :]
+    loads[0].wait()
+
+    def store(v, s, x):
+        mixed_s[pl.ds(v * width + other_at, half), s * width : (s + 1) * width] = x
+
+    contract_and_mix(table_ref, left_ref, piece_s, vec_s, cross_s, store)
+    loads[1].wait()
     mine = lax.broadcasted_iota(jnp.int32, (half, width), 1) // half == core
     for r in range(blocks):
         for v in range(CHANNELS):
-            at = (STATES + v) * half
-            own = own_ref[r, at : at + half, :].astype(jnp.float32)
-            other = other_ref[r, at : at + half, :].astype(jnp.float32)
+            own = right_own[r, v * half : (v + 1) * half, :].astype(jnp.float32)
+            other = right_other[r, v * half : (v + 1) * half, :].astype(jnp.float32)
             other = jnp.concatenate([other[:, half:], other[:, :half]], 1)
             right_s[r * half : (r + 1) * half, v * width : (v + 1) * width] = jnp.where(mine, own, other).astype(jnp.bfloat16)
     image = jnp.dot(right_s[...], mixed_s[...], preferred_element_type=jnp.float32)
@@ -126,29 +173,28 @@
         out_ref[order[r]] = image[r * half : (r + 1) * half].astype(jnp.bfloat16)
 
 
-def terms(order, core, table, left, own, other):
+def terms(order, core, table, left, mixed, right, other):
     def step(*refs):
         terms_kernel(order, *refs)
 
-    blocks, rows, width = own.shape
+    blocks, rows, width = other.shape
     half = rows // (STATES + CHANNELS)
     return pl.pallas_call(
         step,
         out_shape=jax.ShapeDtypeStruct((blocks, half, STATES * width), jnp.bfloat16),
-        in_specs=[SMEM, SMEM, VMEM, HBM, HBM],
+        in_specs=[SMEM, SMEM, VMEM, VMEM, VMEM, HBM],
         out_specs=VMEM,
         scratch_shapes=[
-            pltpu.VMEM((STATES * width, blocks * width), jnp.bfloat16),
-            pltpu.VMEM((blocks * width, CHANNELS * width), jnp.bfloat16),
+            pltpu.VMEM((blocks, STATES * half, width), jnp.bfloat16),
+            pltpu.VMEM((blocks, CHANNELS * half, width), jnp.bfloat16),
+            pltpu.VMEM((STATES * half, blocks * width), jnp.bfloat16),
+            pltpu.VMEM((STATES * half, CHANNELS * width), jnp.float32),
             pltpu.VMEM((blocks * half, CHANNELS * width), jnp.bfloat16),
-            pltpu.VMEM((STATES * width, CHANNELS * width), jnp.float32),
             pltpu.VMEM((CHANNELS * width, STATES * width), jnp.bfloat16),
-            pltpu.VMEM(own.shape, jnp.bfloat16),
-            pltpu.VMEM(other.shape, jnp.bfloat16),
-            pltpu.SemaphoreType.DMA((2, 2)),
+            pltpu.SemaphoreType.DMA((2,)),
         ],
         compiler_params=LARGE,
-    )(core, table, left, in_hbm(own), in_hbm(other))
+    )(core, table, left, mixed, right, in_hbm(other))
 
 
 def near_kernel(pieces_ref, out_ref):
@@ -292,7 +338,9 @@
     own, left = lax.optimization_barrier((own, left))
     left = (left.astype(jnp.float32) * (1.0 / SCALE)).astype(jnp.bfloat16)
     order = [n_far * (z % n_near) + z // n_near for z in range(n_z)]
-    sent = terms(order, core, table, left, own, other_core(own))
+    other = other_core(own)
+    left, mixed, right = own_part(table, left, own)
+    sent = terms(order, core, table, left, mixed, right, other)
 
     pieces = lax.all_to_all(sent, COL, 0, 0, axis_index_groups=neighbours(n_far, n_near), tiled=True)
     pieces = all_to_all(near_sum(pieces.reshape(n_near, n_far, *pieces.shape[1:])), FAR)

time: 154 us -> 151 us (0.981)
  waiting for transfers between devices: 2.95 us -> 0.01 us
    pallas_call x0 -> x1, Pallas kernels: none -> 4.12 us  [own_part(): pl.pallas_call(own_kernel, out_shape=(jax.ShapeDtypeStruct((left.shape[0]...]
    pallas_call x1, Pallas kernels: 8.89 us -> 5.23 us  [terms(): pl.pallas_call(step, out_shape=jax.ShapeDtypeStruct((blocks, half, STATES...]
    ppermute x1, waiting for transfers between devices: 2.94 us -> 0.01 us  [other_core(): return lax.ppermute(x, C, [(0, 1), (1, 0)])]
  transfers between devices with their start and end apart: 2 -> 2, of which waited for: 1 -> 0; matrix products, arithmetic and copies ran while one was open for 1% -> 1% of each run, Pallas kernels for 0% -> 3%
where the time goes in v6:
time: 151 us
  blocking collectives  125 us (83%)
  Pallas kernels  13.2 us (9%)
  starting transfers between devices  9.82 us (7%)
    all_to_all x3, blocking collectives, all_to_all(): return lax.all_to_all(x, axes, 0, 0, tiled=True)  56.2 us
    all_gather x1, blocking collectives, body(): left = lax.all_gather(left, COL, axis=0)  44.7 us
    all_to_all x1, blocking collectives, body(): lax.all_to_all(sent, COL, 0, 0, axis_index_groups=neighbours(n_far, n_nea...  24.1 us
    all_to_all x1, starting transfers between devices, all_to_all(): return lax.all_to_all(x, axes, 0, 0, tiled=True)  7.76 us
    pallas_call x1, Pallas kernels, terms(): pl.pallas_call(step, out_shape=jax.ShapeDtypeStruct((blocks, half, STATES...  5.23 us
    pallas_call x1, Pallas kernels, own_part(): pl.pallas_call(own_kernel, out_shape=(jax.ShapeDtypeStruct((left.shape[0]...  4.12 us
  transfers between devices with their start and end apart: 2, of which 0 were waited for; matrix products, arithmetic and copies ran while one was open for 1% of the time, Pallas kernels for 3%

profile of v6, /device:TPU:1, one launch (start us, length us, event | category | flops | bytes accessed | tf_op | source)
XLA Modules:
  0.0 150.6 jit_solution(8514942128144099510)
XLA Ops:
  0.6 0.0 copy-start
  0.6 2.7 %shard_map.68 = bf16[16,576,128]{2,1,0:T(8,128)(2,1)} custom-call(bf16[4,64,128]{2,1,0:T(8,128)(2,1)} %bitcast.13, bf16[5,64,128]{2,1,0:T(8,128)(2,1)} %right_hbm.1), custom_call_target="tpu_custom_call" | custom-call | tf_op jit(solution)/shard_map/pallas_call | solution.py:63
  3.4 0.0 copy-start.2
  3.4 0.0 copy-start.3
  3.4 7.8 %all-to-all-start = ((bf16[16,576,128]{2,1,0:T(8,128)(2,1)}), bf16[16,576,128]{2,1,0:T(8,128)(2,1)}, u32[]{:S(2)}, u32[]{:S(2)}) async-start(bf16[16,576,128]{2,1,0:T(8,128)(2,1)} %shard_map.68), calls=%async_computation | async-start | bytes 4718592 | tf_op jit(solution)/shard_map/all_to_all | solution.py:317
  11.2 0.0 copy-done.2
  11.2 44.7 %all-gather.1 = f16[32,320,128]{2,1,0:T(8,128)(2,1)S(1)} all-gather(f16[1,320,128]{2,1,0:T(8,128)(2,1)S(1)} %bitcast.16), channel_id=1, replica_groups=mesh['row_0'=4,'row_1'=4,'far'=4,'near'=4,'core'=2] {'far','near','core'}, dimensions={0}, use_global_device_ids=true | all-gather | bytes 2703360 | tf_op jit(solution)/shard_map/all_gather | solution.py:337
  55.9 0.0 all-to-all-done.own_hbm
  55.9 2.1 %collective-permute-start = (bf16[16,576,128]{2,1,0:T(8,128)(2,1)}, bf16[16,576,128]{2,1,0:T(8,128)(2,1)}, u32[]{:S(2)}, u32[]{:S(2)}) collective-permute-start(bf16[16,576,128]{2,1,0:T(8,128)(2,1)} %all-to-all-done.own_hbm), channel_id=1, source_target_pairs={{0,1},{1,0},{2,3},{3,2},{4,5},{5,4},{6,7},{7,6},{8,9},{9,8},{10,11... | collective-permute-start | bytes 7077896 | tf_op jit(solution)/shard_map/ppermute | solution.py:321
  58.0 0.0 copy-done
  58.0 0.0 copy-done.3
  58.0 0.4 convolution_bitcast_fusion
  58.4 0.4 copy.15
  58.8 0.1 reshape.35.table_ref.refs_1_
  58.9 0.8 multiply_convert_fusion.left_ref
  59.8 4.1 %shard_map.69 = (bf16[2048,640]{1,0:T(8,128)(2,1)S(1)}, bf16[320,512]{1,0:T(8,128)(2,1)S(1)}, bf16[16,320,128]{2,1,0:T(8,128)(2,1)S(1)}) custom-call(f32[20,20]{1,0:T(8,128)S(1)} %reshape.35.table_ref.refs_1_, bf16[32,320,128]{2,1,0:T(8,128)(2,1)S(1)} %multiply_convert_fusion.left_ref, bf16[16,576,128]{2,1,0:T(8,128)(2,1)} %all-to-all-done.own_hbm), custom_call_target="tpu_custom_call" | custom-call | tf_op jit(solution)/shard_map/pallas_call | solution.py:120
  63.9 0.0 collective-permute-done.refs_5_
  63.9 5.2 %shard_map.70 = bf16[16,64,512]{2,1,0:T(8,128)(2,1)S(1)} custom-call(s32[1]{0:T(128)} %bitcast.refs_0_, f32[20,20]{1,0:T(8,128)S(1)} %reshape.35.table_ref.refs_1_, bf16[2048,640]{1,0:T(8,128)(2,1)S(1)} %get-tuple-element.13.refs_2_, bf16[320,512]{1,0:T(8,128)(2,1)S(1)} %get-tuple-element.14.refs_3_, bf16[16,320,128]{2,1,0:T(8,128)(2,1)S(1)} %get-tuple-element.15.refs_4_, ...), custom_call_target="tpu_custom_call" | custom-call | tf_op jit(solution)/shard_map/pallas_call | solution.py:182
  69.1 0.0 copy-start.1
  69.1 24.1 %all_to_all.25 = bf16[16,64,512]{2,1,0:T(8,128)(2,1)S(1)} all-to-all(bf16[16,64,512]{2,1,0:T(8,128)(2,1)S(1)} %shard_map.70), channel_id=1, replica_groups={{0,2,4,6},{8,10,12,14},{16,18,20,22},{24,26,28,30},{9,11,5,7},{17,19,13..., dimensions={0} | all-to-all | bytes 2097152 | tf_op jit(solution)/shard_map/all_to_all | solution.py:345
  93.3 0.1 shard_map.71
  93.4 21.6 %all_to_all.26.pieces_ref = bf16[4,64,512]{2,1,0:T(8,128)(2,1)S(1)} all-to-all(bf16[4,64,512]{2,1,0:T(8,128)(2,1)S(1)} %shard_map.71), channel_id=1, replica_groups=mesh['row_0'=4,'row_1'=4,'far'=4,'near'=4,'core'=2] {'far'}, dimensions={0} | all-to-all | bytes 524288 | tf_op jit(solution)/shard_map/all_to_all | solution.py:317
  115.0 0.0 copy-done.1
  115.0 0.2 shard_map.72
  115.2 17.7 %all_to_all.27.pieces_ref = f32[32,1,128]{2,1,0:T(1,128)S(1)} all-to-all(f32[32,1,128]{2,1,0:T(1,128)S(1)} %get-tuple-element.16), channel_id=1, replica_groups=mesh['row_0'=4,'row_1'=4,'far'=4,'near'=4,'core'=2] {'row_0','row_1','co..., dimensions={0} | all-to-all | bytes 32768 | tf_op jit(solution)/shard_map/all_to_all | solution.py:317
  133.0 16.9 %all_to_all.28.refs_0_ = f32[16,1,128]{2,1,0:T(1,128)S(1)} all-to-all(f32[16,1,128]{2,1,0:T(1,128)S(1)} %shard_map.73), channel_id=1, replica_groups=mesh['row_0'=4,'row_1'=4,'far'=4,'near'=4,'core'=2] {'far','near'}, dimensions={0} | all-to-all | bytes 16384 | tf_op jit(solution)/shard_map/all_to_all | solution.py:317
  149.8 0.8 shard_map.74
  (2 shorter events, 0.1 us)
Async XLA Ops:
  0.6 57.4 %copy-start = (f32[5,5,2,2]{1,3,2,0:T(2,128)S(1)}, f32[5,5,2,2]{1,3,2,0:T(2,128)}, u32[]{:S(2)}) copy-start(f32[5,5,2,2]{1,3,2,0:T(2,128)} %param.8) | copy-start | bytes 1204
  3.4 7.8 %copy-start.2 = (bf16[5,128,64]{1,2,0:T(8,128)(2,1)S(1)}, bf16[5,128,64]{1,2,0:T(8,128)(2,1)}, u32[]{:S(2)}) copy-start(bf16[5,128,64]{1,2,0:T(8,128)(2,1)} %param.6) | copy-start | bytes 245764
  3.4 54.6 %copy-start.3 = (f32[5,5,2,2]{1,3,2,0:T(2,128)S(1)}, f32[5,5,2,2]{1,3,2,0:T(2,128)}, u32[]{:S(2)}) copy-start(f32[5,5,2,2]{1,3,2,0:T(2,128)} %param.9) | copy-start | bytes 1204
  3.4 52.5 %all-to-all-start = ((bf16[16,576,128]{2,1,0:T(8,128)(2,1)}), bf16[16,576,128]{2,1,0:T(8,128)(2,1)}, u32[]{:S(2)}, u32[]{:S(2)}) async-start(bf16[16,576,128]{2,1,0:T(8,128)(2,1)} %shard_map.68), calls=%async_computation | async-start | bytes 4718592 | tf_op jit(solution)/shard_map/all_to_all | solution.py:317
  55.9 8.0 %collective-permute-start = (bf16[16,576,128]{2,1,0:T(8,128)(2,1)}, bf16[16,576,128]{2,1,0:T(8,128)(2,1)}, u32[]{:S(2)}, u32[]{:S(2)}) collective-permute-start(bf16[16,576,128]{2,1,0:T(8,128)(2,1)} %all-to-all-done.own_hbm), channel_id=1, source_target_pairs={{0,1},{1,0},{2,3},{3,2},{4,5},{5,4},{6,7},{7,6},{8,9},{9,8},{10,11... | collective-permute-start | bytes 7077896 | tf_op jit(solution)/shard_map/ppermute | solution.py:321
  69.1 45.8 %copy-start.1 = (bf16[4,128,64]{1,2,0:T(8,128)(2,1)S(1)}, bf16[4,128,64]{1,2,0:T(8,128)(2,1)}, u32[]{:S(2)}) copy-start(bf16[4,128,64]{1,2,0:T(8,128)(2,1)} %param.5) | copy-start | bytes 196612

commit v7 on v6

--- a/solution.py
+++ b/solution.py
@@ -12,7 +12,6 @@
 COL = (FAR, NEAR, C)
 STATES = 4
 CHANNELS = 5
-PAIRS = STATES * CHANNELS
 
 epsilon = 1e-06
 SCALE = 8192.0
@@ -26,11 +25,6 @@
 
 def in_hbm(x):
     return pltpu.with_memory_space_constraint(x, pltpu.HBM)
-
-
-def coupling(left_tensor, right_tensor):
-    joined = jnp.einsum("wuac,uvbd->vabwcd", left_tensor, right_tensor, precision=lax.Precision.HIGHEST)
-    return joined.reshape(PAIRS, PAIRS)
 
 
 def pack_kernel(vector_hbm, right_hbm, out_hbm, vector_s, right_s, piece_s, in_sems, out_sems):
@@ -76,32 +70,59 @@
     )(in_hbm(vector), in_hbm(right))
 
 
-def contract_and_mix(table_ref, left_ref, source, vec_s, cross_s, store):
+def site_copies(left_site, right_site, left_t, right_t, left_sem, right_sem):
+    loads = (
+        pltpu.make_async_copy(left_site, left_t, left_sem),
+        pltpu.make_async_copy(right_site, right_t, right_sem),
+    )
+    for load in loads:
+        load.start()
+    return loads
+
+
+def combined(terms):
+    total = None
+    for scale, x in terms:
+        total = scale * x if total is None else total + scale * x
+    return total
+
+
+def contract_and_mix(site_loads, left_t, right_t, left_ref, source, vec_s, cross_s, half_s, store):
     blocks, rows, width = source.shape
     half = rows // STATES
     for r in range(blocks):
         vec_s[:, r * width : (r + 1) * width] = source[r]
     cross_s[...] = jnp.dot(vec_s[...], left_ref[...], preferred_element_type=jnp.float32)
-    for v in range(CHANNELS):
-        for s in range(STATES):
-            total = None
-            for w in range(CHANNELS):
-                for t in range(STATES):
-                    part = (
-                        table_ref[v * STATES + s, w * STATES + t]
-                        * cross_s[t * half : (t + 1) * half, w * width : (w + 1) * width]
+    for load in site_loads:
+        load.wait()
+    for s1 in range(2):
+        for u in range(CHANNELS):
+            for t2 in range(2):
+                half_s[u, t2] = combined(
+                    (
+                        left_t[w, s1, t1, u],
+                        cross_s[(2 * t1 + t2) * half : (2 * t1 + t2 + 1) * half, w * width : (w + 1) * width],
                     )
-                    total = part if total is None else total + part
-            store(v, s, total.astype(jnp.bfloat16))
-
-
-def own_kernel(table_ref, left_ref, own_hbm, left_out, mixed_out, right_out, piece_s, vec_s, cross_s, sems):
+                    for w in range(CHANNELS)
+                    for t1 in range(2)
+                )
+        for v in range(CHANNELS):
+            for s2 in range(2):
+                total = combined((right_t[u, s2, t2, v], half_s[u, t2]) for u in range(CHANNELS) for t2 in range(2))
+                store(v, 2 * s1 + s2, total.astype(jnp.bfloat16))
+
+
+def own_kernel(
+    left_site, right_site, left_ref, own_hbm, left_out, mixed_out, right_out,
+    left_t, right_t, piece_s, vec_s, cross_s, half_s, sems,
+):
     _, rows, width = piece_s.shape
     half = rows // STATES
     load = pltpu.make_async_copy(own_hbm.at[:, pl.ds(0, rows)], piece_s, sems.at[0])
     load.start()
     passed = pltpu.make_async_copy(own_hbm.at[:, pl.ds(rows, CHANNELS * half)], right_out, sems.at[1])
     passed.start()
+    site_loads = site_copies(left_site, right_site, left_t, right_t, sems.at[2], sems.at[3])
     for k in range(left_ref.shape[0]):
         for w in range(CHANNELS):
             left_out[k * half : (k + 1) * half, w * width : (w + 1) * width] = left_ref[k, w * half : (w + 1) * half, :]
@@ -110,11 +131,11 @@
     def store(v, s, x):
         mixed_out[v * half : (v + 1) * half, s * width : (s + 1) * width] = x
 
-    contract_and_mix(table_ref, left_out, piece_s, vec_s, cross_s, store)
+    contract_and_mix(site_loads, left_t, right_t, left_out, piece_s, vec_s, cross_s, half_s, store)
     passed.wait()
 
 
-def own_part(table, left, own):
+def own_part(sites, left, own):
     blocks, rows, width = own.shape
     half = rows // (STATES + CHANNELS)
     return pl.pallas_call(
@@ -124,21 +145,23 @@
             jax.ShapeDtypeStruct((CHANNELS * half, STATES * width), jnp.bfloat16),
             jax.ShapeDtypeStruct((blocks, CHANNELS * half, width), jnp.bfloat16),
         ),
-        in_specs=[SMEM, VMEM, HBM],
+        in_specs=[HBM, HBM, VMEM, HBM],
         out_specs=(VMEM, VMEM, VMEM),
         scratch_shapes=[
+            *(pltpu.SMEM(site.shape, jnp.float32) for site in sites),
             pltpu.VMEM((blocks, STATES * half, width), jnp.bfloat16),
             pltpu.VMEM((STATES * half, blocks * width), jnp.bfloat16),
             pltpu.VMEM((STATES * half, CHANNELS * width), jnp.float32),
-            pltpu.SemaphoreType.DMA((2,)),
+            pltpu.VMEM((CHANNELS, 2, half, width), jnp.float32),
+            pltpu.SemaphoreType.DMA((4,)),
         ],
         compiler_params=LARGE,
-    )(table, left, in_hbm(own))
+    )(*(in_hbm(site) for site in sites), left, in_hbm(own))
 
 
 def terms_kernel(
-    order, core_ref, table_ref, left_ref, mixed_ref, right_own, other_hbm, out_ref,
-    piece_s, right_other, vec_s, cross_s, right_s, mixed_s, sems,
+    order, core_ref, left_site, right_site, left_ref, mixed_ref, right_own, other_hbm, out_ref,
+    left_t, right_t, piece_s, right_other, vec_s, cross_s, half_s, right_s, mixed_s, sems,
 ):
     blocks, half, _ = out_ref.shape
     width = 2 * half
@@ -152,28 +175,31 @@
     ]
     for load in loads:
         load.start()
+    site_loads = site_copies(left_site, right_site, left_t, right_t, sems.at[2], sems.at[3])
+    mine = lax.broadcasted_iota(jnp.int32, (half, width), 1) // half == core
     for v in range(CHANNELS):
         mixed_s[pl.ds(v * width + own_at, half), :] = mixed_ref[v * half : (v + 1) * half, :]
+        for r in range(blocks):
+            right_s[r * half : (r + 1) * half, v * width : (v + 1) * width] = right_own[r, v * half : (v + 1) * half, :]
     loads[0].wait()
 
     def store(v, s, x):
         mixed_s[pl.ds(v * width + other_at, half), s * width : (s + 1) * width] = x
 
-    contract_and_mix(table_ref, left_ref, piece_s, vec_s, cross_s, store)
+    contract_and_mix(site_loads, left_t, right_t, left_ref, piece_s, vec_s, cross_s, half_s, store)
     loads[1].wait()
-    mine = lax.broadcasted_iota(jnp.int32, (half, width), 1) // half == core
     for r in range(blocks):
         for v in range(CHANNELS):
-            own = right_own[r, v * half : (v + 1) * half, :].astype(jnp.float32)
+            at = (slice(r * half, (r + 1) * half), slice(v * width, (v + 1) * width))
             other = right_other[r, v * half : (v + 1) * half, :].astype(jnp.float32)
             other = jnp.concatenate([other[:, half:], other[:, :half]], 1)
-            right_s[r * half : (r + 1) * half, v * width : (v + 1) * width] = jnp.where(mine, own, other).astype(jnp.bfloat16)
+            right_s[at] = jnp.where(mine, right_s[at].astype(jnp.float32), other).astype(jnp.bfloat16)
     image = jnp.dot(right_s[...], mixed_s[...], preferred_element_type=jnp.float32)
     for r in range(blocks):
         out_ref[order[r]] = image[r * half : (r + 1) * half].astype(jnp.bfloat16)
 
 
-def terms(order, core, table, left, mixed, right, other):
+def terms(order, core, sites, left, mixed, right, other):
     def step(*refs):
         terms_kernel(order, *refs)
 
@@ -182,19 +208,21 @@
     return pl.pallas_call(
         step,
         out_shape=jax.ShapeDtypeStruct((blocks, half, STATES * width), jnp.bfloat16),
-        in_specs=[SMEM, SMEM, VMEM, VMEM, VMEM, HBM],
+        in_specs=[SMEM, HBM, HBM, VMEM, VMEM, VMEM, HBM],
         out_specs=VMEM,
         scratch_shapes=[
+            *(pltpu.SMEM(site.shape, jnp.float32) for site in sites),
             pltpu.VMEM((blocks, STATES * half, width), jnp.bfloat16),
             pltpu.VMEM((blocks, CHANNELS * half, width), jnp.bfloat16),
             pltpu.VMEM((STATES * half, blocks * width), jnp.bfloat16),
             pltpu.VMEM((STATES * half, CHANNELS * width), jnp.float32),
+            pltpu.VMEM((CHANNELS, 2, half, width), jnp.float32),
             pltpu.VMEM((blocks * half, CHANNELS * width), jnp.bfloat16),
             pltpu.VMEM((CHANNELS * width, STATES * width), jnp.bfloat16),
-            pltpu.SemaphoreType.DMA((2,)),
+            pltpu.SemaphoreType.DMA((4,)),
         ],
         compiler_params=LARGE,
-    )(core, table, left, mixed, right, in_hbm(other))
+    )(core, *(in_hbm(site) for site in sites), left, mixed, right, in_hbm(other))
 
 
 def near_kernel(pieces_ref, out_ref):
@@ -328,7 +356,7 @@
     _, rows, half = start_vector.shape
     entries = float(STATES * rows * half * n_row * n_z * lax.axis_size(C))
     core = lax.axis_index(C).astype(jnp.int32).reshape(1)
-    table = coupling(left_tensor, right_tensor)
+    sites = tuple(jnp.transpose(tensor, (0, 2, 3, 1)) for tensor in (left_tensor, right_tensor))
     vector = jnp.swapaxes(start_vector, 1, 2)
     left = jnp.swapaxes(left_env, 1, 2).reshape(CHANNELS * half, rows)
     left = (left.astype(jnp.float32) * SCALE).astype(jnp.float16)
@@ -339,14 +367,14 @@
     left = (left.astype(jnp.float32) * (1.0 / SCALE)).astype(jnp.bfloat16)
     order = [n_far * (z % n_near) + z // n_near for z in range(n_z)]
     other = other_core(own)
-    left, mixed, right = own_part(table, left, own)
-    sent = terms(order, core, table, left, mixed, right, other)
+    left, mixed, right = own_part(sites, left, own)
+    sent = terms(order, core, sites, left, mixed, right, other)
 
     pieces = lax.all_to_all(sent, COL, 0, 0, axis_index_groups=neighbours(n_far, n_near), tiled=True)
     pieces = all_to_all(near_sum(pieces.reshape(n_near, n_far, *pieces.shape[1:])), FAR)
-    image, sums = sums_of(pieces, vector, lax.axis_size((X, Y, C)))
-    sums = again(all_to_all(sums, (X, Y, C)), n_z)
-    next_vector, coefficients = last(entries, all_to_all(sums, Z), image, vector)
+    image, sums = sums_of(pieces, vector, n_z)
+    sums = again(all_to_all(sums, Z), lax.axis_size((X, Y, C)))
+    next_vector, coefficients = last(entries, all_to_all(sums, (X, Y, C)), image, vector)
     return jnp.swapaxes(next_vector, 1, 2), coefficients
 
 

time: 151 us -> 150 us (level)
  Pallas kernels: 13.2 us -> 11.2 us
  transfers between devices with their start and end apart: 2 -> 2, of which waited for: 0 -> 1; matrix products, arithmetic and copies ran while one was open for 1% -> 1% of each run, Pallas kernels for 3% -> 2%
where the time goes in v7:
time: 150 us
  blocking collectives  126 us (84%)
  Pallas kernels  11.2 us (7%)
  starting transfers between devices  9.82 us (7%)
    all_to_all x3, blocking collectives, all_to_all(): return lax.all_to_all(x, axes, 0, 0, tiled=True)  57.6 us
    all_gather x1, blocking collectives, body(): left = lax.all_gather(left, COL, axis=0)  44.7 us
    all_to_all x1, blocking collectives, body(): lax.all_to_all(sent, COL, 0, 0, axis_index_groups=neighbours(n_far, n_nea...  24.1 us
    all_to_all x1, starting transfers between devices, all_to_all(): return lax.all_to_all(x, axes, 0, 0, tiled=True)  7.76 us
    pallas_call x1, Pallas kernels, terms(): pl.pallas_call(step, out_shape=jax.ShapeDtypeStruct((blocks, half, STATES...  4.22 us
    pallas_call x1, Pallas kernels, own_part(): pl.pallas_call(own_kernel, out_shape=(jax.ShapeDtypeStruct((left.shape[0]...  3.15 us
  transfers between devices with their start and end apart: 2, of which 1 were waited for; matrix products, arithmetic and copies ran while one was open for 1% of the time, Pallas kernels for 2%

profile of v7, /device:TPU:1, one launch (start us, length us, event | category | flops | bytes accessed | tf_op | source)
XLA Modules:
  0.0 149.8 jit_solution(6345306140889249577)
XLA Ops:
  0.6 2.7 %shard_map.68 = bf16[16,576,128]{2,1,0:T(8,128)(2,1)} custom-call(bf16[4,64,128]{2,1,0:T(8,128)(2,1)} %bitcast.10, bf16[5,64,128]{2,1,0:T(8,128)(2,1)} %right_hbm.1), custom_call_target="tpu_custom_call" | custom-call | tf_op jit(solution)/shard_map/pallas_call | solution.py:57
  3.3 0.0 copy-start.1
  3.4 7.8 %all-to-all-start = ((bf16[16,576,128]{2,1,0:T(8,128)(2,1)}), bf16[16,576,128]{2,1,0:T(8,128)(2,1)}, u32[]{:S(2)}, u32[]{:S(2)}) async-start(bf16[16,576,128]{2,1,0:T(8,128)(2,1)} %shard_map.68), calls=%async_computation | async-start | bytes 4718592 | tf_op jit(solution)/shard_map/all_to_all | solution.py:345
  11.1 0.0 copy-done.1
  11.2 44.7 %all-gather.1 = f16[32,320,128]{2,1,0:T(8,128)(2,1)S(1)} all-gather(f16[1,320,128]{2,1,0:T(8,128)(2,1)S(1)} %bitcast.13), channel_id=1, replica_groups=mesh['row_0'=4,'row_1'=4,'far'=4,'near'=4,'core'=2] {'far','near','core'}, dimensions={0}, use_global_device_ids=true | all-gather | bytes 2703360 | tf_op jit(solution)/shard_map/all_gather | solution.py:365
  55.9 0.0 all-to-all-done.own_hbm
  55.9 2.1 %collective-permute-start = (bf16[16,576,128]{2,1,0:T(8,128)(2,1)}, bf16[16,576,128]{2,1,0:T(8,128)(2,1)}, u32[]{:S(2)}, u32[]{:S(2)}) collective-permute-start(bf16[16,576,128]{2,1,0:T(8,128)(2,1)} %all-to-all-done.own_hbm), channel_id=1, source_target_pairs={{0,1},{1,0},{2,3},{3,2},{4,5},{5,4},{6,7},{7,6},{8,9},{9,8},{10,11... | collective-permute-start | bytes 7077896 | tf_op jit(solution)/shard_map/ppermute | solution.py:349
  58.0 0.8 multiply_convert_fusion.left_ref
  58.8 3.1 %shard_map.69 = (bf16[2048,640]{1,0:T(8,128)(2,1)S(1)}, bf16[320,512]{1,0:T(8,128)(2,1)S(1)}, bf16[16,320,128]{2,1,0:T(8,128)(2,1)S(1)}) custom-call(f32[5,2,2,5]{3,2,1,0:T(2,128)} %bitcast.14, f32[5,2,2,5]{3,2,1,0:T(2,128)} %bitcast.16, bf16[32,320,128]{2,1,0:T(8,128)(2,1)S(1)} %multiply_convert_fusion.left_ref, bf16[16,576,128]{2,1,0:T(8,128)(2,1)} %all-to-all-done.own_hbm), custom_call_target="tpu_custom_call" | custom-call | tf_op jit(solution)/shard_map/pallas_call | solution.py:141
  61.9 0.7 collective-permute-done.refs_6_
  62.7 4.2 %shard_map.70 = bf16[16,64,512]{2,1,0:T(8,128)(2,1)S(1)} custom-call(s32[1]{0:T(128)} %bitcast.refs_0_, f32[5,2,2,5]{3,2,1,0:T(2,128)} %bitcast.15, f32[5,2,2,5]{3,2,1,0:T(2,128)} %bitcast.17, bf16[2048,640]{1,0:T(8,128)(2,1)S(1)} %get-tuple-element.13.refs_3_, bf16[320,512]{1,0:T(8,128)(2,1)S(1)} %get-tuple-element.14.refs_4_, ...), custom_call_target="tpu_custom_call" | custom-call | tf_op jit(solution)/shard_map/pallas_call | solution.py:208
  66.9 0.0 copy-start
  66.9 24.1 %all_to_all.25 = bf16[16,64,512]{2,1,0:T(8,128)(2,1)S(1)} all-to-all(bf16[16,64,512]{2,1,0:T(8,128)(2,1)S(1)} %shard_map.70), channel_id=1, replica_groups={{0,2,4,6},{8,10,12,14},{16,18,20,22},{24,26,28,30},{9,11,5,7},{17,19,13..., dimensions={0} | all-to-all | bytes 2097152 | tf_op jit(solution)/shard_map/all_to_all | solution.py:373
  91.0 0.1 shard_map.71
  91.2 21.6 %all_to_all.26.pieces_ref = bf16[4,64,512]{2,1,0:T(8,128)(2,1)S(1)} all-to-all(bf16[4,64,512]{2,1,0:T(8,128)(2,1)S(1)} %shard_map.71), channel_id=1, replica_groups=mesh['row_0'=4,'row_1'=4,'far'=4,'near'=4,'core'=2] {'far'}, dimensions={0} | all-to-all | bytes 524288 | tf_op jit(solution)/shard_map/all_to_all | solution.py:345
  112.7 0.0 copy-done
  112.7 0.2 shard_map.72
  112.9 19.8 %all_to_all.27.pieces_ref = f32[16,1,128]{2,1,0:T(1,128)S(1)} all-to-all(f32[16,1,128]{2,1,0:T(1,128)S(1)} %get-tuple-element.16), channel_id=1, replica_groups=mesh['row_0'=4,'row_1'=4,'far'=4,'near'=4,'core'=2] {'far','near'}, dimensions={0} | all-to-all | bytes 16384 | tf_op jit(solution)/shard_map/all_to_all | solution.py:345
  132.8 16.2 %all_to_all.28.refs_0_ = f32[32,1,128]{2,1,0:T(1,128)S(1)} all-to-all(f32[32,1,128]{2,1,0:T(1,128)S(1)} %shard_map.73), channel_id=1, replica_groups=mesh['row_0'=4,'row_1'=4,'far'=4,'near'=4,'core'=2] {'row_0','row_1','co..., dimensions={0} | all-to-all | bytes 32768 | tf_op jit(solution)/shard_map/all_to_all | solution.py:345
  149.0 0.8 shard_map.74
  (2 shorter events, 0.1 us)
Async XLA Ops:
  3.3 7.8 %copy-start.1 = (bf16[5,128,64]{1,2,0:T(8,128)(2,1)S(1)}, bf16[5,128,64]{1,2,0:T(8,128)(2,1)}, u32[]{:S(2)}) copy-start(bf16[5,128,64]{1,2,0:T(8,128)(2,1)} %param.6) | copy-start | bytes 245764
  3.4 52.5 %all-to-all-start = ((bf16[16,576,128]{2,1,0:T(8,128)(2,1)}), bf16[16,576,128]{2,1,0:T(8,128)(2,1)}, u32[]{:S(2)}, u32[]{:S(2)}) async-start(bf16[16,576,128]{2,1,0:T(8,128)(2,1)} %shard_map.68), calls=%async_computation | async-start | bytes 4718592 | tf_op jit(solution)/shard_map/all_to_all | solution.py:345
  55.9 6.8 %collective-permute-start = (bf16[16,576,128]{2,1,0:T(8,128)(2,1)}, bf16[16,576,128]{2,1,0:T(8,128)(2,1)}, u32[]{:S(2)}, u32[]{:S(2)}) collective-permute-start(bf16[16,576,128]{2,1,0:T(8,128)(2,1)} %all-to-all-done.own_hbm), channel_id=1, source_target_pairs={{0,1},{1,0},{2,3},{3,2},{4,5},{5,4},{6,7},{7,6},{8,9},{9,8},{10,11... | collective-permute-start | bytes 7077896 | tf_op jit(solution)/shard_map/ppermute | solution.py:349
  66.9 45.9 %copy-start = (bf16[4,128,64]{1,2,0:T(8,128)(2,1)S(1)}, bf16[4,128,64]{1,2,0:T(8,128)(2,1)}, u32[]{:S(2)}) copy-start(bf16[4,128,64]{1,2,0:T(8,128)(2,1)} %param.5) | copy-start | bytes 196612

commit v8 on v7

--- a/solution.py
+++ b/solution.py
@@ -27,53 +27,55 @@
     return pltpu.with_memory_space_constraint(x, pltpu.HBM)
 
 
-def pack_kernel(vector_hbm, right_hbm, out_hbm, vector_s, right_s, piece_s, in_sems, out_sems):
-    states, half, width = vector_s.shape
-    rights = right_s.shape[0]
+def pack_kernel(vector_hbm, right_hbm, out_hbm, vector_s, right_s, turned_s, in_sems, out_sems):
+    half, _ = right_s.shape[1:]
+    rows = vector_s.shape[0]
     loads = [
         pltpu.make_async_copy(vector_hbm, vector_s, in_sems.at[0]),
         pltpu.make_async_copy(right_hbm, right_s, in_sems.at[1]),
     ]
     for load in loads:
         load.start()
+    places = range(out_hbm.shape[0])
+    stores = [pltpu.make_async_copy(vector_s, out_hbm.at[r, pl.ds(0, rows)], out_sems.at[0, r]) for r in places]
     loads[0].wait()
-    for t in range(states):
-        piece_s[t * half : (t + 1) * half, :] = vector_s[t]
+    for store in stores:
+        store.start()
     loads[1].wait()
-    for v in range(rights):
+    for v in range(right_s.shape[0]):
         turned = right_s[v].astype(jnp.float32).T
         turned = jnp.concatenate([turned[:half], turned[half:]], 1).astype(jnp.bfloat16)
-        piece_s[(states + v) * half : (states + v + 1) * half, :] = turned
-    stores = [pltpu.make_async_copy(piece_s, out_hbm.at[r], out_sems.at[r]) for r in range(out_hbm.shape[0])]
-    for store in stores:
+        turned_s[v * half : (v + 1) * half, :] = turned
+    more = [pltpu.make_async_copy(turned_s, out_hbm.at[r, pl.ds(rows, turned_s.shape[0])], out_sems.at[1, r]) for r in places]
+    for store in more:
         store.start()
-    for store in stores:
+    for store in stores + more:
         store.wait()
 
 
 def pack(vector, right, size):
-    states, half, width = vector.shape
-    rows = (states + right.shape[0]) * half
+    rows, width = vector.shape
+    channels, half, _ = right.shape
     return pl.pallas_call(
         pack_kernel,
-        out_shape=pltpu.HBM((size, rows, width), jnp.bfloat16),
+        out_shape=pltpu.HBM((size, rows + channels * half, width), jnp.bfloat16),
         in_specs=[HBM, HBM],
         out_specs=HBM,
         scratch_shapes=[
             pltpu.VMEM(vector.shape, jnp.bfloat16),
             pltpu.VMEM(right.shape, jnp.bfloat16),
-            pltpu.VMEM((rows, width), jnp.bfloat16),
+            pltpu.VMEM((channels * half, width), jnp.bfloat16),
             pltpu.SemaphoreType.DMA((2,)),
-            pltpu.SemaphoreType.DMA((size,)),
+            pltpu.SemaphoreType.DMA((2, size)),
         ],
         compiler_params=SMALL,
     )(in_hbm(vector), in_hbm(right))
 
 
-def site_copies(left_site, right_site, left_t, right_t, left_sem, right_sem):
+def site_copies(left_site, right_site, left_t, right_t, sems):
     loads = (
-        pltpu.make_async_copy(left_site, left_t, left_sem),
-        pltpu.make_async_copy(right_site, right_t, right_sem),
+        pltpu.make_async_copy(left_site, left_t, sems.at[0]),
+        pltpu.make_async_copy(right_site, right_t, sems.at[1]),
     )
     for load in loads:
         load.start()
@@ -87,11 +89,21 @@
     return total
 
 
-def contract_and_mix(site_loads, left_t, right_t, left_ref, source, vec_s, cross_s, half_s, store):
-    blocks, rows, width = source.shape
-    half = rows // STATES
-    for r in range(blocks):
-        vec_s[:, r * width : (r + 1) * width] = source[r]
+def vector_copies(source, vec_s, sems):
+    rows = vec_s.shape[0]
+    width = source.shape[2]
+    loads = [
+        pltpu.make_async_copy(source.at[r, pl.ds(0, rows)], vec_s.at[:, pl.ds(r * width, width)], sems.at[r])
+        for r in range(source.shape[0])
+    ]
+    for load in loads:
+        load.start()
+    return loads
+
+
+def contract_and_mix(site_loads, left_t, right_t, left_ref, vec_s, cross_s, half_s, store):
+    half = vec_s.shape[0] // STATES
+    width = 2 * half
     cross_s[...] = jnp.dot(vec_s[...], left_ref[...], preferred_element_type=jnp.float32)
     for load in site_loads:
         load.wait()
@@ -114,46 +126,54 @@
 
 def own_kernel(
     left_site, right_site, left_ref, own_hbm, left_out, mixed_out, right_out,
-    left_t, right_t, piece_s, vec_s, cross_s, half_s, sems,
+    left_t, right_t, vec_s, cross_s, half_s, vec_sems, right_sems, site_sems,
 ):
-    _, rows, width = piece_s.shape
-    half = rows // STATES
-    load = pltpu.make_async_copy(own_hbm.at[:, pl.ds(0, rows)], piece_s, sems.at[0])
-    load.start()
-    passed = pltpu.make_async_copy(own_hbm.at[:, pl.ds(rows, CHANNELS * half)], right_out, sems.at[1])
-    passed.start()
-    site_loads = site_copies(left_site, right_site, left_t, right_t, sems.at[2], sems.at[3])
+    width = own_hbm.shape[2]
+    half = width // 2
+    loads = vector_copies(own_hbm, vec_s, vec_sems)
+    site_loads = site_copies(left_site, right_site, left_t, right_t, site_sems)
+    passed = [
+        pltpu.make_async_copy(
+            own_hbm.at[:, pl.ds((STATES + v) * half, half)], right_out.at[:, :, pl.ds(v * width, width)], right_sems.at[v]
+        )
+        for v in range(CHANNELS)
+    ]
+    for copy in passed:
+        copy.start()
     for k in range(left_ref.shape[0]):
         for w in range(CHANNELS):
             left_out[k * half : (k + 1) * half, w * width : (w + 1) * width] = left_ref[k, w * half : (w + 1) * half, :]
-    load.wait()
+    for load in loads:
+        load.wait()
 
     def store(v, s, x):
         mixed_out[v * half : (v + 1) * half, s * width : (s + 1) * width] = x
 
-    contract_and_mix(site_loads, left_t, right_t, left_out, piece_s, vec_s, cross_s, half_s, store)
-    passed.wait()
+    contract_and_mix(site_loads, left_t, right_t, left_out, vec_s, cross_s, half_s, store)
+    for copy in passed:
+        copy.wait()
 
 
 def own_part(sites, left, own):
-    blocks, rows, width = own.shape
-    half = rows // (STATES + CHANNELS)
+    blocks, _, width = own.shape
+    half = width // 2
     return pl.pallas_call(
         own_kernel,
         out_shape=(
             jax.ShapeDtypeStruct((left.shape[0] * half, CHANNELS * width), jnp.bfloat16),
             jax.ShapeDtypeStruct((CHANNELS * half, STATES * width), jnp.bfloat16),
-            jax.ShapeDtypeStruct((blocks, CHANNELS * half, width), jnp.bfloat16),
+            jax.ShapeDtypeStruct((blocks, half, CHANNELS * width), jnp.bfloat16),
         ),
         in_specs=[HBM, HBM, VMEM, HBM],
         out_specs=(VMEM, VMEM, VMEM),
         scratch_shapes=[
             *(pltpu.SMEM(site.shape, jnp.float32) for site in sites),
-            pltpu.VMEM((blocks, STATES * half, width), jnp.bfloat16),
             pltpu.VMEM((STATES * half, blocks * width), jnp.bfloat16),
             pltpu.VMEM((STATES * half, CHANNELS * width), jnp.float32),
             pltpu.VMEM((CHANNELS, 2, half, width), jnp.float32),
-            pltpu.SemaphoreType.DMA((4,)),
+            pltpu.SemaphoreType.DMA((blocks,)),
+            pltpu.SemaphoreType.DMA((CHANNELS,)),
+            pltpu.SemaphoreType.DMA((2,)),
         ],
         compiler_params=LARGE,
     )(*(in_hbm(site) for site in sites), left, in_hbm(own))
@@ -161,39 +181,34 @@
 
 def terms_kernel(
     order, core_ref, left_site, right_site, left_ref, mixed_ref, right_own, other_hbm, out_ref,
-    left_t, right_t, piece_s, right_other, vec_s, cross_s, half_s, right_s, mixed_s, sems,
+    left_t, right_t, right_other, vec_s, cross_s, half_s, right_s, mixed_s, vec_sems, right_sem, site_sems,
 ):
     blocks, half, _ = out_ref.shape
     width = 2 * half
     core = core_ref[0]
     own_at = pl.multiple_of(core * half, half)
     other_at = pl.multiple_of((1 - core) * half, half)
-    vectors, rights = pl.ds(0, STATES * half), pl.ds(STATES * half, CHANNELS * half)
-    loads = [
-        pltpu.make_async_copy(other_hbm.at[:, vectors], piece_s, sems.at[0]),
-        pltpu.make_async_copy(other_hbm.at[:, rights], right_other, sems.at[1]),
-    ]
-    for load in loads:
-        load.start()
-    site_loads = site_copies(left_site, right_site, left_t, right_t, sems.at[2], sems.at[3])
+    loads = vector_copies(other_hbm, vec_s, vec_sems)
+    site_loads = site_copies(left_site, right_site, left_t, right_t, site_sems)
+    right_load = pltpu.make_async_copy(other_hbm.at[:, pl.ds(STATES * half, CHANNELS * half)], right_other, right_sem)
+    right_load.start()
     mine = lax.broadcasted_iota(jnp.int32, (half, width), 1) // half == core
     for v in range(CHANNELS):
         mixed_s[pl.ds(v * width + own_at, half), :] = mixed_ref[v * half : (v + 1) * half, :]
-        for r in range(blocks):
-            right_s[r * half : (r + 1) * half, v * width : (v + 1) * width] = right_own[r, v * half : (v + 1) * half, :]
-    loads[0].wait()
+    for load in loads:
+        load.wait()
 
     def store(v, s, x):
         mixed_s[pl.ds(v * width + other_at, half), s * width : (s + 1) * width] = x
 
-    contract_and_mix(site_loads, left_t, right_t, left_ref, piece_s, vec_s, cross_s, half_s, store)
-    loads[1].wait()
+    contract_and_mix(site_loads, left_t, right_t, left_ref, vec_s, cross_s, half_s, store)
+    right_load.wait()
     for r in range(blocks):
         for v in range(CHANNELS):
-            at = (slice(r * half, (r + 1) * half), slice(v * width, (v + 1) * width))
+            own = right_own[r, :, v * width : (v + 1) * width].astype(jnp.float32)
             other = right_other[r, v * half : (v + 1) * half, :].astype(jnp.float32)
             other = jnp.concatenate([other[:, half:], other[:, :half]], 1)
-            right_s[at] = jnp.where(mine, right_s[at].astype(jnp.float32), other).astype(jnp.bfloat16)
+            right_s[r * half : (r + 1) * half, v * width : (v + 1) * width] = jnp.where(mine, own, other).astype(jnp.bfloat16)
     image = jnp.dot(right_s[...], mixed_s[...], preferred_element_type=jnp.float32)
     for r in range(blocks):
         out_ref[order[r]] = image[r * half : (r + 1) * half].astype(jnp.bfloat16)
@@ -203,8 +218,8 @@
     def step(*refs):
         terms_kernel(order, *refs)
 
-    blocks, rows, width = other.shape
-    half = rows // (STATES + CHANNELS)
+    blocks, _, width = other.shape
+    half = width // 2
     return pl.pallas_call(
         step,
         out_shape=jax.ShapeDtypeStruct((blocks, half, STATES * width), jnp.bfloat16),
@@ -212,14 +227,15 @@
         out_specs=VMEM,
         scratch_shapes=[
             *(pltpu.SMEM(site.shape, jnp.float32) for site in sites),
-            pltpu.VMEM((blocks, STATES * half, width), jnp.bfloat16),
             pltpu.VMEM((blocks, CHANNELS * half, width), jnp.bfloat16),
             pltpu.VMEM((STATES * half, blocks * width), jnp.bfloat16),
             pltpu.VMEM((STATES * half, CHANNELS * width), jnp.float32),
             pltpu.VMEM((CHANNELS, 2, half, width), jnp.float32),
             pltpu.VMEM((blocks * half, CHANNELS * width), jnp.bfloat16),
             pltpu.VMEM((CHANNELS * width, STATES * width), jnp.bfloat16),
-            pltpu.SemaphoreType.DMA((4,)),
+            pltpu.SemaphoreType.DMA((blocks,)),
+            pltpu.SemaphoreType.DMA,
+            pltpu.SemaphoreType.DMA((2,)),
         ],
         compiler_params=LARGE,
     )(core, *(in_hbm(site) for site in sites), left, mixed, right, in_hbm(other))
@@ -361,7 +377,7 @@
     left = jnp.swapaxes(left_env, 1, 2).reshape(CHANNELS * half, rows)
     left = (left.astype(jnp.float32) * SCALE).astype(jnp.float16)
 
-    own = all_to_all(pack(vector, right_env, n_row), ROW)
+    own = all_to_all(pack(vector.reshape(STATES * half, rows), right_env, n_row), ROW)
     left = lax.all_gather(left, COL, axis=0)
     own, left = lax.optimization_barrier((own, left))
     left = (left.astype(jnp.float32) * (1.0 / SCALE)).astype(jnp.bfloat16)
@@ -372,9 +388,9 @@
 
     pieces = lax.all_to_all(sent, COL, 0, 0, axis_index_groups=neighbours(n_far, n_near), tiled=True)
     pieces = all_to_all(near_sum(pieces.reshape(n_near, n_far, *pieces.shape[1:])), FAR)
-    image, sums = sums_of(pieces, vector, n_z)
-    sums = again(all_to_all(sums, Z), lax.axis_size((X, Y, C)))
-    next_vector, coefficients = last(entries, all_to_all(sums, (X, Y, C)), image, vector)
+    image, sums = sums_of(pieces, vector, lax.axis_size((X, Y, C)))
+    sums = again(all_to_all(sums, (X, Y, C)), n_z)
+    next_vector, coefficients = last(entries, all_to_all(sums, Z), image, vector)
     return jnp.swapaxes(next_vector, 1, 2), coefficients
 
 

time: 150 us -> 149 us (level)
  no operation moved by 1% of the time
where the time goes in v8:
time: 149 us; the launch traced here: 148 us
  blocking collectives  125 us (84%)
  Pallas kernels  11.4 us (8%)
  starting transfers between devices  9.82 us (7%)
    all_to_all x3, blocking collectives, all_to_all(): return lax.all_to_all(x, axes, 0, 0, tiled=True)  56.2 us
    all_gather x1, blocking collectives, body(): left = lax.all_gather(left, COL, axis=0)  44.7 us
    all_to_all x1, blocking collectives, body(): lax.all_to_all(sent, COL, 0, 0, axis_index_groups=neighbours(n_far, n_nea...  24.1 us
    all_to_all x1, starting transfers between devices, all_to_all(): return lax.all_to_all(x, axes, 0, 0, tiled=True)  7.76 us
    pallas_call x1, Pallas kernels, terms(): pl.pallas_call(step, out_shape=jax.ShapeDtypeStruct((blocks, half, STATES...  4.34 us
    pallas_call x1, Pallas kernels, own_part(): pl.pallas_call(own_kernel, out_shape=(jax.ShapeDtypeStruct((left.shape[0]...  3.32 us
  transfers between devices with their start and end apart: 2, of which 1 were waited for; matrix products, arithmetic and copies ran while one was open for 1% of the time, Pallas kernels for 2%

profile of v8, /device:TPU:1, one launch (start us, length us, event | category | flops | bytes accessed | tf_op | source)
XLA Modules:
  0.0 148.4 jit_solution(2093382243356421388)
XLA Ops:
  0.6 2.6 %shard_map.68 = bf16[16,576,128]{2,1,0:T(8,128)(2,1)} custom-call(bf16[256,128]{1,0:T(8,128)(2,1)} %bitcast.12, bf16[5,64,128]{2,1,0:T(8,128)(2,1)} %right_hbm.1), custom_call_target="tpu_custom_call" | custom-call | tf_op jit(solution)/shard_map/pallas_call | solution.py:59
  3.2 0.0 copy-start.1
  3.2 7.8 %all-to-all-start = ((bf16[16,576,128]{2,1,0:T(8,128)(2,1)}), bf16[16,576,128]{2,1,0:T(8,128)(2,1)}, u32[]{:S(2)}, u32[]{:S(2)}) async-start(bf16[16,576,128]{2,1,0:T(8,128)(2,1)} %shard_map.68), calls=%async_computation | async-start | bytes 4718592 | tf_op jit(solution)/shard_map/all_to_all | solution.py:361
  11.0 0.0 copy-done.1
  11.0 44.7 %all-gather.1 = f16[32,320,128]{2,1,0:T(8,128)(2,1)S(1)} all-gather(f16[1,320,128]{2,1,0:T(8,128)(2,1)S(1)} %bitcast.15), channel_id=1, replica_groups=mesh['row_0'=4,'row_1'=4,'far'=4,'near'=4,'core'=2] {'far','near','core'}, dimensions={0}, use_global_device_ids=true | all-gather | bytes 2703360 | tf_op jit(solution)/shard_map/all_gather | solution.py:381
  55.8 0.0 all-to-all-done.own_hbm
  55.8 2.1 %collective-permute-start = (bf16[16,576,128]{2,1,0:T(8,128)(2,1)}, bf16[16,576,128]{2,1,0:T(8,128)(2,1)}, u32[]{:S(2)}, u32[]{:S(2)}) collective-permute-start(bf16[16,576,128]{2,1,0:T(8,128)(2,1)} %all-to-all-done.own_hbm), channel_id=1, source_target_pairs={{0,1},{1,0},{2,3},{3,2},{4,5},{5,4},{6,7},{7,6},{8,9},{9,8},{10,11... | collective-permute-start | bytes 7077896 | tf_op jit(solution)/shard_map/ppermute | solution.py:365
  57.8 0.8 multiply_convert_fusion.left_ref
  58.6 3.3 %shard_map.69 = (bf16[2048,640]{1,0:T(8,128)(2,1)S(1)}, bf16[320,512]{1,0:T(8,128)(2,1)S(1)}, bf16[16,64,640]{2,1,0:T(8,128)(2,1)S(1)}) custom-call(f32[5,2,2,5]{3,2,1,0:T(2,128)} %bitcast.16, f32[5,2,2,5]{3,2,1,0:T(2,128)} %bitcast.18, bf16[32,320,128]{2,1,0:T(8,128)(2,1)S(1)} %multiply_convert_fusion.left_ref, bf16[16,576,128]{2,1,0:T(8,128)(2,1)} %all-to-all-done.own_hbm), custom_call_target="tpu_custom_call" | custom-call | tf_op jit(solution)/shard_map/pallas_call | solution.py:160
  62.0 0.5 collective-permute-done.refs_6_
  62.5 4.3 %shard_map.70 = bf16[16,64,512]{2,1,0:T(8,128)(2,1)S(1)} custom-call(s32[1]{0:T(128)} %bitcast.refs_0_, f32[5,2,2,5]{3,2,1,0:T(2,128)} %bitcast.17, f32[5,2,2,5]{3,2,1,0:T(2,128)} %bitcast.19, bf16[2048,640]{1,0:T(8,128)(2,1)S(1)} %get-tuple-element.13.refs_3_, bf16[320,512]{1,0:T(8,128)(2,1)S(1)} %get-tuple-element.14.refs_4_, ...), custom_call_target="tpu_custom_call" | custom-call | tf_op jit(solution)/shard_map/pallas_call | solution.py:223
  66.9 0.0 copy-start
  66.9 24.1 %all_to_all.25 = bf16[16,64,512]{2,1,0:T(8,128)(2,1)S(1)} all-to-all(bf16[16,64,512]{2,1,0:T(8,128)(2,1)S(1)} %shard_map.70), channel_id=1, replica_groups={{0,2,4,6},{8,10,12,14},{16,18,20,22},{24,26,28,30},{9,11,5,7},{17,19,13..., dimensions={0} | all-to-all | bytes 2097152 | tf_op jit(solution)/shard_map/all_to_all | solution.py:389
  91.0 0.1 shard_map.71
  91.1 21.6 %all_to_all.26.pieces_ref = bf16[4,64,512]{2,1,0:T(8,128)(2,1)S(1)} all-to-all(bf16[4,64,512]{2,1,0:T(8,128)(2,1)S(1)} %shard_map.71), channel_id=1, replica_groups=mesh['row_0'=4,'row_1'=4,'far'=4,'near'=4,'core'=2] {'far'}, dimensions={0} | all-to-all | bytes 524288 | tf_op jit(solution)/shard_map/all_to_all | solution.py:361
  112.7 0.0 copy-done
  112.7 0.2 shard_map.72
  112.9 17.8 %all_to_all.27.pieces_ref = f32[32,1,128]{2,1,0:T(1,128)S(1)} all-to-all(f32[32,1,128]{2,1,0:T(1,128)S(1)} %get-tuple-element.16), channel_id=1, replica_groups=mesh['row_0'=4,'row_1'=4,'far'=4,'near'=4,'core'=2] {'row_0','row_1','co..., dimensions={0} | all-to-all | bytes 32768 | tf_op jit(solution)/shard_map/all_to_all | solution.py:361
  130.7 16.9 %all_to_all.28.refs_0_ = f32[16,1,128]{2,1,0:T(1,128)S(1)} all-to-all(f32[16,1,128]{2,1,0:T(1,128)S(1)} %shard_map.73), channel_id=1, replica_groups=mesh['row_0'=4,'row_1'=4,'far'=4,'near'=4,'core'=2] {'far','near'}, dimensions={0} | all-to-all | bytes 16384 | tf_op jit(solution)/shard_map/all_to_all | solution.py:361
  147.6 0.8 shard_map.74
  (2 shorter events, 0.1 us)
Async XLA Ops:
  3.2 7.8 %copy-start.1 = (bf16[5,128,64]{1,2,0:T(8,128)(2,1)S(1)}, bf16[5,128,64]{1,2,0:T(8,128)(2,1)}, u32[]{:S(2)}) copy-start(bf16[5,128,64]{1,2,0:T(8,128)(2,1)} %param.6) | copy-start | bytes 245764
  3.2 52.5 %all-to-all-start = ((bf16[16,576,128]{2,1,0:T(8,128)(2,1)}), bf16[16,576,128]{2,1,0:T(8,128)(2,1)}, u32[]{:S(2)}, u32[]{:S(2)}) async-start(bf16[16,576,128]{2,1,0:T(8,128)(2,1)} %shard_map.68), calls=%async_computation | async-start | bytes 4718592 | tf_op jit(solution)/shard_map/all_to_all | solution.py:361
  55.8 6.8 %collective-permute-start = (bf16[16,576,128]{2,1,0:T(8,128)(2,1)}, bf16[16,576,128]{2,1,0:T(8,128)(2,1)}, u32[]{:S(2)}, u32[]{:S(2)}) collective-permute-start(bf16[16,576,128]{2,1,0:T(8,128)(2,1)} %all-to-all-done.own_hbm), channel_id=1, source_target_pairs={{0,1},{1,0},{2,3},{3,2},{4,5},{5,4},{6,7},{7,6},{8,9},{9,8},{10,11... | collective-permute-start | bytes 7077896 | tf_op jit(solution)/shard_map/ppermute | solution.py:365
  66.9 45.8 %copy-start = (bf16[4,128,64]{1,2,0:T(8,128)(2,1)S(1)}, bf16[4,128,64]{1,2,0:T(8,128)(2,1)}, u32[]{:S(2)}) copy-start(bf16[4,128,64]{1,2,0:T(8,128)(2,1)} %param.5) | copy-start | bytes 196612

commit v9 on v8

--- a/solution.py
+++ b/solution.py
@@ -101,10 +101,18 @@
     return loads
 
 
-def contract_and_mix(site_loads, left_t, right_t, left_ref, vec_s, cross_s, half_s, store):
+def contract_and_mix(loads, place_left, site_loads, left_t, right_t, left_ref, vec_s, cross_s, half_s, store):
     half = vec_s.shape[0] // STATES
     width = 2 * half
-    cross_s[...] = jnp.dot(vec_s[...], left_ref[...], preferred_element_type=jnp.float32)
+    parts = 2
+    depth = vec_s.shape[1] // parts
+    for g in range(parts):
+        place_left(g, parts)
+        for load in loads[g * len(loads) // parts : (g + 1) * len(loads) // parts]:
+            load.wait()
+        at = slice(g * depth, (g + 1) * depth)
+        part = jnp.dot(vec_s[:, at], left_ref[at, :], preferred_element_type=jnp.float32)
+        cross_s[...] = part if g == 0 else cross_s[...] + part
     for load in site_loads:
         load.wait()
     for s1 in range(2):
@@ -140,16 +148,17 @@
     ]
     for copy in passed:
         copy.start()
-    for k in range(left_ref.shape[0]):
-        for w in range(CHANNELS):
-            left_out[k * half : (k + 1) * half, w * width : (w + 1) * width] = left_ref[k, w * half : (w + 1) * half, :]
-    for load in loads:
-        load.wait()
+
+    def place_left(g, parts):
+        count = left_ref.shape[0] // parts
+        for k in range(g * count, (g + 1) * count):
+            for w in range(CHANNELS):
+                left_out[k * half : (k + 1) * half, w * width : (w + 1) * width] = left_ref[k, w * half : (w + 1) * half, :]
 
     def store(v, s, x):
         mixed_out[v * half : (v + 1) * half, s * width : (s + 1) * width] = x
 
-    contract_and_mix(site_loads, left_t, right_t, left_out, vec_s, cross_s, half_s, store)
+    contract_and_mix(loads, place_left, site_loads, left_t, right_t, left_out, vec_s, cross_s, half_s, store)
     for copy in passed:
         copy.wait()
 
@@ -195,13 +204,11 @@
     mine = lax.broadcasted_iota(jnp.int32, (half, width), 1) // half == core
     for v in range(CHANNELS):
         mixed_s[pl.ds(v * width + own_at, half), :] = mixed_ref[v * half : (v + 1) * half, :]
-    for load in loads:
-        load.wait()
 
     def store(v, s, x):
         mixed_s[pl.ds(v * width + other_at, half), s * width : (s + 1) * width] = x
 
-    contract_and_mix(site_loads, left_t, right_t, left_ref, vec_s, cross_s, half_s, store)
+    contract_and_mix(loads, lambda g, parts: None, site_loads, left_t, right_t, left_ref, vec_s, cross_s, half_s, store)
     right_load.wait()
     for r in range(blocks):
         for v in range(CHANNELS):

time: 149 us -> 149 us (level)
  no operation moved by 1% of the time
where the time goes in v9:
time: 149 us; the launch traced here: 148 us
  blocking collectives  125 us (84%)
  Pallas kernels  11.6 us (8%)
  starting transfers between devices  9.82 us (7%)
    all_to_all x3, blocking collectives, all_to_all(): return lax.all_to_all(x, axes, 0, 0, tiled=True)  56.2 us
    all_gather x1, blocking collectives, body(): left = lax.all_gather(left, COL, axis=0)  44.7 us
    all_to_all x1, blocking collectives, body(): lax.all_to_all(sent, COL, 0, 0, axis_index_groups=neighbours(n_far, n_nea...  24.1 us
    all_to_all x1, starting transfers between devices, all_to_all(): return lax.all_to_all(x, axes, 0, 0, tiled=True)  7.76 us
    pallas_call x1, Pallas kernels, terms(): pl.pallas_call(step, out_shape=jax.ShapeDtypeStruct((blocks, half, STATES...  4.34 us
    pallas_call x1, Pallas kernels, own_part(): pl.pallas_call(own_kernel, out_shape=(jax.ShapeDtypeStruct((left.shape[0]...  3.54 us
  transfers between devices with their start and end apart: 2, of which 1 were waited for; matrix products, arithmetic and copies ran while one was open for 1% of the time, Pallas kernels for 2%

profile of v9, /device:TPU:1, one launch (start us, length us, event | category | flops | bytes accessed | tf_op | source)
XLA Modules:
  0.0 148.4 jit_solution(13782078569565117214)
XLA Ops:
  0.6 2.6 %shard_map.68 = bf16[16,576,128]{2,1,0:T(8,128)(2,1)} custom-call(bf16[256,128]{1,0:T(8,128)(2,1)} %bitcast.12, bf16[5,64,128]{2,1,0:T(8,128)(2,1)} %right_hbm.1), custom_call_target="tpu_custom_call" | custom-call | tf_op jit(solution)/shard_map/pallas_call | solution.py:59
  3.2 0.0 copy-start.1
  3.2 7.8 %all-to-all-start = ((bf16[16,576,128]{2,1,0:T(8,128)(2,1)}), bf16[16,576,128]{2,1,0:T(8,128)(2,1)}, u32[]{:S(2)}, u32[]{:S(2)}) async-start(bf16[16,576,128]{2,1,0:T(8,128)(2,1)} %shard_map.68), calls=%async_computation | async-start | bytes 4718592 | tf_op jit(solution)/shard_map/all_to_all | solution.py:368
  11.0 0.0 copy-done.1
  11.0 44.7 %all-gather.1 = f16[32,320,128]{2,1,0:T(8,128)(2,1)S(1)} all-gather(f16[1,320,128]{2,1,0:T(8,128)(2,1)S(1)} %bitcast.15), channel_id=1, replica_groups=mesh['row_0'=4,'row_1'=4,'far'=4,'near'=4,'core'=2] {'far','near','core'}, dimensions={0}, use_global_device_ids=true | all-gather | bytes 2703360 | tf_op jit(solution)/shard_map/all_gather | solution.py:388
  55.8 0.0 all-to-all-done.own_hbm
  55.8 2.1 %collective-permute-start = (bf16[16,576,128]{2,1,0:T(8,128)(2,1)}, bf16[16,576,128]{2,1,0:T(8,128)(2,1)}, u32[]{:S(2)}, u32[]{:S(2)}) collective-permute-start(bf16[16,576,128]{2,1,0:T(8,128)(2,1)} %all-to-all-done.own_hbm), channel_id=1, source_target_pairs={{0,1},{1,0},{2,3},{3,2},{4,5},{5,4},{6,7},{7,6},{8,9},{9,8},{10,11... | collective-permute-start | bytes 7077896 | tf_op jit(solution)/shard_map/ppermute | solution.py:372
  57.8 0.8 multiply_convert_fusion.left_ref
  58.6 3.5 %shard_map.69 = (bf16[2048,640]{1,0:T(8,128)(2,1)S(1)}, bf16[320,512]{1,0:T(8,128)(2,1)S(1)}, bf16[16,64,640]{2,1,0:T(8,128)(2,1)S(1)}) custom-call(f32[5,2,2,5]{3,2,1,0:T(2,128)} %bitcast.16, f32[5,2,2,5]{3,2,1,0:T(2,128)} %bitcast.18, bf16[32,320,128]{2,1,0:T(8,128)(2,1)S(1)} %multiply_convert_fusion.left_ref, bf16[16,576,128]{2,1,0:T(8,128)(2,1)} %all-to-all-done.own_hbm), custom_call_target="tpu_custom_call" | custom-call | tf_op jit(solution)/shard_map/pallas_call | solution.py:169
  62.2 0.3 collective-permute-done.refs_6_
  62.5 4.3 %shard_map.70 = bf16[16,64,512]{2,1,0:T(8,128)(2,1)S(1)} custom-call(s32[1]{0:T(128)} %bitcast.refs_0_, f32[5,2,2,5]{3,2,1,0:T(2,128)} %bitcast.17, f32[5,2,2,5]{3,2,1,0:T(2,128)} %bitcast.19, bf16[2048,640]{1,0:T(8,128)(2,1)S(1)} %get-tuple-element.13.refs_3_, bf16[320,512]{1,0:T(8,128)(2,1)S(1)} %get-tuple-element.14.refs_4_, ...), custom_call_target="tpu_custom_call" | custom-call | tf_op jit(solution)/shard_map/pallas_call | solution.py:230
  66.9 0.0 copy-start
  66.9 24.1 %all_to_all.25 = bf16[16,64,512]{2,1,0:T(8,128)(2,1)S(1)} all-to-all(bf16[16,64,512]{2,1,0:T(8,128)(2,1)S(1)} %shard_map.70), channel_id=1, replica_groups={{0,2,4,6},{8,10,12,14},{16,18,20,22},{24,26,28,30},{9,11,5,7},{17,19,13..., dimensions={0} | all-to-all | bytes 2097152 | tf_op jit(solution)/shard_map/all_to_all | solution.py:396
  91.0 0.1 shard_map.71
  91.1 21.6 %all_to_all.26.pieces_ref = bf16[4,64,512]{2,1,0:T(8,128)(2,1)S(1)} all-to-all(bf16[4,64,512]{2,1,0:T(8,128)(2,1)S(1)} %shard_map.71), channel_id=1, replica_groups=mesh['row_0'=4,'row_1'=4,'far'=4,'near'=4,'core'=2] {'far'}, dimensions={0} | all-to-all | bytes 524288 | tf_op jit(solution)/shard_map/all_to_all | solution.py:368
  112.7 0.0 copy-done
  112.7 0.2 shard_map.72
  112.9 17.8 %all_to_all.27.pieces_ref = f32[32,1,128]{2,1,0:T(1,128)S(1)} all-to-all(f32[32,1,128]{2,1,0:T(1,128)S(1)} %get-tuple-element.16), channel_id=1, replica_groups=mesh['row_0'=4,'row_1'=4,'far'=4,'near'=4,'core'=2] {'row_0','row_1','co..., dimensions={0} | all-to-all | bytes 32768 | tf_op jit(solution)/shard_map/all_to_all | solution.py:368
  130.7 16.9 %all_to_all.28.refs_0_ = f32[16,1,128]{2,1,0:T(1,128)S(1)} all-to-all(f32[16,1,128]{2,1,0:T(1,128)S(1)} %shard_map.73), channel_id=1, replica_groups=mesh['row_0'=4,'row_1'=4,'far'=4,'near'=4,'core'=2] {'far','near'}, dimensions={0} | all-to-all | bytes 16384 | tf_op jit(solution)/shard_map/all_to_all | solution.py:368
  147.6 0.8 shard_map.74
  (2 shorter events, 0.1 us)
Async XLA Ops:
  3.2 7.8 %copy-start.1 = (bf16[5,128,64]{1,2,0:T(8,128)(2,1)S(1)}, bf16[5,128,64]{1,2,0:T(8,128)(2,1)}, u32[]{:S(2)}) copy-start(bf16[5,128,64]{1,2,0:T(8,128)(2,1)} %param.6) | copy-start | bytes 245764
  3.2 52.5 %all-to-all-start = ((bf16[16,576,128]{2,1,0:T(8,128)(2,1)}), bf16[16,576,128]{2,1,0:T(8,128)(2,1)}, u32[]{:S(2)}, u32[]{:S(2)}) async-start(bf16[16,576,128]{2,1,0:T(8,128)(2,1)} %shard_map.68), calls=%async_computation | async-start | bytes 4718592 | tf_op jit(solution)/shard_map/all_to_all | solution.py:368
  55.8 6.8 %collective-permute-start = (bf16[16,576,128]{2,1,0:T(8,128)(2,1)}, bf16[16,576,128]{2,1,0:T(8,128)(2,1)}, u32[]{:S(2)}, u32[]{:S(2)}) collective-permute-start(bf16[16,576,128]{2,1,0:T(8,128)(2,1)} %all-to-all-done.own_hbm), channel_id=1, source_target_pairs={{0,1},{1,0},{2,3},{3,2},{4,5},{5,4},{6,7},{7,6},{8,9},{9,8},{10,11... | collective-permute-start | bytes 7077896 | tf_op jit(solution)/shard_map/ppermute | solution.py:372
  66.9 45.9 %copy-start = (bf16[4,128,64]{1,2,0:T(8,128)(2,1)S(1)}, bf16[4,128,64]{1,2,0:T(8,128)(2,1)}, u32[]{:S(2)}) copy-start(bf16[4,128,64]{1,2,0:T(8,128)(2,1)} %param.5) | copy-start | bytes 196612

commit v10 on v8

--- a/solution.py
+++ b/solution.py
@@ -125,7 +125,7 @@
 
 
 def own_kernel(
-    left_site, right_site, left_ref, own_hbm, left_out, mixed_out, right_out,
+    left_site, right_site, left_ref, own_hbm, mixed_out, right_out,
     left_t, right_t, vec_s, cross_s, half_s, vec_sems, right_sems, site_sems,
 ):
     width = own_hbm.shape[2]
@@ -140,16 +140,13 @@
     ]
     for copy in passed:
         copy.start()
-    for k in range(left_ref.shape[0]):
-        for w in range(CHANNELS):
-            left_out[k * half : (k + 1) * half, w * width : (w + 1) * width] = left_ref[k, w * half : (w + 1) * half, :]
     for load in loads:
         load.wait()
 
     def store(v, s, x):
         mixed_out[v * half : (v + 1) * half, s * width : (s + 1) * width] = x
 
-    contract_and_mix(site_loads, left_t, right_t, left_out, vec_s, cross_s, half_s, store)
+    contract_and_mix(site_loads, left_t, right_t, left_ref, vec_s, cross_s, half_s, store)
     for copy in passed:
         copy.wait()
 
@@ -160,12 +157,11 @@
     return pl.pallas_call(
         own_kernel,
         out_shape=(
-            jax.ShapeDtypeStruct((left.shape[0] * half, CHANNELS * width), jnp.bfloat16),
             jax.ShapeDtypeStruct((CHANNELS * half, STATES * width), jnp.bfloat16),
             jax.ShapeDtypeStruct((blocks, half, CHANNELS * width), jnp.bfloat16),
         ),
         in_specs=[HBM, HBM, VMEM, HBM],
-        out_specs=(VMEM, VMEM, VMEM),
+        out_specs=(VMEM, VMEM),
         scratch_shapes=[
             *(pltpu.SMEM(site.shape, jnp.float32) for site in sites),
             pltpu.VMEM((STATES * half, blocks * width), jnp.bfloat16),
@@ -374,16 +370,16 @@
     core = lax.axis_index(C).astype(jnp.int32).reshape(1)
     sites = tuple(jnp.transpose(tensor, (0, 2, 3, 1)) for tensor in (left_tensor, right_tensor))
     vector = jnp.swapaxes(start_vector, 1, 2)
-    left = jnp.swapaxes(left_env, 1, 2).reshape(CHANNELS * half, rows)
+    left = jnp.transpose(left_env, (2, 0, 1)).reshape(half, CHANNELS * rows)
     left = (left.astype(jnp.float32) * SCALE).astype(jnp.float16)
 
     own = all_to_all(pack(vector.reshape(STATES * half, rows), right_env, n_row), ROW)
-    left = lax.all_gather(left, COL, axis=0)
+    left = lax.all_gather(left, COL, axis=0, tiled=True)
     own, left = lax.optimization_barrier((own, left))
     left = (left.astype(jnp.float32) * (1.0 / SCALE)).astype(jnp.bfloat16)
     order = [n_far * (z % n_near) + z // n_near for z in range(n_z)]
     other = other_core(own)
-    left, mixed, right = own_part(sites, left, own)
+    mixed, right = own_part(sites, left, own)
     sent = terms(order, core, sites, left, mixed, right, other)
 
     pieces = lax.all_to_all(sent, COL, 0, 0, axis_index_groups=neighbours(n_far, n_near), tiled=True)

time: 149 us -> 149 us (level)
  transfers between devices with their start and end apart: 2 -> 2, of which waited for: 1 -> 1; matrix products, arithmetic and copies ran while one was open for 1% -> 0% of each run, Pallas kernels for 2% -> 2%
where the time goes in v10:
time: 149 us; the launch traced here: 148 us
  blocking collectives  125 us (84%)
  Pallas kernels  11.4 us (8%)
  starting transfers between devices  9.82 us (7%)
    all_to_all x3, blocking collectives, all_to_all(): return lax.all_to_all(x, axes, 0, 0, tiled=True)  56.2 us
    all_gather x1, blocking collectives, body(): left = lax.all_gather(left, COL, axis=0, tiled=True)  44.7 us
    all_to_all x1, blocking collectives, body(): lax.all_to_all(sent, COL, 0, 0, axis_index_groups=neighbours(n_far, n_nea...  24.1 us
    all_to_all x1, starting transfers between devices, all_to_all(): return lax.all_to_all(x, axes, 0, 0, tiled=True)  7.76 us
    pallas_call x1, Pallas kernels, terms(): pl.pallas_call(step, out_shape=jax.ShapeDtypeStruct((blocks, half, STATES...  4.39 us
    pallas_call x1, Pallas kernels, own_part(): pl.pallas_call(own_kernel, out_shape=(jax.ShapeDtypeStruct((CHANNELS * ha...  3.35 us
  transfers between devices with their start and end apart: 2, of which 1 were waited for; matrix products, arithmetic and copies ran while one was open for 0% of the time, Pallas kernels for 2%

profile of v10, /device:TPU:1, one launch (start us, length us, event | category | flops | bytes accessed | tf_op | source)
XLA Modules:
  0.0 148.4 jit_solution(15250286752588793238)
XLA Ops:
  0.6 2.6 %shard_map.68 = bf16[16,576,128]{2,1,0:T(8,128)(2,1)} custom-call(bf16[256,128]{1,0:T(8,128)(2,1)} %bitcast.15, bf16[5,64,128]{2,1,0:T(8,128)(2,1)} %right_hbm.1), custom_call_target="tpu_custom_call" | custom-call | tf_op jit(solution)/shard_map/pallas_call | solution.py:59
  3.2 0.0 copy-start.1
  3.2 7.8 %all-to-all-start = ((bf16[16,576,128]{2,1,0:T(8,128)(2,1)}), bf16[16,576,128]{2,1,0:T(8,128)(2,1)}, u32[]{:S(2)}, u32[]{:S(2)}) async-start(bf16[16,576,128]{2,1,0:T(8,128)(2,1)} %shard_map.68), calls=%async_computation | async-start | bytes 4718592 | tf_op jit(solution)/shard_map/all_to_all | solution.py:357
  11.0 0.0 copy-done.1
  11.0 44.7 %all-gather.1 = f16[2048,640]{1,0:T(8,128)(2,1)S(1)} all-gather(f16[64,640]{1,0:T(8,128)(2,1)S(1)} %copy_bitcast_fusion), channel_id=1, replica_groups=mesh['row_0'=4,'row_1'=4,'far'=4,'near'=4,'core'=2] {'far','near','core'}, dimensions={0}, use_global_device_ids=true | all-gather | bytes 2703360 | tf_op jit(solution)/shard_map/all_gather | solution.py:377
  55.8 0.0 all-to-all-done.own_hbm
  55.8 2.1 %collective-permute-start = (bf16[16,576,128]{2,1,0:T(8,128)(2,1)}, bf16[16,576,128]{2,1,0:T(8,128)(2,1)}, u32[]{:S(2)}, u32[]{:S(2)}) collective-permute-start(bf16[16,576,128]{2,1,0:T(8,128)(2,1)} %all-to-all-done.own_hbm), channel_id=1, source_target_pairs={{0,1},{1,0},{2,3},{3,2},{4,5},{5,4},{6,7},{7,6},{8,9},{9,8},{10,11... | collective-permute-start | bytes 7077896 | tf_op jit(solution)/shard_map/ppermute | solution.py:361
  57.8 0.6 multiply_convert_fusion.left_ref.refs_3_
  58.4 3.3 %shard_map.69 = (bf16[320,512]{1,0:T(8,128)(2,1)S(1)}, bf16[16,64,640]{2,1,0:T(8,128)(2,1)S(1)}) custom-call(f32[5,2,2,5]{3,2,1,0:T(2,128)} %bitcast.18, f32[5,2,2,5]{3,2,1,0:T(2,128)} %bitcast.20, bf16[2048,640]{1,0:T(8,128)(2,1)S(1)} %multiply_convert_fusion.left_ref.refs_3_, bf16[16,576,128]{2,1,0:T(8,128)(2,1)} %all-to-all-done.own_hbm), custom_call_target="tpu_custom_call" | custom-call | tf_op jit(solution)/shard_map/pallas_call | solution.py:157
  61.7 0.8 collective-permute-done.refs_6_
  62.5 4.4 %shard_map.70 = bf16[16,64,512]{2,1,0:T(8,128)(2,1)S(1)} custom-call(s32[1]{0:T(128)} %bitcast.refs_0_, f32[5,2,2,5]{3,2,1,0:T(2,128)} %bitcast.19, f32[5,2,2,5]{3,2,1,0:T(2,128)} %bitcast.21, bf16[2048,640]{1,0:T(8,128)(2,1)S(1)} %multiply_convert_fusion.left_ref.refs_3_, bf16[320,512]{1,0:T(8,128)(2,1)S(1)} %get-tuple-element.12.refs_4_, ...), custom_call_target="tpu_custom_call" | custom-call | tf_op jit(solution)/shard_map/pallas_call | solution.py:219
  66.9 0.0 copy-start
  66.9 24.1 %all_to_all.25 = bf16[16,64,512]{2,1,0:T(8,128)(2,1)S(1)} all-to-all(bf16[16,64,512]{2,1,0:T(8,128)(2,1)S(1)} %shard_map.70), channel_id=1, replica_groups={{0,2,4,6},{8,10,12,14},{16,18,20,22},{24,26,28,30},{9,11,5,7},{17,19,13..., dimensions={0} | all-to-all | bytes 2097152 | tf_op jit(solution)/shard_map/all_to_all | solution.py:385
  91.1 0.1 shard_map.71
  91.2 21.6 %all_to_all.26.pieces_ref = bf16[4,64,512]{2,1,0:T(8,128)(2,1)S(1)} all-to-all(bf16[4,64,512]{2,1,0:T(8,128)(2,1)S(1)} %shard_map.71), channel_id=1, replica_groups=mesh['row_0'=4,'row_1'=4,'far'=4,'near'=4,'core'=2] {'far'}, dimensions={0} | all-to-all | bytes 524288 | tf_op jit(solution)/shard_map/all_to_all | solution.py:357
  112.8 0.0 copy-done
  112.8 0.2 shard_map.72
  113.0 17.7 %all_to_all.27.pieces_ref = f32[32,1,128]{2,1,0:T(1,128)S(1)} all-to-all(f32[32,1,128]{2,1,0:T(1,128)S(1)} %get-tuple-element.14), channel_id=1, replica_groups=mesh['row_0'=4,'row_1'=4,'far'=4,'near'=4,'core'=2] {'row_0','row_1','co..., dimensions={0} | all-to-all | bytes 32768 | tf_op jit(solution)/shard_map/all_to_all | solution.py:357
  130.8 16.9 %all_to_all.28.refs_0_ = f32[16,1,128]{2,1,0:T(1,128)S(1)} all-to-all(f32[16,1,128]{2,1,0:T(1,128)S(1)} %shard_map.73), channel_id=1, replica_groups=mesh['row_0'=4,'row_1'=4,'far'=4,'near'=4,'core'=2] {'far','near'}, dimensions={0} | all-to-all | bytes 16384 | tf_op jit(solution)/shard_map/all_to_all | solution.py:357
  147.6 0.8 shard_map.74
  (2 shorter events, 0.1 us)
Async XLA Ops:
  3.2 7.8 %copy-start.1 = (bf16[5,128,64]{1,2,0:T(8,128)(2,1)S(1)}, bf16[5,128,64]{1,2,0:T(8,128)(2,1)}, u32[]{:S(2)}) copy-start(bf16[5,128,64]{1,2,0:T(8,128)(2,1)} %param.6) | copy-start | bytes 245764
  3.2 52.5 %all-to-all-start = ((bf16[16,576,128]{2,1,0:T(8,128)(2,1)}), bf16[16,576,128]{2,1,0:T(8,128)(2,1)}, u32[]{:S(2)}, u32[]{:S(2)}) async-start(bf16[16,576,128]{2,1,0:T(8,128)(2,1)} %shard_map.68), calls=%async_computation | async-start | bytes 4718592 | tf_op jit(solution)/shard_map/all_to_all | solution.py:357
  55.8 6.8 %collective-permute-start = (bf16[16,576,128]{2,1,0:T(8,128)(2,1)}, bf16[16,576,128]{2,1,0:T(8,128)(2,1)}, u32[]{:S(2)}, u32[]{:S(2)}) collective-permute-start(bf16[16,576,128]{2,1,0:T(8,128)(2,1)} %all-to-all-done.own_hbm), channel_id=1, source_target_pairs={{0,1},{1,0},{2,3},{3,2},{4,5},{5,4},{6,7},{7,6},{8,9},{9,8},{10,11... | collective-permute-start | bytes 7077896 | tf_op jit(solution)/shard_map/ppermute | solution.py:361
  66.9 45.9 %copy-start = (bf16[4,128,64]{1,2,0:T(8,128)(2,1)S(1)}, bf16[4,128,64]{1,2,0:T(8,128)(2,1)}, u32[]{:S(2)}) copy-start(bf16[4,128,64]{1,2,0:T(8,128)(2,1)} %param.5) | copy-start | bytes 196612

commit v11 on v10

--- a/solution.py
+++ b/solution.py
@@ -138,10 +138,10 @@
         )
         for v in range(CHANNELS)
     ]
+    for load in loads:
+        load.wait()
     for copy in passed:
         copy.start()
-    for load in loads:
-        load.wait()
 
     def store(v, s, x):
         mixed_out[v * half : (v + 1) * half, s * width : (s + 1) * width] = x
@@ -187,12 +187,12 @@
     loads = vector_copies(other_hbm, vec_s, vec_sems)
     site_loads = site_copies(left_site, right_site, left_t, right_t, site_sems)
     right_load = pltpu.make_async_copy(other_hbm.at[:, pl.ds(STATES * half, CHANNELS * half)], right_other, right_sem)
-    right_load.start()
     mine = lax.broadcasted_iota(jnp.int32, (half, width), 1) // half == core
     for v in range(CHANNELS):
         mixed_s[pl.ds(v * width + own_at, half), :] = mixed_ref[v * half : (v + 1) * half, :]
     for load in loads:
         load.wait()
+    right_load.start()
 
     def store(v, s, x):
         mixed_s[pl.ds(v * width + other_at, half), s * width : (s + 1) * width] = x

time: 149 us -> 149 us (level)
  no operation moved by 1% of the time
where the time goes in v11:
time: 149 us
  blocking collectives  125 us (84%)
  Pallas kernels  11.6 us (8%)
  starting transfers between devices  9.82 us (7%)
    all_to_all x3, blocking collectives, all_to_all(): return lax.all_to_all(x, axes, 0, 0, tiled=True)  56.2 us
    all_gather x1, blocking collectives, body(): left = lax.all_gather(left, COL, axis=0, tiled=True)  44.7 us
    all_to_all x1, blocking collectives, body(): lax.all_to_all(sent, COL, 0, 0, axis_index_groups=neighbours(n_far, n_nea...  24.1 us
    all_to_all x1, starting transfers between devices, all_to_all(): return lax.all_to_all(x, axes, 0, 0, tiled=True)  7.76 us
    pallas_call x1, Pallas kernels, terms(): pl.pallas_call(step, out_shape=jax.ShapeDtypeStruct((blocks, half, STATES...  4.56 us
    pallas_call x1, Pallas kernels, own_part(): pl.pallas_call(own_kernel, out_shape=(jax.ShapeDtypeStruct((CHANNELS * ha...  3.35 us
  transfers between devices with their start and end apart: 2, of which 1 were waited for; matrix products, arithmetic and copies ran while one was open for 0% of the time, Pallas kernels for 2%

profile of v11, /device:TPU:1, one launch (start us, length us, event | category | flops | bytes accessed | tf_op | source)
XLA Modules:
  0.0 148.6 jit_solution(1569653684978272335)
XLA Ops:
  0.6 2.6 %shard_map.68 = bf16[16,576,128]{2,1,0:T(8,128)(2,1)} custom-call(bf16[256,128]{1,0:T(8,128)(2,1)} %bitcast.15, bf16[5,64,128]{2,1,0:T(8,128)(2,1)} %right_hbm.1), custom_call_target="tpu_custom_call" | custom-call | tf_op jit(solution)/shard_map/pallas_call | solution.py:59
  3.2 0.0 copy-start.1
  3.2 7.8 %all-to-all-start = ((bf16[16,576,128]{2,1,0:T(8,128)(2,1)}), bf16[16,576,128]{2,1,0:T(8,128)(2,1)}, u32[]{:S(2)}, u32[]{:S(2)}) async-start(bf16[16,576,128]{2,1,0:T(8,128)(2,1)} %shard_map.68), calls=%async_computation | async-start | bytes 4718592 | tf_op jit(solution)/shard_map/all_to_all | solution.py:357
  11.0 0.0 copy-done.1
  11.0 44.7 %all-gather.1 = f16[2048,640]{1,0:T(8,128)(2,1)S(1)} all-gather(f16[64,640]{1,0:T(8,128)(2,1)S(1)} %copy_bitcast_fusion), channel_id=1, replica_groups=mesh['row_0'=4,'row_1'=4,'far'=4,'near'=4,'core'=2] {'far','near','core'}, dimensions={0}, use_global_device_ids=true | all-gather | bytes 2703360 | tf_op jit(solution)/shard_map/all_gather | solution.py:377
  55.8 0.0 all-to-all-done.own_hbm
  55.8 2.1 %collective-permute-start = (bf16[16,576,128]{2,1,0:T(8,128)(2,1)}, bf16[16,576,128]{2,1,0:T(8,128)(2,1)}, u32[]{:S(2)}, u32[]{:S(2)}) collective-permute-start(bf16[16,576,128]{2,1,0:T(8,128)(2,1)} %all-to-all-done.own_hbm), channel_id=1, source_target_pairs={{0,1},{1,0},{2,3},{3,2},{4,5},{5,4},{6,7},{7,6},{8,9},{9,8},{10,11... | collective-permute-start | bytes 7077896 | tf_op jit(solution)/shard_map/ppermute | solution.py:361
  57.8 0.6 multiply_convert_fusion.left_ref.refs_3_
  58.4 3.4 %shard_map.69 = (bf16[320,512]{1,0:T(8,128)(2,1)S(1)}, bf16[16,64,640]{2,1,0:T(8,128)(2,1)S(1)}) custom-call(f32[5,2,2,5]{3,2,1,0:T(2,128)} %bitcast.18, f32[5,2,2,5]{3,2,1,0:T(2,128)} %bitcast.20, bf16[2048,640]{1,0:T(8,128)(2,1)S(1)} %multiply_convert_fusion.left_ref.refs_3_, bf16[16,576,128]{2,1,0:T(8,128)(2,1)} %all-to-all-done.own_hbm), custom_call_target="tpu_custom_call" | custom-call | tf_op jit(solution)/shard_map/pallas_call | solution.py:157
  61.7 0.8 collective-permute-done.refs_6_
  62.5 4.6 %shard_map.70 = bf16[16,64,512]{2,1,0:T(8,128)(2,1)S(1)} custom-call(s32[1]{0:T(128)} %bitcast.refs_0_, f32[5,2,2,5]{3,2,1,0:T(2,128)} %bitcast.19, f32[5,2,2,5]{3,2,1,0:T(2,128)} %bitcast.21, bf16[2048,640]{1,0:T(8,128)(2,1)S(1)} %multiply_convert_fusion.left_ref.refs_3_, bf16[320,512]{1,0:T(8,128)(2,1)S(1)} %get-tuple-element.12.refs_4_, ...), custom_call_target="tpu_custom_call" | custom-call | tf_op jit(solution)/shard_map/pallas_call | solution.py:219
  67.1 0.0 copy-start
  67.1 24.1 %all_to_all.25 = bf16[16,64,512]{2,1,0:T(8,128)(2,1)S(1)} all-to-all(bf16[16,64,512]{2,1,0:T(8,128)(2,1)S(1)} %shard_map.70), channel_id=1, replica_groups={{0,2,4,6},{8,10,12,14},{16,18,20,22},{24,26,28,30},{9,11,5,7},{17,19,13..., dimensions={0} | all-to-all | bytes 2097152 | tf_op jit(solution)/shard_map/all_to_all | solution.py:385
  91.2 0.1 shard_map.71
  91.4 21.6 %all_to_all.26.pieces_ref = bf16[4,64,512]{2,1,0:T(8,128)(2,1)S(1)} all-to-all(bf16[4,64,512]{2,1,0:T(8,128)(2,1)S(1)} %shard_map.71), channel_id=1, replica_groups=mesh['row_0'=4,'row_1'=4,'far'=4,'near'=4,'core'=2] {'far'}, dimensions={0} | all-to-all | bytes 524288 | tf_op jit(solution)/shard_map/all_to_all | solution.py:357
  112.9 0.0 copy-done
  112.9 0.2 shard_map.72
  113.1 17.7 %all_to_all.27.pieces_ref = f32[32,1,128]{2,1,0:T(1,128)S(1)} all-to-all(f32[32,1,128]{2,1,0:T(1,128)S(1)} %get-tuple-element.14), channel_id=1, replica_groups=mesh['row_0'=4,'row_1'=4,'far'=4,'near'=4,'core'=2] {'row_0','row_1','co..., dimensions={0} | all-to-all | bytes 32768 | tf_op jit(solution)/shard_map/all_to_all | solution.py:357
  130.9 16.9 %all_to_all.28.refs_0_ = f32[16,1,128]{2,1,0:T(1,128)S(1)} all-to-all(f32[16,1,128]{2,1,0:T(1,128)S(1)} %shard_map.73), channel_id=1, replica_groups=mesh['row_0'=4,'row_1'=4,'far'=4,'near'=4,'core'=2] {'far','near'}, dimensions={0} | all-to-all | bytes 16384 | tf_op jit(solution)/shard_map/all_to_all | solution.py:357
  147.8 0.8 shard_map.74
  (2 shorter events, 0.1 us)
Async XLA Ops:
  3.2 7.8 %copy-start.1 = (bf16[5,128,64]{1,2,0:T(8,128)(2,1)S(1)}, bf16[5,128,64]{1,2,0:T(8,128)(2,1)}, u32[]{:S(2)}) copy-start(bf16[5,128,64]{1,2,0:T(8,128)(2,1)} %param.6) | copy-start | bytes 245764
  3.2 52.5 %all-to-all-start = ((bf16[16,576,128]{2,1,0:T(8,128)(2,1)}), bf16[16,576,128]{2,1,0:T(8,128)(2,1)}, u32[]{:S(2)}, u32[]{:S(2)}) async-start(bf16[16,576,128]{2,1,0:T(8,128)(2,1)} %shard_map.68), calls=%async_computation | async-start | bytes 4718592 | tf_op jit(solution)/shard_map/all_to_all | solution.py:357
  55.8 6.8 %collective-permute-start = (bf16[16,576,128]{2,1,0:T(8,128)(2,1)}, bf16[16,576,128]{2,1,0:T(8,128)(2,1)}, u32[]{:S(2)}, u32[]{:S(2)}) collective-permute-start(bf16[16,576,128]{2,1,0:T(8,128)(2,1)} %all-to-all-done.own_hbm), channel_id=1, source_target_pairs={{0,1},{1,0},{2,3},{3,2},{4,5},{5,4},{6,7},{7,6},{8,9},{9,8},{10,11... | collective-permute-start | bytes 7077896 | tf_op jit(solution)/shard_map/ppermute | solution.py:361
  67.1 45.9 %copy-start = (bf16[4,128,64]{1,2,0:T(8,128)(2,1)S(1)}, bf16[4,128,64]{1,2,0:T(8,128)(2,1)}, u32[]{:S(2)}) copy-start(bf16[4,128,64]{1,2,0:T(8,128)(2,1)} %param.5) | copy-start | bytes 196612

commit v12 on v11

--- a/solution.py
+++ b/solution.py
@@ -89,21 +89,11 @@
     return total
 
 
-def vector_copies(source, vec_s, sems):
-    rows = vec_s.shape[0]
-    width = source.shape[2]
-    loads = [
-        pltpu.make_async_copy(source.at[r, pl.ds(0, rows)], vec_s.at[:, pl.ds(r * width, width)], sems.at[r])
-        for r in range(source.shape[0])
-    ]
-    for load in loads:
-        load.start()
-    return loads
-
-
-def contract_and_mix(site_loads, left_t, right_t, left_ref, vec_s, cross_s, half_s, store):
-    half = vec_s.shape[0] // STATES
-    width = 2 * half
+def contract_and_mix(site_loads, left_t, right_t, left_ref, piece_s, vec_s, cross_s, half_s, store):
+    blocks, rows, width = piece_s.shape
+    half = rows // STATES
+    for r in range(blocks):
+        vec_s[:, r * width : (r + 1) * width] = piece_s[r]
     cross_s[...] = jnp.dot(vec_s[...], left_ref[...], preferred_element_type=jnp.float32)
     for load in site_loads:
         load.wait()
@@ -126,29 +116,22 @@
 
 def own_kernel(
     left_site, right_site, left_ref, own_hbm, mixed_out, right_out,
-    left_t, right_t, vec_s, cross_s, half_s, vec_sems, right_sems, site_sems,
+    left_t, right_t, piece_s, vec_s, cross_s, half_s, sems, site_sems,
 ):
-    width = own_hbm.shape[2]
-    half = width // 2
-    loads = vector_copies(own_hbm, vec_s, vec_sems)
+    _, rows, width = piece_s.shape
+    half = rows // STATES
+    load = pltpu.make_async_copy(own_hbm.at[:, pl.ds(0, rows)], piece_s, sems.at[0])
+    load.start()
+    passed = pltpu.make_async_copy(own_hbm.at[:, pl.ds(rows, CHANNELS * half)], right_out, sems.at[1])
+    passed.start()
     site_loads = site_copies(left_site, right_site, left_t, right_t, site_sems)
-    passed = [
-        pltpu.make_async_copy(
-            own_hbm.at[:, pl.ds((STATES + v) * half, half)], right_out.at[:, :, pl.ds(v * width, width)], right_sems.at[v]
-        )
-        for v in range(CHANNELS)
-    ]
-    for load in loads:
-        load.wait()
-    for copy in passed:
-        copy.start()
+    load.wait()
 
     def store(v, s, x):
         mixed_out[v * half : (v + 1) * half, s * width : (s + 1) * width] = x
 
-    contract_and_mix(site_loads, left_t, right_t, left_ref, vec_s, cross_s, half_s, store)
-    for copy in passed:
-        copy.wait()
+    contract_and_mix(site_loads, left_t, right_t, left_ref, piece_s, vec_s, cross_s, half_s, store)
+    passed.wait()
 
 
 def own_part(sites, left, own):
@@ -158,17 +141,17 @@
         own_kernel,
         out_shape=(
             jax.ShapeDtypeStruct((CHANNELS * half, STATES * width), jnp.bfloat16),
-            jax.ShapeDtypeStruct((blocks, half, CHANNELS * width), jnp.bfloat16),
+            jax.ShapeDtypeStruct((blocks, CHANNELS * half, width), jnp.bfloat16),
         ),
         in_specs=[HBM, HBM, VMEM, HBM],
         out_specs=(VMEM, VMEM),
         scratch_shapes=[
             *(pltpu.SMEM(site.shape, jnp.float32) for site in sites),
+            pltpu.VMEM((blocks, STATES * half, width), jnp.bfloat16),
             pltpu.VMEM((STATES * half, blocks * width), jnp.bfloat16),
             pltpu.VMEM((STATES * half, CHANNELS * width), jnp.float32),
             pltpu.VMEM((CHANNELS, 2, half, width), jnp.float32),
-            pltpu.SemaphoreType.DMA((blocks,)),
-            pltpu.SemaphoreType.DMA((CHANNELS,)),
+            pltpu.SemaphoreType.DMA((2,)),
             pltpu.SemaphoreType.DMA((2,)),
         ],
         compiler_params=LARGE,
@@ -177,34 +160,36 @@
 
 def terms_kernel(
     order, core_ref, left_site, right_site, left_ref, mixed_ref, right_own, other_hbm, out_ref,
-    left_t, right_t, right_other, vec_s, cross_s, half_s, right_s, mixed_s, vec_sems, right_sem, site_sems,
+    left_t, right_t, piece_s, right_other, vec_s, cross_s, half_s, right_s, mixed_s, sems, site_sems,
 ):
     blocks, half, _ = out_ref.shape
     width = 2 * half
     core = core_ref[0]
     own_at = pl.multiple_of(core * half, half)
     other_at = pl.multiple_of((1 - core) * half, half)
-    loads = vector_copies(other_hbm, vec_s, vec_sems)
+    load = pltpu.make_async_copy(other_hbm.at[:, pl.ds(0, STATES * half)], piece_s, sems.at[0])
+    load.start()
+    right_load = pltpu.make_async_copy(other_hbm.at[:, pl.ds(STATES * half, CHANNELS * half)], right_other, sems.at[1])
+    right_load.start()
     site_loads = site_copies(left_site, right_site, left_t, right_t, site_sems)
-    right_load = pltpu.make_async_copy(other_hbm.at[:, pl.ds(STATES * half, CHANNELS * half)], right_other, right_sem)
     mine = lax.broadcasted_iota(jnp.int32, (half, width), 1) // half == core
     for v in range(CHANNELS):
         mixed_s[pl.ds(v * width + own_at, half), :] = mixed_ref[v * half : (v + 1) * half, :]
-    for load in loads:
-        load.wait()
-    right_load.start()
+        for r in range(blocks):
+            right_s[r * half : (r + 1) * half, v * width : (v + 1) * width] = right_own[r, v * half : (v + 1) * half, :]
+    load.wait()
 
     def store(v, s, x):
         mixed_s[pl.ds(v * width + other_at, half), s * width : (s + 1) * width] = x
 
-    contract_and_mix(site_loads, left_t, right_t, left_ref, vec_s, cross_s, half_s, store)
+    contract_and_mix(site_loads, left_t, right_t, left_ref, piece_s, vec_s, cross_s, half_s, store)
     right_load.wait()
     for r in range(blocks):
         for v in range(CHANNELS):
-            own = right_own[r, :, v * width : (v + 1) * width].astype(jnp.float32)
+            at = (slice(r * half, (r + 1) * half), slice(v * width, (v + 1) * width))
             other = right_other[r, v * half : (v + 1) * half, :].astype(jnp.float32)
             other = jnp.concatenate([other[:, half:], other[:, :half]], 1)
-            right_s[r * half : (r + 1) * half, v * width : (v + 1) * width] = jnp.where(mine, own, other).astype(jnp.bfloat16)
+            right_s[at] = jnp.where(mine, right_s[at].astype(jnp.float32), other).astype(jnp.bfloat16)
     image = jnp.dot(right_s[...], mixed_s[...], preferred_element_type=jnp.float32)
     for r in range(blocks):
         out_ref[order[r]] = image[r * half : (r + 1) * half].astype(jnp.bfloat16)
@@ -223,14 +208,14 @@
         out_specs=VMEM,
         scratch_shapes=[
             *(pltpu.SMEM(site.shape, jnp.float32) for site in sites),
+            pltpu.VMEM((blocks, STATES * half, width), jnp.bfloat16),
             pltpu.VMEM((blocks, CHANNELS * half, width), jnp.bfloat16),
             pltpu.VMEM((STATES * half, blocks * width), jnp.bfloat16),
             pltpu.VMEM((STATES * half, CHANNELS * width), jnp.float32),
             pltpu.VMEM((CHANNELS, 2, half, width), jnp.float32),
             pltpu.VMEM((blocks * half, CHANNELS * width), jnp.bfloat16),
             pltpu.VMEM((CHANNELS * width, STATES * width), jnp.bfloat16),
-            pltpu.SemaphoreType.DMA((blocks,)),
-            pltpu.SemaphoreType.DMA,
+            pltpu.SemaphoreType.DMA((2,)),
             pltpu.SemaphoreType.DMA((2,)),
         ],
         compiler_params=LARGE,

time: 149 us -> 149 us (level)
  no operation moved by 1% of the time
where the time goes in v12:
time: 149 us; the launch traced here: 148 us
  blocking collectives  125 us (84%)
  Pallas kernels  11.2 us (8%)
  starting transfers between devices  9.82 us (7%)
    all_to_all x3, blocking collectives, all_to_all(): return lax.all_to_all(x, axes, 0, 0, tiled=True)  56.2 us
    all_gather x1, blocking collectives, body(): left = lax.all_gather(left, COL, axis=0, tiled=True)  44.7 us
    all_to_all x1, blocking collectives, body(): lax.all_to_all(sent, COL, 0, 0, axis_index_groups=neighbours(n_far, n_nea...  24.1 us
    all_to_all x1, starting transfers between devices, all_to_all(): return lax.all_to_all(x, axes, 0, 0, tiled=True)  7.76 us
    pallas_call x1, Pallas kernels, terms(): pl.pallas_call(step, out_shape=jax.ShapeDtypeStruct((blocks, half, STATES...  4.27 us
    pallas_call x1, Pallas kernels, own_part(): pl.pallas_call(own_kernel, out_shape=(jax.ShapeDtypeStruct((CHANNELS * ha...  3.18 us
  transfers between devices with their start and end apart: 2, of which 1 were waited for; matrix products, arithmetic and copies ran while one was open for 0% of the time, Pallas kernels for 2%

profile of v12, /device:TPU:1, one launch (start us, length us, event | category | flops | bytes accessed | tf_op | source)
XLA Modules:
  0.0 148.3 jit_solution(11053225533661734031)
XLA Ops:
  0.6 2.6 %shard_map.68 = bf16[16,576,128]{2,1,0:T(8,128)(2,1)} custom-call(bf16[256,128]{1,0:T(8,128)(2,1)} %bitcast.15, bf16[5,64,128]{2,1,0:T(8,128)(2,1)} %right_hbm.1), custom_call_target="tpu_custom_call" | custom-call | tf_op jit(solution)/shard_map/pallas_call | solution.py:59
  3.2 0.0 copy-start.1
  3.2 7.8 %all-to-all-start = ((bf16[16,576,128]{2,1,0:T(8,128)(2,1)}), bf16[16,576,128]{2,1,0:T(8,128)(2,1)}, u32[]{:S(2)}, u32[]{:S(2)}) async-start(bf16[16,576,128]{2,1,0:T(8,128)(2,1)} %shard_map.68), calls=%async_computation | async-start | bytes 4718592 | tf_op jit(solution)/shard_map/all_to_all | solution.py:342
  11.0 0.0 copy-done.1
  11.0 44.7 %all-gather.1 = f16[2048,640]{1,0:T(8,128)(2,1)S(1)} all-gather(f16[64,640]{1,0:T(8,128)(2,1)S(1)} %copy_bitcast_fusion), channel_id=1, replica_groups=mesh['row_0'=4,'row_1'=4,'far'=4,'near'=4,'core'=2] {'far','near','core'}, dimensions={0}, use_global_device_ids=true | all-gather | bytes 2703360 | tf_op jit(solution)/shard_map/all_gather | solution.py:362
  55.8 0.0 all-to-all-done.own_hbm
  55.8 2.1 %collective-permute-start = (bf16[16,576,128]{2,1,0:T(8,128)(2,1)}, bf16[16,576,128]{2,1,0:T(8,128)(2,1)}, u32[]{:S(2)}, u32[]{:S(2)}) collective-permute-start(bf16[16,576,128]{2,1,0:T(8,128)(2,1)} %all-to-all-done.own_hbm), channel_id=1, source_target_pairs={{0,1},{1,0},{2,3},{3,2},{4,5},{5,4},{6,7},{7,6},{8,9},{9,8},{10,11... | collective-permute-start | bytes 7077896 | tf_op jit(solution)/shard_map/ppermute | solution.py:346
  57.8 0.6 multiply_convert_fusion.left_ref.refs_3_
  58.4 3.2 %shard_map.69 = (bf16[320,512]{1,0:T(8,128)(2,1)S(1)}, bf16[16,320,128]{2,1,0:T(8,128)(2,1)S(1)}) custom-call(f32[5,2,2,5]{3,2,1,0:T(2,128)} %bitcast.18, f32[5,2,2,5]{3,2,1,0:T(2,128)} %bitcast.20, bf16[2048,640]{1,0:T(8,128)(2,1)S(1)} %multiply_convert_fusion.left_ref.refs_3_, bf16[16,576,128]{2,1,0:T(8,128)(2,1)} %all-to-all-done.own_hbm), custom_call_target="tpu_custom_call" | custom-call | tf_op jit(solution)/shard_map/pallas_call | solution.py:140
  61.6 0.9 collective-permute-done.refs_6_
  62.5 4.3 %shard_map.70 = bf16[16,64,512]{2,1,0:T(8,128)(2,1)S(1)} custom-call(s32[1]{0:T(128)} %bitcast.refs_0_, f32[5,2,2,5]{3,2,1,0:T(2,128)} %bitcast.19, f32[5,2,2,5]{3,2,1,0:T(2,128)} %bitcast.21, bf16[2048,640]{1,0:T(8,128)(2,1)S(1)} %multiply_convert_fusion.left_ref.refs_3_, bf16[320,512]{1,0:T(8,128)(2,1)S(1)} %get-tuple-element.12.refs_4_, ...), custom_call_target="tpu_custom_call" | custom-call | tf_op jit(solution)/shard_map/pallas_call | solution.py:204
  66.8 0.0 copy-start
  66.8 24.1 %all_to_all.25 = bf16[16,64,512]{2,1,0:T(8,128)(2,1)S(1)} all-to-all(bf16[16,64,512]{2,1,0:T(8,128)(2,1)S(1)} %shard_map.70), channel_id=1, replica_groups={{0,2,4,6},{8,10,12,14},{16,18,20,22},{24,26,28,30},{9,11,5,7},{17,19,13..., dimensions={0} | all-to-all | bytes 2097152 | tf_op jit(solution)/shard_map/all_to_all | solution.py:370
  90.9 0.1 shard_map.71
  91.1 21.6 %all_to_all.26.pieces_ref = bf16[4,64,512]{2,1,0:T(8,128)(2,1)S(1)} all-to-all(bf16[4,64,512]{2,1,0:T(8,128)(2,1)S(1)} %shard_map.71), channel_id=1, replica_groups=mesh['row_0'=4,'row_1'=4,'far'=4,'near'=4,'core'=2] {'far'}, dimensions={0} | all-to-all | bytes 524288 | tf_op jit(solution)/shard_map/all_to_all | solution.py:342
  112.7 0.0 copy-done
  112.7 0.2 shard_map.72
  112.8 17.7 %all_to_all.27.pieces_ref = f32[32,1,128]{2,1,0:T(1,128)S(1)} all-to-all(f32[32,1,128]{2,1,0:T(1,128)S(1)} %get-tuple-element.14), channel_id=1, replica_groups=mesh['row_0'=4,'row_1'=4,'far'=4,'near'=4,'core'=2] {'row_0','row_1','co..., dimensions={0} | all-to-all | bytes 32768 | tf_op jit(solution)/shard_map/all_to_all | solution.py:342
  130.6 16.9 %all_to_all.28.refs_0_ = f32[16,1,128]{2,1,0:T(1,128)S(1)} all-to-all(f32[16,1,128]{2,1,0:T(1,128)S(1)} %shard_map.73), channel_id=1, replica_groups=mesh['row_0'=4,'row_1'=4,'far'=4,'near'=4,'core'=2] {'far','near'}, dimensions={0} | all-to-all | bytes 16384 | tf_op jit(solution)/shard_map/all_to_all | solution.py:342
  147.5 0.8 shard_map.74
  (2 shorter events, 0.1 us)
Async XLA Ops:
  3.2 7.8 %copy-start.1 = (bf16[5,128,64]{1,2,0:T(8,128)(2,1)S(1)}, bf16[5,128,64]{1,2,0:T(8,128)(2,1)}, u32[]{:S(2)}) copy-start(bf16[5,128,64]{1,2,0:T(8,128)(2,1)} %param.6) | copy-start | bytes 245764
  3.2 52.5 %all-to-all-start = ((bf16[16,576,128]{2,1,0:T(8,128)(2,1)}), bf16[16,576,128]{2,1,0:T(8,128)(2,1)}, u32[]{:S(2)}, u32[]{:S(2)}) async-start(bf16[16,576,128]{2,1,0:T(8,128)(2,1)} %shard_map.68), calls=%async_computation | async-start | bytes 4718592 | tf_op jit(solution)/shard_map/all_to_all | solution.py:342
  55.8 6.8 %collective-permute-start = (bf16[16,576,128]{2,1,0:T(8,128)(2,1)}, bf16[16,576,128]{2,1,0:T(8,128)(2,1)}, u32[]{:S(2)}, u32[]{:S(2)}) collective-permute-start(bf16[16,576,128]{2,1,0:T(8,128)(2,1)} %all-to-all-done.own_hbm), channel_id=1, source_target_pairs={{0,1},{1,0},{2,3},{3,2},{4,5},{5,4},{6,7},{7,6},{8,9},{9,8},{10,11... | collective-permute-start | bytes 7077896 | tf_op jit(solution)/shard_map/ppermute | solution.py:346
  66.8 45.9 %copy-start = (bf16[4,128,64]{1,2,0:T(8,128)(2,1)S(1)}, bf16[4,128,64]{1,2,0:T(8,128)(2,1)}, u32[]{:S(2)}) copy-start(bf16[4,128,64]{1,2,0:T(8,128)(2,1)} %param.5) | copy-start | bytes 196612

commit v13 on v12

--- a/solution.py
+++ b/solution.py
@@ -245,7 +245,7 @@
     groups = []
     for core in range(2):
         for j in range(n_far):
-            first = j * n_near + core * (n_near // 2)
+            first = j * n_near + (1 - core) * (n_near // 2)
             chips = sorted(((first + i) % n_z for i in range(n_near)), key=lambda z: z % n_near)
             groups.append([2 * z + core for z in chips])
     return groups

time: 149 us -> 147 us (0.987)
  no operation moved by 1% of the time
where the time goes in v13:
time: 147 us
  blocking collectives  124 us (84%)
  Pallas kernels  11.2 us (8%)
  starting transfers between devices  9.82 us (7%)
    all_to_all x3, blocking collectives, all_to_all(): return lax.all_to_all(x, axes, 0, 0, tiled=True)  55.7 us
    all_gather x1, blocking collectives, body(): left = lax.all_gather(left, COL, axis=0, tiled=True)  44.7 us
    all_to_all x1, blocking collectives, body(): lax.all_to_all(sent, COL, 0, 0, axis_index_groups=neighbours(n_far, n_nea...  23.2 us
    all_to_all x1, starting transfers between devices, all_to_all(): return lax.all_to_all(x, axes, 0, 0, tiled=True)  7.76 us
    pallas_call x1, Pallas kernels, terms(): pl.pallas_call(step, out_shape=jax.ShapeDtypeStruct((blocks, half, STATES...  4.27 us
    pallas_call x1, Pallas kernels, own_part(): pl.pallas_call(own_kernel, out_shape=(jax.ShapeDtypeStruct((CHANNELS * ha...  3.18 us
  transfers between devices with their start and end apart: 2, of which 1 were waited for; matrix products, arithmetic and copies ran while one was open for 0% of the time, Pallas kernels for 2%

profile of v13, /device:TPU:1, one launch (start us, length us, event | category | flops | bytes accessed | tf_op | source)
XLA Modules:
  0.0 146.8 jit_solution(3479701036240173852)
XLA Ops:
  0.6 2.6 %shard_map.68 = bf16[16,576,128]{2,1,0:T(8,128)(2,1)} custom-call(bf16[256,128]{1,0:T(8,128)(2,1)} %bitcast.15, bf16[5,64,128]{2,1,0:T(8,128)(2,1)} %right_hbm.1), custom_call_target="tpu_custom_call" | custom-call | tf_op jit(solution)/shard_map/pallas_call | solution.py:59
  3.2 0.0 copy-start.1
  3.2 7.8 %all-to-all-start = ((bf16[16,576,128]{2,1,0:T(8,128)(2,1)}), bf16[16,576,128]{2,1,0:T(8,128)(2,1)}, u32[]{:S(2)}, u32[]{:S(2)}) async-start(bf16[16,576,128]{2,1,0:T(8,128)(2,1)} %shard_map.68), calls=%async_computation | async-start | bytes 4718592 | tf_op jit(solution)/shard_map/all_to_all | solution.py:342
  11.0 0.0 copy-done.1
  11.0 44.7 %all-gather.1 = f16[2048,640]{1,0:T(8,128)(2,1)S(1)} all-gather(f16[64,640]{1,0:T(8,128)(2,1)S(1)} %copy_bitcast_fusion), channel_id=1, replica_groups=mesh['row_0'=4,'row_1'=4,'far'=4,'near'=4,'core'=2] {'far','near','core'}, dimensions={0}, use_global_device_ids=true | all-gather | bytes 2703360 | tf_op jit(solution)/shard_map/all_gather | solution.py:362
  55.8 0.0 all-to-all-done.own_hbm
  55.8 2.1 %collective-permute-start = (bf16[16,576,128]{2,1,0:T(8,128)(2,1)}, bf16[16,576,128]{2,1,0:T(8,128)(2,1)}, u32[]{:S(2)}, u32[]{:S(2)}) collective-permute-start(bf16[16,576,128]{2,1,0:T(8,128)(2,1)} %all-to-all-done.own_hbm), channel_id=1, source_target_pairs={{0,1},{1,0},{2,3},{3,2},{4,5},{5,4},{6,7},{7,6},{8,9},{9,8},{10,11... | collective-permute-start | bytes 7077896 | tf_op jit(solution)/shard_map/ppermute | solution.py:346
  57.8 0.6 multiply_convert_fusion.left_ref.refs_3_
  58.4 3.2 %shard_map.69 = (bf16[320,512]{1,0:T(8,128)(2,1)S(1)}, bf16[16,320,128]{2,1,0:T(8,128)(2,1)S(1)}) custom-call(f32[5,2,2,5]{3,2,1,0:T(2,128)} %bitcast.18, f32[5,2,2,5]{3,2,1,0:T(2,128)} %bitcast.20, bf16[2048,640]{1,0:T(8,128)(2,1)S(1)} %multiply_convert_fusion.left_ref.refs_3_, bf16[16,576,128]{2,1,0:T(8,128)(2,1)} %all-to-all-done.own_hbm), custom_call_target="tpu_custom_call" | custom-call | tf_op jit(solution)/shard_map/pallas_call | solution.py:140
  61.6 0.9 collective-permute-done.refs_6_
  62.5 4.3 %shard_map.70 = bf16[16,64,512]{2,1,0:T(8,128)(2,1)S(1)} custom-call(s32[1]{0:T(128)} %bitcast.refs_0_, f32[5,2,2,5]{3,2,1,0:T(2,128)} %bitcast.19, f32[5,2,2,5]{3,2,1,0:T(2,128)} %bitcast.21, bf16[2048,640]{1,0:T(8,128)(2,1)S(1)} %multiply_convert_fusion.left_ref.refs_3_, bf16[320,512]{1,0:T(8,128)(2,1)S(1)} %get-tuple-element.12.refs_4_, ...), custom_call_target="tpu_custom_call" | custom-call | tf_op jit(solution)/shard_map/pallas_call | solution.py:204
  66.8 0.0 copy-start
  66.8 23.2 %all_to_all.25 = bf16[16,64,512]{2,1,0:T(8,128)(2,1)S(1)} all-to-all(bf16[16,64,512]{2,1,0:T(8,128)(2,1)S(1)} %shard_map.70), channel_id=1, replica_groups={{8,10,4,6},{16,18,12,14},{24,26,20,22},{0,2,28,30},{1,3,5,7},{9,11,13,1..., dimensions={0} | all-to-all | bytes 2097152 | tf_op jit(solution)/shard_map/all_to_all | solution.py:370
  90.0 0.1 shard_map.71
  90.1 21.8 %all_to_all.26.pieces_ref = bf16[4,64,512]{2,1,0:T(8,128)(2,1)S(1)} all-to-all(bf16[4,64,512]{2,1,0:T(8,128)(2,1)S(1)} %shard_map.71), channel_id=1, replica_groups=mesh['row_0'=4,'row_1'=4,'far'=4,'near'=4,'core'=2] {'far'}, dimensions={0} | all-to-all | bytes 524288 | tf_op jit(solution)/shard_map/all_to_all | solution.py:342
  111.9 0.0 copy-done
  111.9 0.2 shard_map.72
  112.1 17.4 %all_to_all.27.pieces_ref = f32[32,1,128]{2,1,0:T(1,128)S(1)} all-to-all(f32[32,1,128]{2,1,0:T(1,128)S(1)} %get-tuple-element.14), channel_id=1, replica_groups=mesh['row_0'=4,'row_1'=4,'far'=4,'near'=4,'core'=2] {'row_0','row_1','co..., dimensions={0} | all-to-all | bytes 32768 | tf_op jit(solution)/shard_map/all_to_all | solution.py:342
  129.5 16.5 %all_to_all.28.refs_0_ = f32[16,1,128]{2,1,0:T(1,128)S(1)} all-to-all(f32[16,1,128]{2,1,0:T(1,128)S(1)} %shard_map.73), channel_id=1, replica_groups=mesh['row_0'=4,'row_1'=4,'far'=4,'near'=4,'core'=2] {'far','near'}, dimensions={0} | all-to-all | bytes 16384 | tf_op jit(solution)/shard_map/all_to_all | solution.py:342
  146.1 0.8 shard_map.74
  (2 shorter events, 0.1 us)
Async XLA Ops:
  3.2 7.8 %copy-start.1 = (bf16[5,128,64]{1,2,0:T(8,128)(2,1)S(1)}, bf16[5,128,64]{1,2,0:T(8,128)(2,1)}, u32[]{:S(2)}) copy-start(bf16[5,128,64]{1,2,0:T(8,128)(2,1)} %param.6) | copy-start | bytes 245764
  3.2 52.5 %all-to-all-start = ((bf16[16,576,128]{2,1,0:T(8,128)(2,1)}), bf16[16,576,128]{2,1,0:T(8,128)(2,1)}, u32[]{:S(2)}, u32[]{:S(2)}) async-start(bf16[16,576,128]{2,1,0:T(8,128)(2,1)} %shard_map.68), calls=%async_computation | async-start | bytes 4718592 | tf_op jit(solution)/shard_map/all_to_all | solution.py:342
  55.8 6.8 %collective-permute-start = (bf16[16,576,128]{2,1,0:T(8,128)(2,1)}, bf16[16,576,128]{2,1,0:T(8,128)(2,1)}, u32[]{:S(2)}, u32[]{:S(2)}) collective-permute-start(bf16[16,576,128]{2,1,0:T(8,128)(2,1)} %all-to-all-done.own_hbm), channel_id=1, source_target_pairs={{0,1},{1,0},{2,3},{3,2},{4,5},{5,4},{6,7},{7,6},{8,9},{9,8},{10,11... | collective-permute-start | bytes 7077896 | tf_op jit(solution)/shard_map/ppermute | solution.py:346
  66.8 45.1 %copy-start = (bf16[4,128,64]{1,2,0:T(8,128)(2,1)S(1)}, bf16[4,128,64]{1,2,0:T(8,128)(2,1)}, u32[]{:S(2)}) copy-start(bf16[4,128,64]{1,2,0:T(8,128)(2,1)} %param.5) | copy-start | bytes 196612

commit v14 on v13

--- a/solution.py
+++ b/solution.py
@@ -90,10 +90,10 @@
 
 
 def contract_and_mix(site_loads, left_t, right_t, left_ref, piece_s, vec_s, cross_s, half_s, store):
-    blocks, rows, width = piece_s.shape
-    half = rows // STATES
+    blocks, _, width = piece_s.shape
+    half = width // 2
     for r in range(blocks):
-        vec_s[:, r * width : (r + 1) * width] = piece_s[r]
+        vec_s[:, r * width : (r + 1) * width] = piece_s[r, : STATES * half, :]
     cross_s[...] = jnp.dot(vec_s[...], left_ref[...], preferred_element_type=jnp.float32)
     for load in site_loads:
         load.wait()
@@ -159,35 +159,29 @@
 
 
 def terms_kernel(
-    order, core_ref, left_site, right_site, left_ref, mixed_ref, right_own, other_hbm, out_ref,
-    left_t, right_t, piece_s, right_other, vec_s, cross_s, half_s, right_s, mixed_s, sems, site_sems,
+    order, left_site, right_site, left_ref, mixed_ref, right_own, other_ref, out_ref,
+    left_t, right_t, vec_s, cross_s, half_s, right_s, mixed_s, site_sems,
 ):
     blocks, half, _ = out_ref.shape
     width = 2 * half
-    core = core_ref[0]
+    core = lax.axis_index(C)
     own_at = pl.multiple_of(core * half, half)
     other_at = pl.multiple_of((1 - core) * half, half)
-    load = pltpu.make_async_copy(other_hbm.at[:, pl.ds(0, STATES * half)], piece_s, sems.at[0])
-    load.start()
-    right_load = pltpu.make_async_copy(other_hbm.at[:, pl.ds(STATES * half, CHANNELS * half)], right_other, sems.at[1])
-    right_load.start()
     site_loads = site_copies(left_site, right_site, left_t, right_t, site_sems)
     mine = lax.broadcasted_iota(jnp.int32, (half, width), 1) // half == core
     for v in range(CHANNELS):
         mixed_s[pl.ds(v * width + own_at, half), :] = mixed_ref[v * half : (v + 1) * half, :]
         for r in range(blocks):
             right_s[r * half : (r + 1) * half, v * width : (v + 1) * width] = right_own[r, v * half : (v + 1) * half, :]
-    load.wait()
 
     def store(v, s, x):
         mixed_s[pl.ds(v * width + other_at, half), s * width : (s + 1) * width] = x
 
-    contract_and_mix(site_loads, left_t, right_t, left_ref, piece_s, vec_s, cross_s, half_s, store)
-    right_load.wait()
+    contract_and_mix(site_loads, left_t, right_t, left_ref, other_ref, vec_s, cross_s, half_s, store)
     for r in range(blocks):
         for v in range(CHANNELS):
             at = (slice(r * half, (r + 1) * half), slice(v * width, (v + 1) * width))
-            other = right_other[r, v * half : (v + 1) * half, :].astype(jnp.float32)
+            other = other_ref[r, (STATES + v) * half : (STATES + v + 1) * half, :].astype(jnp.float32)
             other = jnp.concatenate([other[:, half:], other[:, :half]], 1)
             right_s[at] = jnp.where(mine, right_s[at].astype(jnp.float32), other).astype(jnp.bfloat16)
     image = jnp.dot(right_s[...], mixed_s[...], preferred_element_type=jnp.float32)
@@ -195,7 +189,7 @@
         out_ref[order[r]] = image[r * half : (r + 1) * half].astype(jnp.bfloat16)
 
 
-def terms(order, core, sites, left, mixed, right, other):
+def terms(order, sites, left, mixed, right, other):
     def step(*refs):
         terms_kernel(order, *refs)
 
@@ -204,22 +198,19 @@
     return pl.pallas_call(
         step,
         out_shape=jax.ShapeDtypeStruct((blocks, half, STATES * width), jnp.bfloat16),
-        in_specs=[SMEM, HBM, HBM, VMEM, VMEM, VMEM, HBM],
+        in_specs=[HBM, HBM, VMEM, VMEM, VMEM, VMEM],
         out_specs=VMEM,
         scratch_shapes=[
             *(pltpu.SMEM(site.shape, jnp.float32) for site in sites),
-            pltpu.VMEM((blocks, STATES * half, width), jnp.bfloat16),
-            pltpu.VMEM((blocks, CHANNELS * half, width), jnp.bfloat16),
             pltpu.VMEM((STATES * half, blocks * width), jnp.bfloat16),
             pltpu.VMEM((STATES * half, CHANNELS * width), jnp.float32),
             pltpu.VMEM((CHANNELS, 2, half, width), jnp.float32),
             pltpu.VMEM((blocks * half, CHANNELS * width), jnp.bfloat16),
             pltpu.VMEM((CHANNELS * width, STATES * width), jnp.bfloat16),
             pltpu.SemaphoreType.DMA((2,)),
-            pltpu.SemaphoreType.DMA((2,)),
         ],
         compiler_params=LARGE,
-    )(core, *(in_hbm(site) for site in sites), left, mixed, right, in_hbm(other))
+    )(*(in_hbm(site) for site in sites), left, mixed, right, other)
 
 
 def near_kernel(pieces_ref, out_ref):
@@ -352,7 +343,6 @@
     n_z = n_far * n_near
     _, rows, half = start_vector.shape
     entries = float(STATES * rows * half * n_row * n_z * lax.axis_size(C))
-    core = lax.axis_index(C).astype(jnp.int32).reshape(1)
     sites = tuple(jnp.transpose(tensor, (0, 2, 3, 1)) for tensor in (left_tensor, right_tensor))
     vector = jnp.swapaxes(start_vector, 1, 2)
     left = jnp.transpose(left_env, (2, 0, 1)).reshape(half, CHANNELS * rows)
@@ -365,7 +355,7 @@
     order = [n_far * (z % n_near) + z // n_near for z in range(n_z)]
     other = other_core(own)
     mixed, right = own_part(sites, left, own)
-    sent = terms(order, core, sites, left, mixed, right, other)
+    sent = terms(order, sites, left, mixed, right, other)
 
     pieces = lax.all_to_all(sent, COL, 0, 0, axis_index_groups=neighbours(n_far, n_near), tiled=True)
     pieces = all_to_all(near_sum(pieces.reshape(n_near, n_far, *pieces.shape[1:])), FAR)

time: 147 us -> 147 us (level)
  no operation moved by 1% of the time
where the time goes in v14:
time: 147 us; the launch traced here: 146 us
  blocking collectives  124 us (84%)
  Pallas kernels  10.9 us (7%)
  starting transfers between devices  9.81 us (7%)
    all_to_all x3, blocking collectives, all_to_all(): return lax.all_to_all(x, axes, 0, 0, tiled=True)  55.7 us
    all_gather x1, blocking collectives, body(): left = lax.all_gather(left, COL, axis=0, tiled=True)  44.7 us
    all_to_all x1, blocking collectives, body(): lax.all_to_all(sent, COL, 0, 0, axis_index_groups=neighbours(n_far, n_nea...  23.2 us
    all_to_all x1, starting transfers between devices, all_to_all(): return lax.all_to_all(x, axes, 0, 0, tiled=True)  7.76 us
    pallas_call x1, Pallas kernels, terms(): pl.pallas_call(step, out_shape=jax.ShapeDtypeStruct((blocks, half, STATES...  4.01 us
    pallas_call x1, Pallas kernels, own_part(): pl.pallas_call(own_kernel, out_shape=(jax.ShapeDtypeStruct((CHANNELS * ha...  3.18 us
  transfers between devices with their start and end apart: 2, of which 1 were waited for; matrix products, arithmetic and copies ran while one was open for 0% of the time, Pallas kernels for 2%

profile of v14, /device:TPU:1, one launch (start us, length us, event | category | flops | bytes accessed | tf_op | source)
XLA Modules:
  0.0 146.5 jit_solution(4003181452350778956)
XLA Ops:
  0.6 2.6 %shard_map.68 = bf16[16,576,128]{2,1,0:T(8,128)(2,1)} custom-call(bf16[256,128]{1,0:T(8,128)(2,1)} %bitcast.14, bf16[5,64,128]{2,1,0:T(8,128)(2,1)} %right_hbm.1), custom_call_target="tpu_custom_call" | custom-call | tf_op jit(solution)/shard_map/pallas_call | solution.py:59
  3.2 0.0 copy-start.1
  3.2 7.8 %all-to-all-start = ((bf16[16,576,128]{2,1,0:T(8,128)(2,1)}), bf16[16,576,128]{2,1,0:T(8,128)(2,1)}, u32[]{:S(2)}, u32[]{:S(2)}) async-start(bf16[16,576,128]{2,1,0:T(8,128)(2,1)} %shard_map.68), calls=%async_computation | async-start | bytes 4718592 | tf_op jit(solution)/shard_map/all_to_all | solution.py:333
  11.0 0.0 copy-done.1
  11.0 44.7 %all-gather.1 = f16[2048,640]{1,0:T(8,128)(2,1)S(1)} all-gather(f16[64,640]{1,0:T(8,128)(2,1)S(1)} %copy_bitcast_fusion), channel_id=1, replica_groups=mesh['row_0'=4,'row_1'=4,'far'=4,'near'=4,'core'=2] {'far','near','core'}, dimensions={0}, use_global_device_ids=true | all-gather | bytes 2703360 | tf_op jit(solution)/shard_map/all_gather | solution.py:352
  55.8 0.0 all-to-all-done.own_hbm
  55.8 2.1 %collective-permute-start = (bf16[16,576,128]{2,1,0:T(8,128)(2,1)}, bf16[16,576,128]{2,1,0:T(8,128)(2,1)S(1)}, u32[]{:S(2)}, u32[]{:S(2)}) collective-permute-start(bf16[16,576,128]{2,1,0:T(8,128)(2,1)} %all-to-all-done.own_hbm), channel_id=1, source_target_pairs={{0,1},{1,0},{2,3},{3,2},{4,5},{5,4},{6,7},{7,6},{8,9},{9,8},{10,11... | collective-permute-start | bytes 7077896 | tf_op jit(solution)/shard_map/ppermute | solution.py:337
  57.8 0.6 multiply_convert_fusion.left_ref.refs_2_
  58.4 3.2 %shard_map.69 = (bf16[320,512]{1,0:T(8,128)(2,1)S(1)}, bf16[16,320,128]{2,1,0:T(8,128)(2,1)S(1)}) custom-call(f32[5,2,2,5]{3,2,1,0:T(2,128)} %bitcast.17, f32[5,2,2,5]{3,2,1,0:T(2,128)} %bitcast.19, bf16[2048,640]{1,0:T(8,128)(2,1)S(1)} %multiply_convert_fusion.left_ref.refs_2_, bf16[16,576,128]{2,1,0:T(8,128)(2,1)} %all-to-all-done.own_hbm), custom_call_target="tpu_custom_call" | custom-call | tf_op jit(solution)/shard_map/pallas_call | solution.py:140
  61.6 0.8 collective-permute-done.refs_5_
  62.4 4.0 %shard_map.70 = bf16[16,64,512]{2,1,0:T(8,128)(2,1)S(1)} custom-call(f32[5,2,2,5]{3,2,1,0:T(2,128)} %bitcast.18, f32[5,2,2,5]{3,2,1,0:T(2,128)} %bitcast.20, bf16[2048,640]{1,0:T(8,128)(2,1)S(1)} %multiply_convert_fusion.left_ref.refs_2_, bf16[320,512]{1,0:T(8,128)(2,1)S(1)} %get-tuple-element.12.refs_3_, ...), custom_call_target="tpu_custom_call" | custom-call | tf_op jit(solution)/shard_map/pallas_call | solution.py:198
  66.4 0.0 copy-start
  66.4 23.2 %all_to_all.25 = bf16[16,64,512]{2,1,0:T(8,128)(2,1)S(1)} all-to-all(bf16[16,64,512]{2,1,0:T(8,128)(2,1)S(1)} %shard_map.70), channel_id=1, replica_groups={{8,10,4,6},{16,18,12,14},{24,26,20,22},{0,2,28,30},{1,3,5,7},{9,11,13,1..., dimensions={0} | all-to-all | bytes 2097152 | tf_op jit(solution)/shard_map/all_to_all | solution.py:360
  89.6 0.1 shard_map.71
  89.7 21.8 %all_to_all.26.pieces_ref = bf16[4,64,512]{2,1,0:T(8,128)(2,1)S(1)} all-to-all(bf16[4,64,512]{2,1,0:T(8,128)(2,1)S(1)} %shard_map.71), channel_id=1, replica_groups=mesh['row_0'=4,'row_1'=4,'far'=4,'near'=4,'core'=2] {'far'}, dimensions={0} | all-to-all | bytes 524288 | tf_op jit(solution)/shard_map/all_to_all | solution.py:333
  111.5 0.0 copy-done
  111.5 0.2 shard_map.72
  111.7 17.4 %all_to_all.27.pieces_ref = f32[32,1,128]{2,1,0:T(1,128)S(1)} all-to-all(f32[32,1,128]{2,1,0:T(1,128)S(1)} %get-tuple-element.14), channel_id=1, replica_groups=mesh['row_0'=4,'row_1'=4,'far'=4,'near'=4,'core'=2] {'row_0','row_1','co..., dimensions={0} | all-to-all | bytes 32768 | tf_op jit(solution)/shard_map/all_to_all | solution.py:333
  129.1 16.5 %all_to_all.28.refs_0_ = f32[16,1,128]{2,1,0:T(1,128)S(1)} all-to-all(f32[16,1,128]{2,1,0:T(1,128)S(1)} %shard_map.73), channel_id=1, replica_groups=mesh['row_0'=4,'row_1'=4,'far'=4,'near'=4,'core'=2] {'far','near'}, dimensions={0} | all-to-all | bytes 16384 | tf_op jit(solution)/shard_map/all_to_all | solution.py:333
  145.7 0.8 shard_map.74
  (2 shorter events, 0.1 us)
Async XLA Ops:
  3.2 7.8 %copy-start.1 = (bf16[5,128,64]{1,2,0:T(8,128)(2,1)S(1)}, bf16[5,128,64]{1,2,0:T(8,128)(2,1)}, u32[]{:S(2)}) copy-start(bf16[5,128,64]{1,2,0:T(8,128)(2,1)} %param.6) | copy-start | bytes 245764
  3.2 52.5 %all-to-all-start = ((bf16[16,576,128]{2,1,0:T(8,128)(2,1)}), bf16[16,576,128]{2,1,0:T(8,128)(2,1)}, u32[]{:S(2)}, u32[]{:S(2)}) async-start(bf16[16,576,128]{2,1,0:T(8,128)(2,1)} %shard_map.68), calls=%async_computation | async-start | bytes 4718592 | tf_op jit(solution)/shard_map/all_to_all | solution.py:333
  55.8 6.6 %collective-permute-start = (bf16[16,576,128]{2,1,0:T(8,128)(2,1)}, bf16[16,576,128]{2,1,0:T(8,128)(2,1)S(1)}, u32[]{:S(2)}, u32[]{:S(2)}) collective-permute-start(bf16[16,576,128]{2,1,0:T(8,128)(2,1)} %all-to-all-done.own_hbm), channel_id=1, source_target_pairs={{0,1},{1,0},{2,3},{3,2},{4,5},{5,4},{6,7},{7,6},{8,9},{9,8},{10,11... | collective-permute-start | bytes 7077896 | tf_op jit(solution)/shard_map/ppermute | solution.py:337
  66.4 45.1 %copy-start = (bf16[4,128,64]{1,2,0:T(8,128)(2,1)S(1)}, bf16[4,128,64]{1,2,0:T(8,128)(2,1)}, u32[]{:S(2)}) copy-start(bf16[4,128,64]{1,2,0:T(8,128)(2,1)} %param.5) | copy-start | bytes 196612

commit v15 on v14

--- a/solution.py
+++ b/solution.py
@@ -171,8 +171,6 @@
     mine = lax.broadcasted_iota(jnp.int32, (half, width), 1) // half == core
     for v in range(CHANNELS):
         mixed_s[pl.ds(v * width + own_at, half), :] = mixed_ref[v * half : (v + 1) * half, :]
-        for r in range(blocks):
-            right_s[r * half : (r + 1) * half, v * width : (v + 1) * width] = right_own[r, v * half : (v + 1) * half, :]
 
     def store(v, s, x):
         mixed_s[pl.ds(v * width + other_at, half), s * width : (s + 1) * width] = x
@@ -183,7 +181,8 @@
             at = (slice(r * half, (r + 1) * half), slice(v * width, (v + 1) * width))
             other = other_ref[r, (STATES + v) * half : (STATES + v + 1) * half, :].astype(jnp.float32)
             other = jnp.concatenate([other[:, half:], other[:, :half]], 1)
-            right_s[at] = jnp.where(mine, right_s[at].astype(jnp.float32), other).astype(jnp.bfloat16)
+            own = right_own[r, v * half : (v + 1) * half, :].astype(jnp.float32)
+            right_s[at] = jnp.where(mine, own, other).astype(jnp.bfloat16)
     image = jnp.dot(right_s[...], mixed_s[...], preferred_element_type=jnp.float32)
     for r in range(blocks):
         out_ref[order[r]] = image[r * half : (r + 1) * half].astype(jnp.bfloat16)

time: 147 us -> 147 us (level)
  no operation moved by 1% of the time
where the time goes in v15:
time: 147 us; the launch traced here: 146 us
  blocking collectives  124 us (84%)
  Pallas kernels  10.5 us (7%)
  starting transfers between devices  9.81 us (7%)
    all_to_all x3, blocking collectives, all_to_all(): return lax.all_to_all(x, axes, 0, 0, tiled=True)  55.7 us
    all_gather x1, blocking collectives, body(): left = lax.all_gather(left, COL, axis=0, tiled=True)  44.7 us
    all_to_all x1, blocking collectives, body(): lax.all_to_all(sent, COL, 0, 0, axis_index_groups=neighbours(n_far, n_nea...  23.2 us
    all_to_all x1, starting transfers between devices, all_to_all(): return lax.all_to_all(x, axes, 0, 0, tiled=True)  7.76 us
    pallas_call x1, Pallas kernels, terms(): pl.pallas_call(step, out_shape=jax.ShapeDtypeStruct((blocks, half, STATES...  3.61 us
    pallas_call x1, Pallas kernels, own_part(): pl.pallas_call(own_kernel, out_shape=(jax.ShapeDtypeStruct((CHANNELS * ha...  3.18 us
  transfers between devices with their start and end apart: 2, of which 1 were waited for; matrix products, arithmetic and copies ran while one was open for 0% of the time, Pallas kernels for 2%

profile of v15, /device:TPU:1, one launch (start us, length us, event | category | flops | bytes accessed | tf_op | source)
XLA Modules:
  0.0 146.1 jit_solution(9544366993604128983)
XLA Ops:
  0.6 2.6 %shard_map.68 = bf16[16,576,128]{2,1,0:T(8,128)(2,1)} custom-call(bf16[256,128]{1,0:T(8,128)(2,1)} %bitcast.14, bf16[5,64,128]{2,1,0:T(8,128)(2,1)} %right_hbm.1), custom_call_target="tpu_custom_call" | custom-call | tf_op jit(solution)/shard_map/pallas_call | solution.py:59
  3.2 0.0 copy-start.1
  3.2 7.8 %all-to-all-start = ((bf16[16,576,128]{2,1,0:T(8,128)(2,1)}), bf16[16,576,128]{2,1,0:T(8,128)(2,1)}, u32[]{:S(2)}, u32[]{:S(2)}) async-start(bf16[16,576,128]{2,1,0:T(8,128)(2,1)} %shard_map.68), calls=%async_computation | async-start | bytes 4718592 | tf_op jit(solution)/shard_map/all_to_all | solution.py:332
  11.0 0.0 copy-done.1
  11.0 44.7 %all-gather.1 = f16[2048,640]{1,0:T(8,128)(2,1)S(1)} all-gather(f16[64,640]{1,0:T(8,128)(2,1)S(1)} %copy_bitcast_fusion), channel_id=1, replica_groups=mesh['row_0'=4,'row_1'=4,'far'=4,'near'=4,'core'=2] {'far','near','core'}, dimensions={0}, use_global_device_ids=true | all-gather | bytes 2703360 | tf_op jit(solution)/shard_map/all_gather | solution.py:351
  55.8 0.0 all-to-all-done.own_hbm
  55.8 2.1 %collective-permute-start = (bf16[16,576,128]{2,1,0:T(8,128)(2,1)}, bf16[16,576,128]{2,1,0:T(8,128)(2,1)S(1)}, u32[]{:S(2)}, u32[]{:S(2)}) collective-permute-start(bf16[16,576,128]{2,1,0:T(8,128)(2,1)} %all-to-all-done.own_hbm), channel_id=1, source_target_pairs={{0,1},{1,0},{2,3},{3,2},{4,5},{5,4},{6,7},{7,6},{8,9},{9,8},{10,11... | collective-permute-start | bytes 7077896 | tf_op jit(solution)/shard_map/ppermute | solution.py:336
  57.8 0.6 multiply_convert_fusion.left_ref.refs_2_
  58.4 3.2 %shard_map.69 = (bf16[320,512]{1,0:T(8,128)(2,1)S(1)}, bf16[16,320,128]{2,1,0:T(8,128)(2,1)S(1)}) custom-call(f32[5,2,2,5]{3,2,1,0:T(2,128)} %bitcast.17, f32[5,2,2,5]{3,2,1,0:T(2,128)} %bitcast.19, bf16[2048,640]{1,0:T(8,128)(2,1)S(1)} %multiply_convert_fusion.left_ref.refs_2_, bf16[16,576,128]{2,1,0:T(8,128)(2,1)} %all-to-all-done.own_hbm), custom_call_target="tpu_custom_call" | custom-call | tf_op jit(solution)/shard_map/pallas_call | solution.py:140
  61.6 0.8 collective-permute-done.refs_5_
  62.4 3.6 %shard_map.70 = bf16[16,64,512]{2,1,0:T(8,128)(2,1)S(1)} custom-call(f32[5,2,2,5]{3,2,1,0:T(2,128)} %bitcast.18, f32[5,2,2,5]{3,2,1,0:T(2,128)} %bitcast.20, bf16[2048,640]{1,0:T(8,128)(2,1)S(1)} %multiply_convert_fusion.left_ref.refs_2_, bf16[320,512]{1,0:T(8,128)(2,1)S(1)} %get-tuple-element.12.refs_3_, ...), custom_call_target="tpu_custom_call" | custom-call | tf_op jit(solution)/shard_map/pallas_call | solution.py:197
  66.0 0.0 copy-start
  66.0 23.2 %all_to_all.25 = bf16[16,64,512]{2,1,0:T(8,128)(2,1)S(1)} all-to-all(bf16[16,64,512]{2,1,0:T(8,128)(2,1)S(1)} %shard_map.70), channel_id=1, replica_groups={{8,10,4,6},{16,18,12,14},{24,26,20,22},{0,2,28,30},{1,3,5,7},{9,11,13,1..., dimensions={0} | all-to-all | bytes 2097152 | tf_op jit(solution)/shard_map/all_to_all | solution.py:359
  89.2 0.1 shard_map.71
  89.3 21.8 %all_to_all.26.pieces_ref = bf16[4,64,512]{2,1,0:T(8,128)(2,1)S(1)} all-to-all(bf16[4,64,512]{2,1,0:T(8,128)(2,1)S(1)} %shard_map.71), channel_id=1, replica_groups=mesh['row_0'=4,'row_1'=4,'far'=4,'near'=4,'core'=2] {'far'}, dimensions={0} | all-to-all | bytes 524288 | tf_op jit(solution)/shard_map/all_to_all | solution.py:332
  111.1 0.0 copy-done
  111.1 0.2 shard_map.72
  111.3 17.4 %all_to_all.27.pieces_ref = f32[32,1,128]{2,1,0:T(1,128)S(1)} all-to-all(f32[32,1,128]{2,1,0:T(1,128)S(1)} %get-tuple-element.14), channel_id=1, replica_groups=mesh['row_0'=4,'row_1'=4,'far'=4,'near'=4,'core'=2] {'row_0','row_1','co..., dimensions={0} | all-to-all | bytes 32768 | tf_op jit(solution)/shard_map/all_to_all | solution.py:332
  128.7 16.5 %all_to_all.28.refs_0_ = f32[16,1,128]{2,1,0:T(1,128)S(1)} all-to-all(f32[16,1,128]{2,1,0:T(1,128)S(1)} %shard_map.73), channel_id=1, replica_groups=mesh['row_0'=4,'row_1'=4,'far'=4,'near'=4,'core'=2] {'far','near'}, dimensions={0} | all-to-all | bytes 16384 | tf_op jit(solution)/shard_map/all_to_all | solution.py:332
  145.3 0.8 shard_map.74
  (2 shorter events, 0.1 us)
Async XLA Ops:
  3.2 7.8 %copy-start.1 = (bf16[5,128,64]{1,2,0:T(8,128)(2,1)S(1)}, bf16[5,128,64]{1,2,0:T(8,128)(2,1)}, u32[]{:S(2)}) copy-start(bf16[5,128,64]{1,2,0:T(8,128)(2,1)} %param.6) | copy-start | bytes 245764
  3.2 52.5 %all-to-all-start = ((bf16[16,576,128]{2,1,0:T(8,128)(2,1)}), bf16[16,576,128]{2,1,0:T(8,128)(2,1)}, u32[]{:S(2)}, u32[]{:S(2)}) async-start(bf16[16,576,128]{2,1,0:T(8,128)(2,1)} %shard_map.68), calls=%async_computation | async-start | bytes 4718592 | tf_op jit(solution)/shard_map/all_to_all | solution.py:332
  55.8 6.6 %collective-permute-start = (bf16[16,576,128]{2,1,0:T(8,128)(2,1)}, bf16[16,576,128]{2,1,0:T(8,128)(2,1)S(1)}, u32[]{:S(2)}, u32[]{:S(2)}) collective-permute-start(bf16[16,576,128]{2,1,0:T(8,128)(2,1)} %all-to-all-done.own_hbm), channel_id=1, source_target_pairs={{0,1},{1,0},{2,3},{3,2},{4,5},{5,4},{6,7},{7,6},{8,9},{9,8},{10,11... | collective-permute-start | bytes 7077896 | tf_op jit(solution)/shard_map/ppermute | solution.py:336
  66.0 45.1 %copy-start = (bf16[4,128,64]{1,2,0:T(8,128)(2,1)S(1)}, bf16[4,128,64]{1,2,0:T(8,128)(2,1)}, u32[]{:S(2)}) copy-start(bf16[4,128,64]{1,2,0:T(8,128)(2,1)} %param.5) | copy-start | bytes 196612
